TPU v7x, 256 devices: a whole 4x4x8 slice. The times are simulated.
256 devices in a mesh: chan: 32 (over y, z_lo, core), slot: 8 (over z_hi, x).
Axes of the slice: x: 4, y: 4, z: 8 (z_hi: 2, z_lo: 4; z = z_hi * 4 + z_lo), core: 2. Of those that a mesh axis runs over, the one named last changes fastest.
Arguments:
- measured_real: float32 [8, 32, 1770], P('slot', 'chan'), may hold values from -60 to 60
- measured_imaginary: float32 [8, 32, 1770], P('slot', 'chan'), may hold values from -60 to 60
- measured_weight: float32 [8, 32, 1770], P('slot', 'chan'), may hold values from 0.3 to 3
- baseline_vectors: float32 [8, 3, 1770], P('slot'), may hold values from -120 to 120
- antenna_pairs: int32 [2, 1770], replicated, may hold values from 0 to 59, as said below
- directions: float32 [3, 200], replicated, may hold values from -0.12 to 0.12
- direction_flux: float32 [32, 200], P('chan'), may hold values from 0.2 to 2
- channel_frequency: float32 [32], P('chan'), may hold values from 1.1 to 1.9
- electron_content_start: float32 [8, 60, 200], P('slot'), may hold values from -6 to 6
- pierce_station_direction: int32 [8, 12000], P('slot'), may hold values from 0 to 11999, each once within a row
- eigen_basis: float32 [12000, 2048], P('chan'), may hold values from -0.0546875 to 0.0546875
- eigen_weight: float32 [2048], replicated, may hold values from 0.1 to 1
Outputs:
- tec_final: float32 [8, 60, 200], P('slot')
- coefficients: float32 [8, 2048], P('slot')
- final_residual_real: float32 [8, 32, 1770], P('slot', 'chan')
- final_residual_imaginary: float32 [8, 32, 1770], P('slot', 'chan')
Inputs may be any that keep to these rules, and one draw needn't show every extreme that they name: `antenna_pairs`: each column is a pair of two different stations, and the 1770 columns hold every unordered pair of stations exactly once. `pierce_station_direction`: each row names every station-direction pair exactly once.
All inputs are finite; a program needn't handle non-finite values.
Results may differ from a plain program's by a relative error of at most 0.00018.
Values sent between devices are 32-bit elements; how exact they have to be, the bound alone decides.
No kernel may reach another device: no remote copies, remote signals or barrier semaphores. Data moves between devices by JAX's collectives and lax.ppermute only.
A program may use at most 64 MiB of HBM per device.

v0:
```python
import jax
import jax.numpy as jnp
from jax import lax
from jax.experimental import pallas as pl
from jax.experimental.pallas import tpu as pltpu
from jax.sharding import PartitionSpec as P

ITERS = 4
TEC_PHASE = -0.8448
SMOOTHING = 0.5
TWO_PI = 6.283185307179586
INTERPRET = False

S, D, K, B = 60, 200, 2048, 1770
SP, DP, BP = 64, 208, 1792
CH, PB, PW = 32, 375, 384
LB = 256
F32, BF16 = jnp.float32, jnp.bfloat16

COS = (0.9999999891722796, -19.73920453209451, 64.93911898389003, -85.45016555018871,
       60.167831730030905, -25.968313296519984, 6.5296104072911)
SIN = (6.283185272722459, -41.341697068957856, 81.60502462263176, -76.70155117699308,
       42.016165826534845, -14.868611009881327, 3.199693676305946)


def horner(coefficients, z):
    value = coefficients[-1] * z + coefficients[-2]
    for term in coefficients[-3::-1]:
        value = value * z + term
    return value


def split3(x):
    high = x.astype(BF16).astype(F32)
    rest = x - high
    middle = rest.astype(BF16).astype(F32)
    return high, middle, rest - middle


def dot_nt(a, b):
    return lax.dot_general(a, b, (((1,), (1,)), ((), ())), preferred_element_type=F32)


def dot_nn(a, b):
    return lax.dot_general(a, b, (((1,), (0,)), ((), ())), preferred_element_type=F32)


def one_hot(numbers, rows):
    return lax.broadcasted_iota(jnp.int32, (rows, numbers.shape[1]), 0) == numbers


def placed_parts(vals, stations, dirs, i):
    v = jnp.concatenate([vals[2 * i], vals[2 * i + 1]], axis=1)
    s = jnp.concatenate([stations[2 * i], stations[2 * i + 1]], axis=1)
    d = jnp.concatenate([dirs[2 * i], dirs[2 * i + 1]], axis=1)
    at = one_hot(s, SP)
    by_station = jnp.concatenate(
        [jnp.where(at, part, 0.0).astype(BF16) for part in split3(v)], axis=0
    )
    by_direction = jnp.where(one_hot(d, DP), 1.0, 0.0).astype(BF16)
    return by_station, by_direction


def picked(parts, s, d):
    at = jnp.where(one_hot(s, SP), 1.0, 0.0).astype(BF16)
    rows = dot_nn(parts, jnp.concatenate([at, at, at], axis=0))
    return jnp.sum(jnp.where(one_hot(d, DP), rows, 0.0), axis=0, keepdims=True)


def stacked(field):
    return jnp.concatenate([part.astype(BF16) for part in split3(field)], axis=1)


def solver(scal, tec, vis, uvw, pairs, cols, stations, dirs, own, out, res, acc, re_s, im_s, first, own_out):
    turn_scale = scal[0]
    tec_scale = scal[1]
    if first:
        parts = stacked(tec[...])
        own_out[...] = picked(parts, own[0], own[1])
    else:
        acc[...] = jnp.zeros_like(acc)

        def place(i, carry):
            by_station, by_direction = placed_parts(tec, stations, dirs, i)
            acc[...] += dot_nt(by_direction, by_station)
            return carry

        lax.fori_loop(0, CH // 2, place, 0)
        parts = acc[...].astype(BF16)

    def chunk(j, carry):
        numer, weight_sum = carry
        lanes = pl.ds(pl.multiple_of(j * LB, LB), LB)
        first_at = one_hot(pairs[0:1, lanes], SP)
        second_at = one_hot(pairs[1:2, lanes], SP)
        sign = jnp.where(first_at, 1.0, jnp.where(second_at, -1.0, 0.0)).astype(BF16)
        mixed = dot_nn(parts, jnp.concatenate([sign, sign, sign], axis=0))
        coords = uvw[:, lanes]
        data = vis[:, lanes]
        sums = []
        for h in range(LB // 128):
            c = coords[:, h * 128 : (h + 1) * 128]
            sum_re = jnp.zeros((8, 128), F32)
            sum_im = jnp.zeros((8, 128), F32)
            for g in range(DP // 8):
                rows = slice(8 * g, 8 * g + 8)
                turns = (
                    cols[0, rows, :] * c[0:1, :]
                    + cols[1, rows, :] * c[1:2, :]
                    + cols[2, rows, :] * c[2:3, :]
                ) + turn_scale * mixed[rows, h * 128 : (h + 1) * 128]
                r = turns - jnp.round(turns)
                z = r * r
                flux = cols[3, rows, :]
                re = flux * horner(COS, z)
                im = flux * (r * horner(SIN, z))
                re_s[rows, h * 128 : (h + 1) * 128] = re
                im_s[rows, h * 128 : (h + 1) * 128] = im
                sum_re = sum_re + re
                sum_im = sum_im + im
            sums.append(
                (jnp.sum(sum_re, axis=0, keepdims=True), jnp.sum(sum_im, axis=0, keepdims=True))
            )
        left_re = data[0:1, :] - jnp.concatenate([a for a, _ in sums], axis=1)
        left_im = data[1:2, :] - jnp.concatenate([b for _, b in sums], axis=1)
        res[0:1, lanes] = left_re
        res[1:2, lanes] = left_im
        weight = data[2:3, :]
        proj = re_s[...] * (weight * left_im) - im_s[...] * (weight * left_re)
        high = proj.astype(BF16)
        low = (proj - high.astype(F32)).astype(BF16)
        numer = numer + (dot_nt(high, sign) + dot_nt(low, sign))
        if first:
            touched = jnp.where(first_at | second_at, weight, 0.0)
            weight_sum = weight_sum + (touched[:, :128] + touched[:, 128:])
        return numer, weight_sum

    numer, weight_sum = lax.fori_loop(
        0, BP // LB, chunk, (jnp.zeros((DP, SP), F32), jnp.zeros((SP, 128), F32))
    )
    numer_parts = stacked(numer * tec_scale)
    if first:
        weight_at = jnp.sum(weight_sum, axis=1, keepdims=True) * (tec_scale * tec_scale)
        flux_col = cols[3, :, 0:1]
        flux_col = flux_col * flux_col

    def pick(i, carry):
        s = jnp.concatenate([stations[2 * i], stations[2 * i + 1]], axis=1)
        d = jnp.concatenate([dirs[2 * i], dirs[2 * i + 1]], axis=1)
        got = picked(numer_parts, s, d)
        out[2 * i, 0:1, 0:PW] = got[:, :PW]
        out[2 * i + 1, 0:1, 0:PW] = got[:, PW:]
        if first:
            w_at = jnp.sum(jnp.where(one_hot(s, SP), weight_at, 0.0), axis=0, keepdims=True)
            f_at = jnp.sum(jnp.where(one_hot(d, DP), flux_col, 0.0), axis=0, keepdims=True)
            den = w_at * f_at
            out[2 * i, 0:1, PW : 2 * PW] = den[:, :PW]
            out[2 * i + 1, 0:1, PW : 2 * PW] = den[:, PW:]
        return carry

    lax.fori_loop(0, CH // 2, pick, 0)


def params():
    return dict(
        compiler_params=pltpu.CompilerParams(),
        interpret=pltpu.InterpretParams() if INTERPRET else False,
    )


VM = pl.BlockSpec(memory_space=pltpu.VMEM)
SM = pl.BlockSpec(memory_space=pltpu.SMEM)
HB = pl.BlockSpec(memory_space=pl.ANY)


def call(kernel, name, out_shape, in_specs, scratch=()):
    return pl.pallas_call(
        kernel,
        name=name,
        out_shape=[jax.ShapeDtypeStruct(s, F32) for s in out_shape],
        in_specs=in_specs,
        out_specs=[VM] * len(out_shape),
        scratch_shapes=list(scratch),
        **params(),
    )


def first_solver(scal, tec, vis, uvw, pairs, cols, stations, dirs, own):
    def kernel(scal, tec, vis, uvw, pairs, cols, stations, dirs, own, out, res, own_out, re_s, im_s):
        solver(scal, tec, vis, uvw, pairs, cols, stations, dirs, own, out, res, None, re_s, im_s, True, own_out)

    return call(
        kernel,
        "first_solver",
        [(CH, 1, 2 * PW), (2, BP), (1, PW)],
        [SM] + [VM] * 8,
        [pltpu.VMEM((DP, LB), F32), pltpu.VMEM((DP, LB), F32)],
    )(scal, tec, vis, uvw, pairs, cols, stations, dirs, own)


def next_solver(scal, tec, vis, uvw, pairs, cols, stations, dirs):
    def kernel(scal, tec, vis, uvw, pairs, cols, stations, dirs, out, res, acc, re_s, im_s):
        solver(scal, tec, vis, uvw, pairs, cols, stations, dirs, None, out, res, acc, re_s, im_s, False, None)

    return call(
        kernel,
        "next_solver",
        [(CH, 1, PW), (2, BP)],
        [SM] + [VM] * 7,
        [pltpu.VMEM((DP, 3 * SP), F32), pltpu.VMEM((DP, LB), F32), pltpu.VMEM((DP, LB), F32)],
    )(scal, tec, vis, uvw, pairs, cols, stations, dirs)


def final_place(vals, stations, dirs):
    def kernel(vals, stations, dirs, out, acc):
        acc[...] = jnp.zeros_like(acc)

        def place(i, carry):
            by_station, by_direction = placed_parts(vals, stations, dirs, i)
            acc[...] += dot_nt(by_station, by_direction)
            return carry

        lax.fori_loop(0, CH // 2, place, 0)
        out[...] = (acc[0:SP, :] + acc[SP : 2 * SP, :]) + acc[2 * SP : 3 * SP, :]

    return call(kernel, "final_place", [(SP, DP)], [VM] * 3, [pltpu.VMEM((3 * SP, DP), F32)])(
        vals, stations, dirs
    )[0]


def own_target(arrived, own, denominator):
    first = denominator is None

    def kernel(arrived, own, *refs):
        total = jnp.sum(arrived[...], axis=0)
        if first:
            out, den_out = refs
            den = total[:, PW:]
            den_out[...] = den
        else:
            den_ref, out = refs
            den = den_ref[...]
        lane = lax.broadcasted_iota(jnp.int32, (1, PW), 1)
        out[...] = jnp.where(lane < PB, own[...] + total[:, :PW] / den, 0.0)

    if first:
        return call(kernel, "own_target_first", [(1, PW), (1, PW)], [VM] * 2)(arrived, own)
    return call(kernel, "own_target", [(1, PW)], [VM] * 3)(arrived, own, denominator)[0], denominator


CUTS = ((0, 96), (96, 96), (192, 96), (288, 87))


def basis_copies(basis, held, sems):
    copies = [
        pltpu.make_async_copy(basis.at[pl.ds(a, n)], held.at[pl.ds(a, n)], sems.at[i])
        for i, (a, n) in enumerate(CUTS)
    ]
    for copy in copies:
        copy.start()
    return copies


def groups_of(a, n):
    return [(r, min(8, a + n - r)) for r in range(a, a + n, 8)]


BASIS_SCRATCH = [pltpu.VMEM((PB, K), F32), pltpu.SemaphoreType.DMA((len(CUTS),))]


def basis_partial(norm, target, near, far, weight, basis):
    def kernel(norm, target, near, far, weight, basis, out, held, sems, tall):
        copies = basis_copies(basis, held, sems)
        x = (target[...] + SMOOTHING * (near[...] + far[...])) / norm[0]
        tall[...] = jnp.broadcast_to(x, (128, PW)).T
        total = jnp.zeros((8, K), F32)
        tail = jnp.zeros((1, K), F32)
        for copy, (a, n) in zip(copies, CUTS):
            copy.wait()
            for r, m in groups_of(a, n):
                column = tall[r : r + m, :]
                piece = held[r : r + m, :] * jnp.concatenate([column] * (K // 128), axis=1)
                if m == 8:
                    total = total + piece
                else:
                    tail = jnp.sum(piece, axis=0, keepdims=True)
        row = (jnp.sum(total, axis=0, keepdims=True) + tail) * weight[...]
        for c in range(CH):
            out[c] = row

    return call(
        kernel,
        "basis_partial",
        [(CH, 1, K)],
        [SM] + [VM] * 4 + [HB],
        BASIS_SCRATCH + [pltpu.VMEM((PW, 128), F32)],
    )(norm, target, near, far, weight, basis)[0]


def own_screen(arrived, basis):
    def kernel(arrived, basis, coef, own, out, held, sems, tall):
        copies = basis_copies(basis, held, sems)
        row = jnp.sum(arrived[...], axis=0)
        coef[...] = row
        spread = jnp.broadcast_to(row, (8, K))
        tall[PW - 16 : PW, :] = jnp.zeros((16, 128), F32)
        for copy, (a, n) in zip(copies, CUTS):
            copy.wait()
            for r, m in groups_of(a, n):
                piece = held[r : r + m, :] * spread[0:m, :]
                parts = [piece[:, k : k + 128] for k in range(0, K, 128)]
                while len(parts) > 1:
                    parts = [u + v for u, v in zip(parts[0::2], parts[1::2])]
                tall[r : r + m, :] = parts[0]
        line = jnp.sum(tall[...].T, axis=0, keepdims=True)
        own[...] = line
        for c in range(CH):
            out[c] = line

    return call(
        kernel,
        "own_screen",
        [(1, K), (1, PW), (CH, 1, PW)],
        [VM, HB],
        BASIS_SCRATCH + [pltpu.VMEM((PW, 128), F32)],
    )(arrived, basis)


def exchange(value):
    return lax.all_to_all(value, "chan", split_axis=0, concat_axis=0, tiled=True)


def per_device(
    measured_real,
    measured_imaginary,
    measured_weight,
    baseline_vectors,
    antenna_pairs,
    directions,
    direction_flux,
    channel_frequency,
    electron_content_start,
    pierce_station_direction,
    eigen_basis,
    eigen_weight,
):
    frequency = channel_frequency[0]
    tec_scale = TEC_PHASE / frequency
    scal = jnp.stack([tec_scale * (1.0 / TWO_PI), tec_scale])
    vis = jnp.concatenate(
        [measured_real[0], measured_imaginary[0], measured_weight[0]], axis=0
    )
    vis = jnp.pad(vis, ((0, 0), (0, BP - B)))
    uvw = jnp.pad(baseline_vectors[0] * frequency, ((0, 0), (0, BP - B)))
    pairs = jnp.pad(antenna_pairs, ((0, 0), (0, BP - B)), constant_values=-1)
    cols = jnp.concatenate([directions, direction_flux], axis=0)
    cols = jnp.broadcast_to(jnp.pad(cols, ((0, 0), (0, DP - D)))[:, :, None], (4, DP, 128))
    tec_start = jnp.pad(electron_content_start[0].T, ((0, DP - D), (0, SP - S)))
    points = pierce_station_direction[0].reshape(CH, 1, PB)
    fill = ((0, 0), (0, 0), (0, PW - PB))
    stations = jnp.pad(points // D, fill, constant_values=-1)
    dirs = jnp.pad(points % D, fill, constant_values=-1)
    mine = lax.axis_index("chan")
    own_points = jnp.stack(
        [
            lax.dynamic_index_in_dim(stations, mine, 0, keepdims=False),
            lax.dynamic_index_in_dim(dirs, mine, 0, keepdims=False),
        ]
    )
    slot = lax.axis_index("slot")
    slots = lax.axis_size("slot")
    inside = (slot > 0).astype(F32) + (slot < slots - 1).astype(F32)
    norm = (1.0 + SMOOTHING * inside).reshape(1)
    weight = eigen_weight[None, :]
    near_pairs = [(i, i ^ 1) for i in range(slots) if i ^ 1 < slots]
    far_pairs = [(i, i - 1 if i % 2 == 0 else i + 1) for i in range(1, slots - 1)]
    far_pairs = [(i, j) for i, j in far_pairs if 0 <= j < slots]
    own = None
    denominator = None
    gathered = None
    coefficients = None
    residual = None
    for iteration in range(ITERS):
        if iteration == 0:
            sent, residual, own = first_solver(
                scal, tec_start, vis, uvw, pairs, cols, stations, dirs, own_points
            )
        else:
            sent, residual = next_solver(
                scal, gathered, vis, uvw, pairs, cols, stations, dirs
            )
        target, denominator = own_target(exchange(sent), own, denominator)
        far = lax.ppermute(target, "slot", far_pairs)
        near = lax.ppermute(target, "slot", near_pairs)
        partial = basis_partial(norm, target, near, far, weight, eigen_basis)
        coefficients, own, spread = own_screen(exchange(partial), eigen_basis)
        gathered = exchange(spread)
    tec_final = final_place(gathered, stations, dirs)[:S, :D]
    return (
        tec_final[None],
        coefficients,
        residual[0:1, :B][None],
        residual[1:2, :B][None],
    )


def solution(mesh):
    in_specs = (
        P("slot", "chan", None),
        P("slot", "chan", None),
        P("slot", "chan", None),
        P("slot", None, None),
        P(),
        P(),
        P("chan", None),
        P("chan"),
        P("slot", None, None),
        P("slot", None),
        P("chan", None),
        P(),
    )
    out_specs = (
        P("slot", None, None),
        P("slot", None),
        P("slot", "chan", None),
        P("slot", "chan", None),
    )
    return jax.shard_map(
        per_device, mesh=mesh, in_specs=in_specs, out_specs=out_specs, check_vma=False
    )
```

profile of v0, /device:TPU:7, one launch (start us, length us, event | category | flops | bytes accessed | tf_op | source)
XLA Modules:
  0.0 329.1 jit_solution(5707659668278269285)
XLA Ops:
  14.0 11.8 %first_solver.1 = (f32[32,1,768]{2,1,0:T(1,128)}, f32[2,1792]{1,0:T(2,128)}, f32[1,384]{1,0:T(1,128)}) custom-call(f32[2]{0:T(128)} %pad_maximum_fusion.scal, f32[208,64]{1,0:T(8,128)} %pad.26.tec, f32[3,1792]{1,0:T(4,128)} %select_maximum_fusion.vis, f32[3,1792]{1,0:T(4,128)} %pad.28.uvw, s32[2,1792]{1,0:T(2,128)} %pad.29.pairs, ...), custom_call_target="tpu_custom_call" | custom-call | tf_op jit(solution)/shard_map/first_solver/pallas_call | solution.py:192
  25.8 17.7 %all_to_all.60.arrived = f32[32,1,768]{2,1,0:T(1,128)} all-to-all(f32[32,1,768]{2,1,0:T(1,128)} %get-tuple-element.20), channel_id=1, replica_groups=mesh['chan'=32,'slot'=8] {'chan'}, dimensions={0} | all-to-all | bytes 196608 | tf_op jit(solution)/shard_map/all_to_all | solution.py:330
  45.0 6.0 %collective-permute-start.1 = (f32[1,384]{1,0:T(1,128)}, f32[1,384]{1,0:T(1,128)S(1)}, u32[]{:S(2)}, u32[]{:S(2)}) collective-permute-start(f32[1,384]{1,0:T(1,128)} %get-tuple-element.22.target), channel_id=1, source_target_pairs={{1,2},{2,1},{3,4},{4,3},{5,6},{6,5},{9,10},{10,9},{11,12},{12,11},... | collective-permute-start | bytes 4616 | tf_op jit(solution)/shard_map/ppermute | solution.py:393
  51.2 4.4 %collective-permute-done.1.far = f32[1,384]{1,0:T(1,128)S(1)} collective-permute-done((f32[1,384]{1,0:T(1,128)}, f32[1,384]{1,0:T(1,128)S(1)}, u32[]{:S(2)}, u32[]{:S(2)}) %collective-permute-start.1) | collective-permute-done | bytes 1568 | tf_op jit(solution)/shard_map/ppermute | solution.py:393
  59.6 17.1 %all_to_all.61.arrived = f32[32,1,2048]{2,1,0:T(1,128)} all-to-all(f32[32,1,2048]{2,1,0:T(1,128)} %basis_partial.4), channel_id=1, replica_groups=mesh['chan'=32,'slot'=8] {'chan'}, dimensions={0} | all-to-all | bytes 524288 | tf_op jit(solution)/shard_map/all_to_all | solution.py:330
  76.7 3.6 %own_screen.4 = (f32[1,2048]{1,0:T(1,128)}, f32[1,384]{1,0:T(1,128)}, f32[32,1,384]{2,1,0:T(1,128)}) custom-call(f32[32,1,2048]{2,1,0:T(1,128)} %all_to_all.61.arrived, f32[375,2048]{1,0:T(8,128)} %basis.15), custom_call_target="tpu_custom_call" | custom-call | tf_op jit(solution)/shard_map/own_screen/pallas_call | solution.py:320
  80.3 11.6 %all_to_all.62.tec = f32[32,1,384]{2,1,0:T(1,128)} all-to-all(f32[32,1,384]{2,1,0:T(1,128)} %get-tuple-element.23), channel_id=1, replica_groups=mesh['chan'=32,'slot'=8] {'chan'}, dimensions={0} | all-to-all | bytes 98304 | tf_op jit(solution)/shard_map/all_to_all | solution.py:330
  91.8 15.1 %next_solver.3 = (f32[32,1,384]{2,1,0:T(1,128)}, f32[2,1792]{1,0:T(2,128)}) custom-call(f32[2]{0:T(128)} %pad_maximum_fusion.scal, f32[32,1,384]{2,1,0:T(1,128)} %all_to_all.62.tec, f32[3,1792]{1,0:T(4,128)} %select_maximum_fusion.vis, f32[3,1792]{1,0:T(4,128)} %pad.28.uvw, s32[2,1792]{1,0:T(2,128)} %pad.29.pairs, f32[4,208,128]{2,1,0:T(8,128)} %broadcast_in_dim.18.cols, ...), custom_call_target="tpu_custom_call" | custom-call | tf_op jit(solution)/shard_map/next_solver/pallas_call | solution.py:205
  106.9 12.4 %all_to_all.63.arrived = f32[32,1,384]{2,1,0:T(1,128)} all-to-all(f32[32,1,384]{2,1,0:T(1,128)} %get-tuple-element.24), channel_id=1, replica_groups=mesh['chan'=32,'slot'=8] {'chan'}, dimensions={0} | all-to-all | bytes 98304 | tf_op jit(solution)/shard_map/all_to_all | solution.py:330
  120.8 6.0 %collective-permute-start.3 = (f32[1,384]{1,0:T(1,128)}, f32[1,384]{1,0:T(1,128)S(1)}, u32[]{:S(2)}, u32[]{:S(2)}) collective-permute-start(f32[1,384]{1,0:T(1,128)} %own_target.3.target), channel_id=1, source_target_pairs={{1,2},{2,1},{3,4},{4,3},{5,6},{6,5},{9,10},{10,9},{11,12},{12,11},... | collective-permute-start | bytes 4616 | tf_op jit(solution)/shard_map/ppermute | solution.py:393
  126.9 4.4 %collective-permute-done.3.far = f32[1,384]{1,0:T(1,128)S(1)} collective-permute-done((f32[1,384]{1,0:T(1,128)}, f32[1,384]{1,0:T(1,128)S(1)}, u32[]{:S(2)}, u32[]{:S(2)}) %collective-permute-start.3) | collective-permute-done | bytes 1568 | tf_op jit(solution)/shard_map/ppermute | solution.py:393
  135.9 17.2 %all_to_all.64.arrived = f32[32,1,2048]{2,1,0:T(1,128)} all-to-all(f32[32,1,2048]{2,1,0:T(1,128)} %basis_partial.5), channel_id=1, replica_groups=mesh['chan'=32,'slot'=8] {'chan'}, dimensions={0} | all-to-all | bytes 524288 | tf_op jit(solution)/shard_map/all_to_all | solution.py:330
  153.1 3.6 %own_screen.5 = (f32[1,2048]{1,0:T(1,128)}, f32[1,384]{1,0:T(1,128)}, f32[32,1,384]{2,1,0:T(1,128)}) custom-call(f32[32,1,2048]{2,1,0:T(1,128)} %all_to_all.64.arrived, f32[375,2048]{1,0:T(8,128)} %basis.15), custom_call_target="tpu_custom_call" | custom-call | tf_op jit(solution)/shard_map/own_screen/pallas_call | solution.py:320
  156.7 11.6 %all_to_all.65.tec = f32[32,1,384]{2,1,0:T(1,128)} all-to-all(f32[32,1,384]{2,1,0:T(1,128)} %get-tuple-element.27), channel_id=1, replica_groups=mesh['chan'=32,'slot'=8] {'chan'}, dimensions={0} | all-to-all | bytes 98304 | tf_op jit(solution)/shard_map/all_to_all | solution.py:330
  168.2 15.1 %next_solver.4 = (f32[32,1,384]{2,1,0:T(1,128)}, f32[2,1792]{1,0:T(2,128)}) custom-call(f32[2]{0:T(128)} %pad_maximum_fusion.scal, f32[32,1,384]{2,1,0:T(1,128)} %all_to_all.65.tec, f32[3,1792]{1,0:T(4,128)} %select_maximum_fusion.vis, f32[3,1792]{1,0:T(4,128)} %pad.28.uvw, s32[2,1792]{1,0:T(2,128)} %pad.29.pairs, f32[4,208,128]{2,1,0:T(8,128)} %broadcast_in_dim.18.cols, ...), custom_call_target="tpu_custom_call" | custom-call | tf_op jit(solution)/shard_map/next_solver/pallas_call | solution.py:205
  183.3 12.4 %all_to_all.66.arrived = f32[32,1,384]{2,1,0:T(1,128)} all-to-all(f32[32,1,384]{2,1,0:T(1,128)} %get-tuple-element.28), channel_id=1, replica_groups=mesh['chan'=32,'slot'=8] {'chan'}, dimensions={0} | all-to-all | bytes 98304 | tf_op jit(solution)/shard_map/all_to_all | solution.py:330
  197.2 6.0 %collective-permute-start.5 = (f32[1,384]{1,0:T(1,128)}, f32[1,384]{1,0:T(1,128)S(1)}, u32[]{:S(2)}, u32[]{:S(2)}) collective-permute-start(f32[1,384]{1,0:T(1,128)} %own_target.4.target), channel_id=1, source_target_pairs={{1,2},{2,1},{3,4},{4,3},{5,6},{6,5},{9,10},{10,9},{11,12},{12,11},... | collective-permute-start | bytes 4616 | tf_op jit(solution)/shard_map/ppermute | solution.py:393
  203.3 4.4 %collective-permute-done.5.far = f32[1,384]{1,0:T(1,128)S(1)} collective-permute-done((f32[1,384]{1,0:T(1,128)}, f32[1,384]{1,0:T(1,128)S(1)}, u32[]{:S(2)}, u32[]{:S(2)}) %collective-permute-start.5) | collective-permute-done | bytes 1568 | tf_op jit(solution)/shard_map/ppermute | solution.py:393
  208.9 3.4 %basis_partial.6 = f32[32,1,2048]{2,1,0:T(1,128)} custom-call(f32[1]{0:T(128)} %bitcast.norm, f32[1,384]{1,0:T(1,128)} %own_target.4.target, f32[1,384]{1,0:T(1,128)} %copy-done.9, f32[1,384]{1,0:T(1,128)} %copy-done.6, f32[1,2048]{1,0:T(1,128)} %bitcast.24, f32[375,2048]{1,0:T(8,128)} %basis.15), custom_call_target="tpu_custom_call" | custom-call | tf_op jit(solution)/shard_map/basis_partial/pallas_call | solution.py:291
  212.3 17.4 %all_to_all.67.arrived = f32[32,1,2048]{2,1,0:T(1,128)} all-to-all(f32[32,1,2048]{2,1,0:T(1,128)} %basis_partial.6), channel_id=1, replica_groups=mesh['chan'=32,'slot'=8] {'chan'}, dimensions={0} | all-to-all | bytes 524288 | tf_op jit(solution)/shard_map/all_to_all | solution.py:330
  229.7 3.6 %own_screen.6 = (f32[1,2048]{1,0:T(1,128)}, f32[1,384]{1,0:T(1,128)}, f32[32,1,384]{2,1,0:T(1,128)}) custom-call(f32[32,1,2048]{2,1,0:T(1,128)} %all_to_all.67.arrived, f32[375,2048]{1,0:T(8,128)} %basis.15), custom_call_target="tpu_custom_call" | custom-call | tf_op jit(solution)/shard_map/own_screen/pallas_call | solution.py:320
  233.3 11.6 %all_to_all.68.tec = f32[32,1,384]{2,1,0:T(1,128)} all-to-all(f32[32,1,384]{2,1,0:T(1,128)} %get-tuple-element.30), channel_id=1, replica_groups=mesh['chan'=32,'slot'=8] {'chan'}, dimensions={0} | all-to-all | bytes 98304 | tf_op jit(solution)/shard_map/all_to_all | solution.py:330
  244.8 15.1 %next_solver.5 = (f32[32,1,384]{2,1,0:T(1,128)}, f32[2,1792]{1,0:T(2,128)}) custom-call(f32[2]{0:T(128)} %pad_maximum_fusion.scal, f32[32,1,384]{2,1,0:T(1,128)} %all_to_all.68.tec, f32[3,1792]{1,0:T(4,128)} %select_maximum_fusion.vis, f32[3,1792]{1,0:T(4,128)} %pad.28.uvw, s32[2,1792]{1,0:T(2,128)} %pad.29.pairs, f32[4,208,128]{2,1,0:T(8,128)} %broadcast_in_dim.18.cols, ...), custom_call_target="tpu_custom_call" | custom-call | tf_op jit(solution)/shard_map/next_solver/pallas_call | solution.py:205
  259.9 12.4 %all_to_all.69.arrived = f32[32,1,384]{2,1,0:T(1,128)} all-to-all(f32[32,1,384]{2,1,0:T(1,128)} %get-tuple-element.31), channel_id=1, replica_groups=mesh['chan'=32,'slot'=8] {'chan'}, dimensions={0} | all-to-all | bytes 98304 | tf_op jit(solution)/shard_map/all_to_all | solution.py:330
  273.8 6.2 %collective-permute-start.7 = (f32[1,384]{1,0:T(1,128)}, f32[1,384]{1,0:T(1,128)S(1)}, u32[]{:S(2)}, u32[]{:S(2)}) collective-permute-start(f32[1,384]{1,0:T(1,128)} %own_target.5.target), channel_id=1, source_target_pairs={{1,2},{2,1},{3,4},{4,3},{5,6},{6,5},{9,10},{10,9},{11,12},{12,11},... | collective-permute-start | bytes 4616 | tf_op jit(solution)/shard_map/ppermute | solution.py:393
  280.1 4.4 %collective-permute-done.7.far = f32[1,384]{1,0:T(1,128)S(1)} collective-permute-done((f32[1,384]{1,0:T(1,128)}, f32[1,384]{1,0:T(1,128)S(1)}, u32[]{:S(2)}, u32[]{:S(2)}) %collective-permute-start.7) | collective-permute-done | bytes 1568 | tf_op jit(solution)/shard_map/ppermute | solution.py:393
  285.6 3.4 %basis_partial.7 = f32[32,1,2048]{2,1,0:T(1,128)} custom-call(f32[1]{0:T(128)} %bitcast.norm, f32[1,384]{1,0:T(1,128)} %own_target.5.target, f32[1,384]{1,0:T(1,128)} %copy-done.7, f32[1,384]{1,0:T(1,128)} %copy-done.4, f32[1,2048]{1,0:T(1,128)} %bitcast.25, f32[375,2048]{1,0:T(8,128)} %basis.15), custom_call_target="tpu_custom_call" | custom-call | tf_op jit(solution)/shard_map/basis_partial/pallas_call | solution.py:291
  289.0 17.2 %all_to_all.70.arrived = f32[32,1,2048]{2,1,0:T(1,128)} all-to-all(f32[32,1,2048]{2,1,0:T(1,128)} %basis_partial.7), channel_id=1, replica_groups=mesh['chan'=32,'slot'=8] {'chan'}, dimensions={0} | all-to-all | bytes 524288 | tf_op jit(solution)/shard_map/all_to_all | solution.py:330
  306.3 3.6 %own_screen.7 = (f32[1,2048]{1,0:T(1,128)}, f32[1,384]{1,0:T(1,128)}, f32[32,1,384]{2,1,0:T(1,128)}) custom-call(f32[32,1,2048]{2,1,0:T(1,128)} %all_to_all.70.arrived, f32[375,2048]{1,0:T(8,128)} %basis.15), custom_call_target="tpu_custom_call" | custom-call | tf_op jit(solution)/shard_map/own_screen/pallas_call | solution.py:320
  309.8 3.6 %all-to-all-start.11 = ((f32[32,1,384]{2,1,0:T(1,128)}), f32[32,1,384]{2,1,0:T(1,128)S(1)}, u32[]{:S(2)}, u32[]{:S(2)}) async-start(f32[32,1,384]{2,1,0:T(1,128)} %get-tuple-element.33), calls=%async_computation.11 | async-start | bytes 98304 | tf_op jit(solution)/shard_map/all_to_all | solution.py:330
  314.1 6.9 %all-to-all-done.11.vals = f32[32,1,384]{2,1,0:T(1,128)S(1)} async-done(((f32[32,1,384]{2,1,0:T(1,128)}), f32[32,1,384]{2,1,0:T(1,128)S(1)}, u32[]{:S(2)}, u32[]{:S(2)}) %all-to-all-start.11) | async-done | bytes 49184 | tf_op jit(solution)/shard_map/all_to_all | solution.py:330
  321.7 5.9 %final_place.1 = f32[64,208]{1,0:T(8,128)} custom-call(f32[32,1,384]{2,1,0:T(1,128)} %copy-done, s32[32,1,384]{2,1,0:T(1,128)} %pad.31.stations, s32[32,1,384]{2,1,0:T(1,128)} %pad.32.dirs), custom_call_target="tpu_custom_call" | custom-call | tf_op jit(solution)/shard_map/final_place/pallas_call | solution.py:226
  (56 shorter events, 32.3 us)
Async XLA Ops:
  45.0 10.5 %collective-permute-start.1 = (f32[1,384]{1,0:T(1,128)}, f32[1,384]{1,0:T(1,128)S(1)}, u32[]{:S(2)}, u32[]{:S(2)}) collective-permute-start(f32[1,384]{1,0:T(1,128)} %get-tuple-element.22.target), channel_id=1, source_target_pairs={{1,2},{2,1},{3,4},{4,3},{5,6},{6,5},{9,10},{10,9},{11,12},{12,11},... | collective-permute-start | bytes 4616 | tf_op jit(solution)/shard_map/ppermute | solution.py:393
  51.1 4.5 %collective-permute-start = (f32[1,384]{1,0:T(1,128)}, f32[1,384]{1,0:T(1,128)S(1)}, u32[]{:S(2)}, u32[]{:S(2)}) collective-permute-start(f32[1,384]{1,0:T(1,128)} %get-tuple-element.22.target), channel_id=1, source_target_pairs={{0,1},{1,0},{2,3},{3,2},{4,5},{5,4},{6,7},{7,6},{8,9},{9,8},{10,11... | collective-permute-start | bytes 4616 | tf_op jit(solution)/shard_map/ppermute | solution.py:394
  55.6 0.6 copy-start.2
  55.6 0.6 copy-start.3
  120.8 10.5 %collective-permute-start.3 = (f32[1,384]{1,0:T(1,128)}, f32[1,384]{1,0:T(1,128)S(1)}, u32[]{:S(2)}, u32[]{:S(2)}) collective-permute-start(f32[1,384]{1,0:T(1,128)} %own_target.3.target), channel_id=1, source_target_pairs={{1,2},{2,1},{3,4},{4,3},{5,6},{6,5},{9,10},{10,9},{11,12},{12,11},... | collective-permute-start | bytes 4616 | tf_op jit(solution)/shard_map/ppermute | solution.py:393
  126.8 4.5 %collective-permute-start.2 = (f32[1,384]{1,0:T(1,128)}, f32[1,384]{1,0:T(1,128)S(1)}, u32[]{:S(2)}, u32[]{:S(2)}) collective-permute-start(f32[1,384]{1,0:T(1,128)} %own_target.3.target), channel_id=1, source_target_pairs={{0,1},{1,0},{2,3},{3,2},{4,5},{5,4},{6,7},{7,6},{8,9},{9,8},{10,11... | collective-permute-start | bytes 4616 | tf_op jit(solution)/shard_map/ppermute | solution.py:394
  131.3 0.6 copy-start.5
  131.9 0.6 copy-start.8
  197.2 10.5 %collective-permute-start.5 = (f32[1,384]{1,0:T(1,128)}, f32[1,384]{1,0:T(1,128)S(1)}, u32[]{:S(2)}, u32[]{:S(2)}) collective-permute-start(f32[1,384]{1,0:T(1,128)} %own_target.4.target), channel_id=1, source_target_pairs={{1,2},{2,1},{3,4},{4,3},{5,6},{6,5},{9,10},{10,9},{11,12},{12,11},... | collective-permute-start | bytes 4616 | tf_op jit(solution)/shard_map/ppermute | solution.py:393
  203.2 4.5 %collective-permute-start.4 = (f32[1,384]{1,0:T(1,128)}, f32[1,384]{1,0:T(1,128)S(1)}, u32[]{:S(2)}, u32[]{:S(2)}) collective-permute-start(f32[1,384]{1,0:T(1,128)} %own_target.4.target), channel_id=1, source_target_pairs={{0,1},{1,0},{2,3},{3,2},{4,5},{5,4},{6,7},{7,6},{8,9},{9,8},{10,11... | collective-permute-start | bytes 4616 | tf_op jit(solution)/shard_map/ppermute | solution.py:394
  207.7 0.6 copy-start.6
  208.3 0.6 copy-start.9
  273.8 39.7 %copy-start.1 = (f32[2,1792]{1,0:T(2,128)S(1)}, f32[2,1792]{1,0:T(2,128)}, u32[]{:S(2)}) copy-start(f32[2,1792]{1,0:T(2,128)} %get-tuple-element.35) | copy-start | bytes 43012
  273.8 10.7 %collective-permute-start.7 = (f32[1,384]{1,0:T(1,128)}, f32[1,384]{1,0:T(1,128)S(1)}, u32[]{:S(2)}, u32[]{:S(2)}) collective-permute-start(f32[1,384]{1,0:T(1,128)} %own_target.5.target), channel_id=1, source_target_pairs={{1,2},{2,1},{3,4},{4,3},{5,6},{6,5},{9,10},{10,9},{11,12},{12,11},... | collective-permute-start | bytes 4616 | tf_op jit(solution)/shard_map/ppermute | solution.py:393
  280.0 4.5 %collective-permute-start.6 = (f32[1,384]{1,0:T(1,128)}, f32[1,384]{1,0:T(1,128)S(1)}, u32[]{:S(2)}, u32[]{:S(2)}) collective-permute-start(f32[1,384]{1,0:T(1,128)} %own_target.5.target), channel_id=1, source_target_pairs={{0,1},{1,0},{2,3},{3,2},{4,5},{5,4},{6,7},{7,6},{8,9},{9,8},{10,11... | collective-permute-start | bytes 4616 | tf_op jit(solution)/shard_map/ppermute | solution.py:394
  284.5 0.6 copy-start.4
  285.0 0.6 copy-start.7
  309.8 11.2 %all-to-all-start.11 = ((f32[32,1,384]{2,1,0:T(1,128)}), f32[32,1,384]{2,1,0:T(1,128)S(1)}, u32[]{:S(2)}, u32[]{:S(2)}) async-start(f32[32,1,384]{2,1,0:T(1,128)} %get-tuple-element.33), calls=%async_computation.11 | async-start | bytes 98304 | tf_op jit(solution)/shard_map/all_to_all | solution.py:330
  321.1 0.6 copy-start
where the time goes:
time: 331 us; the launch traced here: 329 us
  blocking collectives  159 us (48%)
  Pallas kernels  96.7 us (29%)
  starting transfers between devices  28.2 us (9%)
  waiting for transfers between devices  24.6 us (7%)
  local copies, waits for them, and re-layouts  12.9 us (4%)
  other arithmetic  6.35 us (2%)
    all_to_all x11, blocking collectives, exchange(): lax.all_to_all(value, 'chan', split_axis=0, concat_axis=0, tiled=True)  159 us
    pallas_call x3, Pallas kernels, next_solver(): call(kernel, 'next_solver', [(CH, 1, PW), (2, BP)], [SM] + [VM] * 7, [plt...  45.3 us
    ppermute x4, starting transfers between devices, per_device(): far = lax.ppermute(target, 'slot', far_pairs)  24.2 us
    ppermute x4, waiting for transfers between devices, per_device(): far = lax.ppermute(target, 'slot', far_pairs)  17.6 us
    pallas_call x4, Pallas kernels, own_screen(): call(kernel, 'own_screen', [(1, K), (1, PW), (CH, 1, PW)], [VM, HB], BASI...  14.3 us
    pallas_call x4, Pallas kernels, basis_partial(): call(kernel, 'basis_partial', [(CH, 1, K)], [SM] + [VM] * 4 + [HB], BASIS...  13.6 us
    pallas_call x1, Pallas kernels, first_solver(): call(kernel, 'first_solver', [(CH, 1, 2 * PW), (2, BP), (1, PW)], [SM] +...  11.8 us
    all_to_all x1, waiting for transfers between devices, exchange(): lax.all_to_all(value, 'chan', split_axis=0, concat_axis=0, tiled=True)  6.95 us
  transfers between devices with their start and end apart: 9, of which 5 were waited for; matrix products, arithmetic and copies ran while one was open for 0% of the time, Pallas kernels for 0%

commit v1 on v0

--- a/solution.py
+++ b/solution.py
@@ -10,6 +10,7 @@
 SMOOTHING = 0.5
 TWO_PI = 6.283185307179586
 INTERPRET = False
+VMEM_LIMIT = 16 * 1024 * 1024
 
 S, D, K, B = 60, 200, 2048, 1770
 SP, DP, BP = 64, 208, 1792
@@ -71,12 +72,14 @@
     return jnp.concatenate([part.astype(BF16) for part in split3(field)], axis=1)
 
 
-def solver(scal, tec, vis, uvw, pairs, cols, stations, dirs, own, out, res, acc, re_s, im_s, first, own_out):
-    turn_scale = scal[0]
-    tec_scale = scal[1]
+def solver(freq, tec, vis, uvw, pairs, cols, stations, dirs, out, work, own=None, kept=None):
+    acc, re_s, im_s = work
+    tec_scale = TEC_PHASE / freq[...]
+    turn_scale = jnp.broadcast_to(tec_scale * (1.0 / TWO_PI), (8, 128))
+    first = own is not None
     if first:
-        parts = stacked(tec[...])
-        own_out[...] = picked(parts, own[0], own[1])
+        parts, mine, own_out = own
+        own_out[...] = picked(parts, stations[mine], dirs[mine])
     else:
         acc[...] = jnp.zeros_like(acc)
 
@@ -123,8 +126,9 @@
             )
         left_re = data[0:1, :] - jnp.concatenate([a for a, _ in sums], axis=1)
         left_im = data[1:2, :] - jnp.concatenate([b for _, b in sums], axis=1)
-        res[0:1, lanes] = left_re
-        res[1:2, lanes] = left_im
+        if kept is not None:
+            kept[0][0:1, lanes] = left_re
+            kept[0][1:2, lanes] = left_im
         weight = data[2:3, :]
         proj = re_s[...] * (weight * left_im) - im_s[...] * (weight * left_re)
         high = proj.astype(BF16)
@@ -138,6 +142,9 @@
     numer, weight_sum = lax.fori_loop(
         0, BP // LB, chunk, (jnp.zeros((DP, SP), F32), jnp.zeros((SP, 128), F32))
     )
+    if kept is not None:
+        kept[1][0] = kept[0][0:1, 0:B]
+        kept[2][0] = kept[0][1:2, 0:B]
     numer_parts = stacked(numer * tec_scale)
     if first:
         weight_at = jnp.sum(weight_sum, axis=1, keepdims=True) * (tec_scale * tec_scale)
@@ -163,21 +170,23 @@
 
 def params():
     return dict(
-        compiler_params=pltpu.CompilerParams(),
+        compiler_params=pltpu.CompilerParams(vmem_limit_bytes=VMEM_LIMIT),
         interpret=pltpu.InterpretParams() if INTERPRET else False,
     )
 
 
 VM = pl.BlockSpec(memory_space=pltpu.VMEM)
 SM = pl.BlockSpec(memory_space=pltpu.SMEM)
-HB = pl.BlockSpec(memory_space=pl.ANY)
 
 
 def call(kernel, name, out_shape, in_specs, scratch=()):
     return pl.pallas_call(
         kernel,
         name=name,
-        out_shape=[jax.ShapeDtypeStruct(s, F32) for s in out_shape],
+        out_shape=[
+            s if isinstance(s, jax.ShapeDtypeStruct) else jax.ShapeDtypeStruct(s, F32)
+            for s in out_shape
+        ],
         in_specs=in_specs,
         out_specs=[VM] * len(out_shape),
         scratch_shapes=list(scratch),
@@ -185,30 +194,80 @@
     )
 
 
-def first_solver(scal, tec, vis, uvw, pairs, cols, stations, dirs, own):
-    def kernel(scal, tec, vis, uvw, pairs, cols, stations, dirs, own, out, res, own_out, re_s, im_s):
-        solver(scal, tec, vis, uvw, pairs, cols, stations, dirs, own, out, res, None, re_s, im_s, True, own_out)
-
+WORK = [
+    pltpu.VMEM((DP, 3 * SP), F32),
+    pltpu.VMEM((DP, LB), F32),
+    pltpu.VMEM((DP, LB), F32),
+]
+
+
+def first_solver(ids, freq, real, imag, weight, coords, pairs, directions, flux, start, points):
+    def kernel(
+        ids, freq, real, imag, weight, coords, pairs, directions, flux, start, points,
+        out, own, vis, uvw, ants, cols, stations, dirs, acc, re_s, im_s, rows, tall,
+    ):
+        vis[...] = jnp.zeros_like(vis)
+        vis[0:1, 0:B] = real[0]
+        vis[1:2, 0:B] = imag[0]
+        vis[2:3, 0:B] = weight[0]
+        uvw[...] = jnp.zeros_like(uvw)
+        uvw[:, 0:B] = coords[0] * freq[...]
+        ants[...] = jnp.full(ants.shape, -1, jnp.int32)
+        ants[:, 0:B] = pairs[...]
+        rows[...] = jnp.zeros_like(rows)
+        rows[0:3, 0:D] = directions[...]
+        rows[3:4, 0:D] = flux[...]
+        for c in range(4):
+            cols[c] = jnp.broadcast_to(rows[c : c + 1, :], (128, 256)).T[:DP, :]
+        tall[...] = jnp.zeros_like(tall)
+        tall[0:S, 0:D] = start[0]
+        parts = stacked(tall[...].T[:DP, :SP])
+        q = points[...]
+        s = jnp.floor((q.astype(F32) + 0.5) * (1.0 / D)).astype(jnp.int32)
+        d = q - s * D
+        blank = jnp.full((1, PW), -1, jnp.int32)
+        for c in range(CH):
+            stations[c] = blank
+            stations[c, 0:1, 0:PB] = s[:, c * PB : (c + 1) * PB]
+            dirs[c] = blank
+            dirs[c, 0:1, 0:PB] = d[:, c * PB : (c + 1) * PB]
+        solver(
+            freq, None, vis, uvw, ants, cols, stations, dirs, out, (acc, re_s, im_s),
+            own=(parts, ids[0], own),
+        )
+
+    i32 = lambda *shape: jax.ShapeDtypeStruct(shape, jnp.int32)
     return call(
         kernel,
         "first_solver",
-        [(CH, 1, 2 * PW), (2, BP), (1, PW)],
-        [SM] + [VM] * 8,
-        [pltpu.VMEM((DP, LB), F32), pltpu.VMEM((DP, LB), F32)],
-    )(scal, tec, vis, uvw, pairs, cols, stations, dirs, own)
-
-
-def next_solver(scal, tec, vis, uvw, pairs, cols, stations, dirs):
-    def kernel(scal, tec, vis, uvw, pairs, cols, stations, dirs, out, res, acc, re_s, im_s):
-        solver(scal, tec, vis, uvw, pairs, cols, stations, dirs, None, out, res, acc, re_s, im_s, False, None)
+        [
+            (CH, 1, 2 * PW), (1, PW), (3, BP), (3, BP), i32(2, BP), (4, DP, 128),
+            i32(CH, 1, PW), i32(CH, 1, PW),
+        ],
+        [SM] + [VM] * 10,
+        WORK + [pltpu.VMEM((8, 256), F32), pltpu.VMEM((128, 256), F32)],
+    )(ids, freq, real, imag, weight, coords, pairs, directions, flux, start, points)
+
+
+def next_solver(freq, tec, held, last):
+    def kernel(freq, tec, vis, uvw, ants, cols, stations, dirs, out, *refs):
+        if last:
+            real, imag, acc, re_s, im_s, left = refs
+            kept = (left, real, imag)
+        else:
+            acc, re_s, im_s = refs
+            kept = None
+        solver(
+            freq, tec, vis, uvw, ants, cols, stations, dirs, out, (acc, re_s, im_s), kept=kept
+        )
 
     return call(
         kernel,
-        "next_solver",
-        [(CH, 1, PW), (2, BP)],
-        [SM] + [VM] * 7,
-        [pltpu.VMEM((DP, 3 * SP), F32), pltpu.VMEM((DP, LB), F32), pltpu.VMEM((DP, LB), F32)],
-    )(scal, tec, vis, uvw, pairs, cols, stations, dirs)
+        "last_solver" if last else "next_solver",
+        [(CH, 1, PW)] + ([(1, 1, B), (1, 1, B)] if last else []),
+        [VM] * 8,
+        WORK + ([pltpu.VMEM((2, BP), F32)] if last else []),
+    )(freq, tec, *held)
 
 
 def final_place(vals, stations, dirs):
@@ -221,9 +280,10 @@
             return carry
 
         lax.fori_loop(0, CH // 2, place, 0)
-        out[...] = (acc[0:SP, :] + acc[SP : 2 * SP, :]) + acc[2 * SP : 3 * SP, :]
-
-    return call(kernel, "final_place", [(SP, DP)], [VM] * 3, [pltpu.VMEM((3 * SP, DP), F32)])(
+        whole = (acc[0:SP, :] + acc[SP : 2 * SP, :]) + acc[2 * SP : 3 * SP, :]
+        out[0] = whole[:S, :D]
+
+    return call(kernel, "final_place", [(1, S, D)], [VM] * 3, [pltpu.VMEM((3 * SP, DP), F32)])(
         vals, stations, dirs
     )[0]
 
@@ -248,43 +308,22 @@
     return call(kernel, "own_target", [(1, PW)], [VM] * 3)(arrived, own, denominator)[0], denominator
 
 
-CUTS = ((0, 96), (96, 96), (192, 96), (288, 87))
-
-
-def basis_copies(basis, held, sems):
-    copies = [
-        pltpu.make_async_copy(basis.at[pl.ds(a, n)], held.at[pl.ds(a, n)], sems.at[i])
-        for i, (a, n) in enumerate(CUTS)
-    ]
-    for copy in copies:
-        copy.start()
-    return copies
-
-
-def groups_of(a, n):
-    return [(r, min(8, a + n - r)) for r in range(a, a + n, 8)]
-
-
-BASIS_SCRATCH = [pltpu.VMEM((PB, K), F32), pltpu.SemaphoreType.DMA((len(CUTS),))]
-
-
-def basis_partial(norm, target, near, far, weight, basis):
-    def kernel(norm, target, near, far, weight, basis, out, held, sems, tall):
-        copies = basis_copies(basis, held, sems)
-        x = (target[...] + SMOOTHING * (near[...] + far[...])) / norm[0]
+GROUPS = [(r, min(8, PB - r)) for r in range(0, PB, 8)]
+
+
+def basis_partial(ids, slots, target, near, far, weight, basis):
+    def kernel(ids, target, near, far, weight, basis, out, tall):
+        slot = ids[1]
+        ends = (slot == 0).astype(F32) + (slot == slots - 1).astype(F32)
+        x = (target[...] + SMOOTHING * (near[...] + far[...])) / (1.0 + SMOOTHING * (2.0 - ends))
         tall[...] = jnp.broadcast_to(x, (128, PW)).T
         total = jnp.zeros((8, K), F32)
-        tail = jnp.zeros((1, K), F32)
-        for copy, (a, n) in zip(copies, CUTS):
-            copy.wait()
-            for r, m in groups_of(a, n):
-                column = tall[r : r + m, :]
-                piece = held[r : r + m, :] * jnp.concatenate([column] * (K // 128), axis=1)
-                if m == 8:
-                    total = total + piece
-                else:
-                    tail = jnp.sum(piece, axis=0, keepdims=True)
-        row = (jnp.sum(total, axis=0, keepdims=True) + tail) * weight[...]
+        for r, m in GROUPS:
+            piece = basis[r : r + m, :] * jnp.concatenate([tall[r : r + m, :]] * (K // 128), axis=1)
+            if m == 8:
+                total = total + piece
+        row = jnp.sum(total, axis=0, keepdims=True) + jnp.sum(piece, axis=0, keepdims=True)
+        row = row * weight[...]
         for c in range(CH):
             out[c] = row
 
@@ -292,26 +331,23 @@
         kernel,
         "basis_partial",
         [(CH, 1, K)],
-        [SM] + [VM] * 4 + [HB],
-        BASIS_SCRATCH + [pltpu.VMEM((PW, 128), F32)],
-    )(norm, target, near, far, weight, basis)[0]
+        [SM] + [VM] * 5,
+        [pltpu.VMEM((PW, 128), F32)],
+    )(ids, target, near, far, weight, basis)[0]
 
 
 def own_screen(arrived, basis):
-    def kernel(arrived, basis, coef, own, out, held, sems, tall):
-        copies = basis_copies(basis, held, sems)
+    def kernel(arrived, basis, coef, own, out, tall):
         row = jnp.sum(arrived[...], axis=0)
         coef[...] = row
         spread = jnp.broadcast_to(row, (8, K))
         tall[PW - 16 : PW, :] = jnp.zeros((16, 128), F32)
-        for copy, (a, n) in zip(copies, CUTS):
-            copy.wait()
-            for r, m in groups_of(a, n):
-                piece = held[r : r + m, :] * spread[0:m, :]
-                parts = [piece[:, k : k + 128] for k in range(0, K, 128)]
-                while len(parts) > 1:
-                    parts = [u + v for u, v in zip(parts[0::2], parts[1::2])]
-                tall[r : r + m, :] = parts[0]
+        for r, m in GROUPS:
+            piece = basis[r : r + m, :] * spread[0:m, :]
+            parts = [piece[:, k : k + 128] for k in range(0, K, 128)]
+            while len(parts) > 1:
+                parts = [u + v for u, v in zip(parts[0::2], parts[1::2])]
+            tall[r : r + m, :] = parts[0]
         line = jnp.sum(tall[...].T, axis=0, keepdims=True)
         own[...] = line
         for c in range(CH):
@@ -321,8 +357,8 @@
         kernel,
         "own_screen",
         [(1, K), (1, PW), (CH, 1, PW)],
-        [VM, HB],
-        BASIS_SCRATCH + [pltpu.VMEM((PW, 128), F32)],
+        [VM, VM],
+        [pltpu.VMEM((PW, 128), F32)],
     )(arrived, basis)
 
 
@@ -344,64 +380,29 @@
     eigen_basis,
     eigen_weight,
 ):
-    frequency = channel_frequency[0]
-    tec_scale = TEC_PHASE / frequency
-    scal = jnp.stack([tec_scale * (1.0 / TWO_PI), tec_scale])
-    vis = jnp.concatenate(
-        [measured_real[0], measured_imaginary[0], measured_weight[0]], axis=0
-    )
-    vis = jnp.pad(vis, ((0, 0), (0, BP - B)))
-    uvw = jnp.pad(baseline_vectors[0] * frequency, ((0, 0), (0, BP - B)))
-    pairs = jnp.pad(antenna_pairs, ((0, 0), (0, BP - B)), constant_values=-1)
-    cols = jnp.concatenate([directions, direction_flux], axis=0)
-    cols = jnp.broadcast_to(jnp.pad(cols, ((0, 0), (0, DP - D)))[:, :, None], (4, DP, 128))
-    tec_start = jnp.pad(electron_content_start[0].T, ((0, DP - D), (0, SP - S)))
-    points = pierce_station_direction[0].reshape(CH, 1, PB)
-    fill = ((0, 0), (0, 0), (0, PW - PB))
-    stations = jnp.pad(points // D, fill, constant_values=-1)
-    dirs = jnp.pad(points % D, fill, constant_values=-1)
-    mine = lax.axis_index("chan")
-    own_points = jnp.stack(
-        [
-            lax.dynamic_index_in_dim(stations, mine, 0, keepdims=False),
-            lax.dynamic_index_in_dim(dirs, mine, 0, keepdims=False),
-        ]
-    )
-    slot = lax.axis_index("slot")
     slots = lax.axis_size("slot")
-    inside = (slot > 0).astype(F32) + (slot < slots - 1).astype(F32)
-    norm = (1.0 + SMOOTHING * inside).reshape(1)
+    ids = jnp.stack([lax.axis_index("chan"), lax.axis_index("slot")]).astype(jnp.int32)
+    freq = channel_frequency.reshape(1, 1)
     weight = eigen_weight[None, :]
     near_pairs = [(i, i ^ 1) for i in range(slots) if i ^ 1 < slots]
     far_pairs = [(i, i - 1 if i % 2 == 0 else i + 1) for i in range(1, slots - 1)]
     far_pairs = [(i, j) for i, j in far_pairs if 0 <= j < slots]
-    own = None
+    sent, own, *held = first_solver(
+        ids, freq, measured_real, measured_imaginary, measured_weight, baseline_vectors,
+        antenna_pairs, directions, direction_flux, electron_content_start, pierce_station_direction,
+    )
     denominator = None
-    gathered = None
-    coefficients = None
-    residual = None
     for iteration in range(ITERS):
-        if iteration == 0:
-            sent, residual, own = first_solver(
-                scal, tec_start, vis, uvw, pairs, cols, stations, dirs, own_points
-            )
-        else:
-            sent, residual = next_solver(
-                scal, gathered, vis, uvw, pairs, cols, stations, dirs
-            )
+        if iteration > 0:
+            sent, *left = next_solver(freq, gathered, held, iteration == ITERS - 1)
         target, denominator = own_target(exchange(sent), own, denominator)
         far = lax.ppermute(target, "slot", far_pairs)
         near = lax.ppermute(target, "slot", near_pairs)
-        partial = basis_partial(norm, target, near, far, weight, eigen_basis)
+        partial = basis_partial(ids, slots, target, near, far, weight, eigen_basis)
         coefficients, own, spread = own_screen(exchange(partial), eigen_basis)
         gathered = exchange(spread)
-    tec_final = final_place(gathered, stations, dirs)[:S, :D]
-    return (
-        tec_final[None],
-        coefficients,
-        residual[0:1, :B][None],
-        residual[1:2, :B][None],
-    )
+    tec_final = final_place(gathered, held[4], held[5])
+    return tec_final, coefficients, left[0], left[1]
 
 
 def solution(mesh):

time: 331 us -> 275 us (0.83)
  Pallas kernels: 96.7 us -> 64.1 us
  waiting for transfers between devices: 24.6 us -> 16.8 us
  other arithmetic: 6.35 us -> 0.07 us
  starting transfers between devices: 28.2 us -> 24.5 us
    pallas_call x13, Pallas kernels: 90.9 us -> 63.9 us  [the longest x3 40.7 us: next_solver(): call(kernel, 'last_solver' if last else 'next_solver', [(CH, 1, PW)] + ([...]
    all_to_all x1 -> x0, waiting for transfers between devices: 6.95 us -> none  [exchange(): lax.all_to_all(value, 'chan', split_axis=0, concat_axis=0, tiled=True)]
    pallas_call x3, Pallas kernels: 4.29 us -> 0.16 us  [own_target(): call(kernel, 'own_target', [(1, PW)], [VM] * 3)(arrived, own, denominator)]
    pad x5 -> x0, local copies, waits for them, and re-layouts: 3.89 us -> none  [the longest x1 1.32 us: per_device(): pairs = jnp.pad(antenna_pairs, ((0, 0), (0, BP - B)), constant_values=-1)]
    all_to_all x1 -> x0, starting transfers between devices: 3.64 us -> none  [exchange(): lax.all_to_all(value, 'chan', split_axis=0, concat_axis=0, tiled=True)]
    unnamed x22 -> x25, local copies, waits for them, and re-layouts: 6.15 us -> 9.79 us
    all_to_all x11 -> x12, blocking collectives: 159 us -> 157 us  [exchange(): lax.all_to_all(value, 'chan', split_axis=0, concat_axis=0, tiled=True)]
  transfers between devices with their start and end apart: 9 -> 8, of which waited for: 5 -> 4; matrix products, arithmetic and copies ran while one was open for 0% -> 0% of each run, Pallas kernels for 0% -> 0%
where the time goes in v1:
time: 275 us; the launch traced here: 273 us
  blocking collectives  157 us (57%)
  Pallas kernels  64.1 us (23%)
  starting transfers between devices  24.5 us (9%)
  waiting for transfers between devices  16.8 us (6%)
  local copies, waits for them, and re-layouts  9.79 us (4%)
    all_to_all x12, blocking collectives, exchange(): lax.all_to_all(value, 'chan', split_axis=0, concat_axis=0, tiled=True)  157 us
    pallas_call x3, Pallas kernels, next_solver(): call(kernel, 'last_solver' if last else 'next_solver', [(CH, 1, PW)] + ([...  40.7 us
    ppermute x4, starting transfers between devices, per_device(): far = lax.ppermute(target, 'slot', far_pairs)  24.1 us
    ppermute x4, waiting for transfers between devices, per_device(): far = lax.ppermute(target, 'slot', far_pairs)  16.8 us
    pallas_call x1, Pallas kernels, first_solver(): call(kernel, 'first_solver', [(CH, 1, 2 * PW), (1, PW), (3, BP), (3, BP),...  11.2 us
    unnamed x25, local copies, waits for them, and re-layouts  9.79 us
  transfers between devices with their start and end apart: 8, of which 4 were waited for; matrix products, arithmetic and copies ran while one was open for 0% of the time, Pallas kernels for 0%

profile of v1, /device:TPU:7, one launch (start us, length us, event | category | flops | bytes accessed | tf_op | source)
XLA Modules:
  0.0 273.4 jit_solution(8764892754008728379)
XLA Ops:
  7.9 11.2 %first_solver.1 = (f32[32,1,768]{2,1,0:T(1,128)S(1)}, f32[1,384]{1,0:T(1,128)S(1)}, f32[3,1792]{1,0:T(4,128)S(1)}, f32[3,1792]{1,0:T(4,128)S(1)}, s32[2,1792]{1,...) custom-call(s32[2]{0:T(128)S(1)} %pad_add_fusion.ids, ...), custom_call_target="tpu_custom_call" | custom-call | tf_op jit(solution)/shard_map/first_solver/pallas_call | solution.py:240
  19.1 17.4 %all_to_all.60.arrived = f32[32,1,768]{2,1,0:T(1,128)S(1)} all-to-all(f32[32,1,768]{2,1,0:T(1,128)S(1)} %get-tuple-element.25), channel_id=1, replica_groups=mesh['chan'=32,'slot'=8] {'chan'}, dimensions={0} | all-to-all | bytes 196608 | tf_op jit(solution)/shard_map/all_to_all | solution.py:366
  36.5 6.0 %collective-permute-start.1 = (f32[1,384]{1,0:T(1,128)S(1)}, f32[1,384]{1,0:T(1,128)S(1)}, u32[]{:S(2)}, u32[]{:S(2)}) collective-permute-start(f32[1,384]{1,0:T(1,128)S(1)} %get-tuple-element.27.target), channel_id=1, source_target_pairs={{1,2},{2,1},{3,4},{4,3},{5,6},{6,5},{9,10},{10,9},{11,12},{12,11},... | collective-permute-start | bytes 4616 | tf_op jit(solution)/shard_map/ppermute | solution.py:399
  42.7 4.2 %collective-permute-done.1.far = f32[1,384]{1,0:T(1,128)S(1)} collective-permute-done((f32[1,384]{1,0:T(1,128)S(1)}, f32[1,384]{1,0:T(1,128)S(1)}, u32[]{:S(2)}, u32[]{:S(2)}) %collective-permute-start.1) | collective-permute-done | bytes 1568 | tf_op jit(solution)/shard_map/ppermute | solution.py:399
  46.9 1.9 copy-done
  50.4 15.7 %all_to_all.61.arrived = f32[32,1,2048]{2,1,0:T(1,128)S(1)} all-to-all(f32[32,1,2048]{2,1,0:T(1,128)S(1)} %basis_partial.4), channel_id=1, replica_groups=mesh['chan'=32,'slot'=8] {'chan'}, dimensions={0} | all-to-all | bytes 524288 | tf_op jit(solution)/shard_map/all_to_all | solution.py:366
  66.1 1.0 own_screen.4
  67.1 11.0 %all_to_all.62.tec = f32[32,1,384]{2,1,0:T(1,128)S(1)} all-to-all(f32[32,1,384]{2,1,0:T(1,128)S(1)} %get-tuple-element.28), channel_id=1, replica_groups=mesh['chan'=32,'slot'=8] {'chan'}, dimensions={0} | all-to-all | bytes 98304 | tf_op jit(solution)/shard_map/all_to_all | solution.py:366
  78.1 13.4 %next_solver.2 = f32[32,1,384]{2,1,0:T(1,128)S(1)} custom-call(f32[1,1]{1,0:T(1,128)} %bitcast.5.freq, f32[32,1,384]{2,1,0:T(1,128)S(1)} %all_to_all.62.tec, f32[3,1792]{1,0:T(4,128)S(1)} %get-tuple-element.29.vis, f32[3,1792]{1,0:T(4,128)S(1)} %get-tuple-element.30.uvw, s32[2,1792]{1,0:T(2,128)S(1)} %get-tuple-element.31.ants, ...), custom_call_target="tpu_custom_call" | custom-call | tf_op jit(solution)/shard_map/next_solver/pallas_call | solution.py:264
  91.6 10.9 %all_to_all.63.arrived = f32[32,1,384]{2,1,0:T(1,128)S(1)} all-to-all(f32[32,1,384]{2,1,0:T(1,128)S(1)} %next_solver.2), channel_id=1, replica_groups=mesh['chan'=32,'slot'=8] {'chan'}, dimensions={0} | all-to-all | bytes 98304 | tf_op jit(solution)/shard_map/all_to_all | solution.py:366
  102.5 6.0 %collective-permute-start.3 = (f32[1,384]{1,0:T(1,128)S(1)}, f32[1,384]{1,0:T(1,128)S(1)}, u32[]{:S(2)}, u32[]{:S(2)}) collective-permute-start(f32[1,384]{1,0:T(1,128)S(1)} %own_target.3.target), channel_id=1, source_target_pairs={{1,2},{2,1},{3,4},{4,3},{5,6},{6,5},{9,10},{10,9},{11,12},{12,11},... | collective-permute-start | bytes 4616 | tf_op jit(solution)/shard_map/ppermute | solution.py:399
  108.6 4.2 %collective-permute-done.3.far = f32[1,384]{1,0:T(1,128)S(1)} collective-permute-done((f32[1,384]{1,0:T(1,128)S(1)}, f32[1,384]{1,0:T(1,128)S(1)}, u32[]{:S(2)}, u32[]{:S(2)}) %collective-permute-start.3) | collective-permute-done | bytes 1568 | tf_op jit(solution)/shard_map/ppermute | solution.py:399
  112.8 0.9 basis_partial.5
  113.8 15.6 %all_to_all.64.arrived = f32[32,1,2048]{2,1,0:T(1,128)S(1)} all-to-all(f32[32,1,2048]{2,1,0:T(1,128)S(1)} %basis_partial.5), channel_id=1, replica_groups=mesh['chan'=32,'slot'=8] {'chan'}, dimensions={0} | all-to-all | bytes 524288 | tf_op jit(solution)/shard_map/all_to_all | solution.py:366
  129.4 1.0 own_screen.5
  130.4 11.0 %all_to_all.65.tec = f32[32,1,384]{2,1,0:T(1,128)S(1)} all-to-all(f32[32,1,384]{2,1,0:T(1,128)S(1)} %get-tuple-element.37), channel_id=1, replica_groups=mesh['chan'=32,'slot'=8] {'chan'}, dimensions={0} | all-to-all | bytes 98304 | tf_op jit(solution)/shard_map/all_to_all | solution.py:366
  141.4 13.4 %next_solver.3 = f32[32,1,384]{2,1,0:T(1,128)S(1)} custom-call(f32[1,1]{1,0:T(1,128)} %bitcast.6.freq, f32[32,1,384]{2,1,0:T(1,128)S(1)} %all_to_all.65.tec, f32[3,1792]{1,0:T(4,128)S(1)} %get-tuple-element.29.vis, f32[3,1792]{1,0:T(4,128)S(1)} %get-tuple-element.30.uvw, s32[2,1792]{1,0:T(2,128)S(1)} %get-tuple-element.31.ants, ...), custom_call_target="tpu_custom_call" | custom-call | tf_op jit(solution)/shard_map/next_solver/pallas_call | solution.py:264
  154.8 10.9 %all_to_all.66.arrived = f32[32,1,384]{2,1,0:T(1,128)S(1)} all-to-all(f32[32,1,384]{2,1,0:T(1,128)S(1)} %next_solver.3), channel_id=1, replica_groups=mesh['chan'=32,'slot'=8] {'chan'}, dimensions={0} | all-to-all | bytes 98304 | tf_op jit(solution)/shard_map/all_to_all | solution.py:366
  165.8 6.0 %collective-permute-start.5 = (f32[1,384]{1,0:T(1,128)S(1)}, f32[1,384]{1,0:T(1,128)S(1)}, u32[]{:S(2)}, u32[]{:S(2)}) collective-permute-start(f32[1,384]{1,0:T(1,128)S(1)} %own_target.4.target), channel_id=1, source_target_pairs={{1,2},{2,1},{3,4},{4,3},{5,6},{6,5},{9,10},{10,9},{11,12},{12,11},... | collective-permute-start | bytes 4616 | tf_op jit(solution)/shard_map/ppermute | solution.py:399
  171.9 4.2 %collective-permute-done.5.far = f32[1,384]{1,0:T(1,128)S(1)} collective-permute-done((f32[1,384]{1,0:T(1,128)S(1)}, f32[1,384]{1,0:T(1,128)S(1)}, u32[]{:S(2)}, u32[]{:S(2)}) %collective-permute-start.5) | collective-permute-done | bytes 1568 | tf_op jit(solution)/shard_map/ppermute | solution.py:399
  176.1 0.9 basis_partial.6
  177.0 15.6 %all_to_all.67.arrived = f32[32,1,2048]{2,1,0:T(1,128)S(1)} all-to-all(f32[32,1,2048]{2,1,0:T(1,128)S(1)} %basis_partial.6), channel_id=1, replica_groups=mesh['chan'=32,'slot'=8] {'chan'}, dimensions={0} | all-to-all | bytes 524288 | tf_op jit(solution)/shard_map/all_to_all | solution.py:366
  192.7 1.0 own_screen.6
  193.6 11.0 %all_to_all.68.tec = f32[32,1,384]{2,1,0:T(1,128)S(1)} all-to-all(f32[32,1,384]{2,1,0:T(1,128)S(1)} %get-tuple-element.39), channel_id=1, replica_groups=mesh['chan'=32,'slot'=8] {'chan'}, dimensions={0} | all-to-all | bytes 98304 | tf_op jit(solution)/shard_map/all_to_all | solution.py:366
  204.6 13.8 %last_solver.1 = (f32[32,1,384]{2,1,0:T(1,128)S(1)}, f32[1,1,1770]{2,1,0:T(1,128)}, f32[1,1,1770]{2,1,0:T(1,128)}) custom-call(f32[1,1]{1,0:T(1,128)} %bitcast.7.freq, f32[32,1,384]{2,1,0:T(1,128)S(1)} %all_to_all.68.tec, f32[3,1792]{1,0:T(4,128)S(1)} %get-tuple-element.29.vis, f32[3,1792]{1,0:T(4,128)S(1)} %get-tuple-element.30.uvw, ...), custom_call_target="tpu_custom_call" | custom-call | tf_op jit(solution)/shard_map/last_solver/pallas_call | solution.py:264
  218.4 10.9 %all_to_all.69.arrived = f32[32,1,384]{2,1,0:T(1,128)S(1)} all-to-all(f32[32,1,384]{2,1,0:T(1,128)S(1)} %get-tuple-element.40), channel_id=1, replica_groups=mesh['chan'=32,'slot'=8] {'chan'}, dimensions={0} | all-to-all | bytes 98304 | tf_op jit(solution)/shard_map/all_to_all | solution.py:366
  229.3 6.0 %collective-permute-start.7 = (f32[1,384]{1,0:T(1,128)S(1)}, f32[1,384]{1,0:T(1,128)S(1)}, u32[]{:S(2)}, u32[]{:S(2)}) collective-permute-start(f32[1,384]{1,0:T(1,128)S(1)} %own_target.5.target), channel_id=1, source_target_pairs={{1,2},{2,1},{3,4},{4,3},{5,6},{6,5},{9,10},{10,9},{11,12},{12,11},... | collective-permute-start | bytes 4616 | tf_op jit(solution)/shard_map/ppermute | solution.py:399
  235.5 4.2 %collective-permute-done.7.far = f32[1,384]{1,0:T(1,128)S(1)} collective-permute-done((f32[1,384]{1,0:T(1,128)S(1)}, f32[1,384]{1,0:T(1,128)S(1)}, u32[]{:S(2)}, u32[]{:S(2)}) %collective-permute-start.7) | collective-permute-done | bytes 1568 | tf_op jit(solution)/shard_map/ppermute | solution.py:399
  240.6 15.6 %all_to_all.70.arrived = f32[32,1,2048]{2,1,0:T(1,128)S(1)} all-to-all(f32[32,1,2048]{2,1,0:T(1,128)S(1)} %basis_partial.7), channel_id=1, replica_groups=mesh['chan'=32,'slot'=8] {'chan'}, dimensions={0} | all-to-all | bytes 524288 | tf_op jit(solution)/shard_map/all_to_all | solution.py:366
  256.3 1.0 own_screen.7
  257.3 11.0 %all_to_all.71.vals = f32[32,1,384]{2,1,0:T(1,128)S(1)} all-to-all(f32[32,1,384]{2,1,0:T(1,128)S(1)} %get-tuple-element.42), channel_id=1, replica_groups=mesh['chan'=32,'slot'=8] {'chan'}, dimensions={0} | all-to-all | bytes 98304 | tf_op jit(solution)/shard_map/all_to_all | solution.py:366
  268.3 4.5 %final_place.1 = f32[1,60,200]{2,1,0:T(8,128)S(1)} custom-call(f32[32,1,384]{2,1,0:T(1,128)S(1)} %all_to_all.71.vals, s32[32,1,384]{2,1,0:T(1,128)S(1)} %get-tuple-element.33.stations, s32[32,1,384]{2,1,0:T(1,128)S(1)} %get-tuple-element.34.dirs), custom_call_target="tpu_custom_call" | custom-call | tf_op jit(solution)/shard_map/final_place/pallas_call | solution.py:286
  (39 shorter events, 10.4 us)
Async XLA Ops:
  2.9 0.8 copy-start.4
  3.7 0.7 copy-start.5
  4.4 0.7 copy-start.6
  5.1 0.7 copy-start.7
  5.8 0.7 copy-start.8
  6.5 0.7 copy-start.9
  7.2 0.7 copy-start.10
  36.5 10.3 %collective-permute-start.1 = (f32[1,384]{1,0:T(1,128)S(1)}, f32[1,384]{1,0:T(1,128)S(1)}, u32[]{:S(2)}, u32[]{:S(2)}) collective-permute-start(f32[1,384]{1,0:T(1,128)S(1)} %get-tuple-element.27.target), channel_id=1, source_target_pairs={{1,2},{2,1},{3,4},{4,3},{5,6},{6,5},{9,10},{10,9},{11,12},{12,11},... | collective-permute-start | bytes 4616 | tf_op jit(solution)/shard_map/ppermute | solution.py:399
  42.6 4.3 %collective-permute-start = (f32[1,384]{1,0:T(1,128)S(1)}, f32[1,384]{1,0:T(1,128)S(1)}, u32[]{:S(2)}, u32[]{:S(2)}) collective-permute-start(f32[1,384]{1,0:T(1,128)S(1)} %get-tuple-element.27.target), channel_id=1, source_target_pairs={{0,1},{1,0},{2,3},{3,2},{4,5},{5,4},{6,7},{7,6},{8,9},{9,8},{10,11... | collective-permute-start | bytes 4616 | tf_op jit(solution)/shard_map/ppermute | solution.py:400
  46.9 1.9 copy-start
  48.8 0.7 copy-start.2
  49.5 16.7 %copy-start.1 = (f32[375,2048]{1,0:T(8,128)S(1)}, f32[375,2048]{1,0:T(8,128)}, u32[]{:S(2)}) copy-start(f32[375,2048]{1,0:T(8,128)} %basis.15) | copy-start | bytes 9216004
  50.4 62.5 %copy-start.3 = (f32[2048]{0:T(1024)S(1)}, f32[2048]{0:T(1024)}, u32[]{:S(2)}) copy-start(f32[2048]{0:T(1024)} %param.23) | copy-start | bytes 24580
  102.5 10.3 %collective-permute-start.3 = (f32[1,384]{1,0:T(1,128)S(1)}, f32[1,384]{1,0:T(1,128)S(1)}, u32[]{:S(2)}, u32[]{:S(2)}) collective-permute-start(f32[1,384]{1,0:T(1,128)S(1)} %own_target.3.target), channel_id=1, source_target_pairs={{1,2},{2,1},{3,4},{4,3},{5,6},{6,5},{9,10},{10,9},{11,12},{12,11},... | collective-permute-start | bytes 4616 | tf_op jit(solution)/shard_map/ppermute | solution.py:399
  108.5 4.3 %collective-permute-start.2 = (f32[1,384]{1,0:T(1,128)S(1)}, f32[1,384]{1,0:T(1,128)S(1)}, u32[]{:S(2)}, u32[]{:S(2)}) collective-permute-start(f32[1,384]{1,0:T(1,128)S(1)} %own_target.3.target), channel_id=1, source_target_pairs={{0,1},{1,0},{2,3},{3,2},{4,5},{5,4},{6,7},{7,6},{8,9},{9,8},{10,11... | collective-permute-start | bytes 4616 | tf_op jit(solution)/shard_map/ppermute | solution.py:400
  165.8 10.3 %collective-permute-start.5 = (f32[1,384]{1,0:T(1,128)S(1)}, f32[1,384]{1,0:T(1,128)S(1)}, u32[]{:S(2)}, u32[]{:S(2)}) collective-permute-start(f32[1,384]{1,0:T(1,128)S(1)} %own_target.4.target), channel_id=1, source_target_pairs={{1,2},{2,1},{3,4},{4,3},{5,6},{6,5},{9,10},{10,9},{11,12},{12,11},... | collective-permute-start | bytes 4616 | tf_op jit(solution)/shard_map/ppermute | solution.py:399
  171.8 4.3 %collective-permute-start.4 = (f32[1,384]{1,0:T(1,128)S(1)}, f32[1,384]{1,0:T(1,128)S(1)}, u32[]{:S(2)}, u32[]{:S(2)}) collective-permute-start(f32[1,384]{1,0:T(1,128)S(1)} %own_target.4.target), channel_id=1, source_target_pairs={{0,1},{1,0},{2,3},{3,2},{4,5},{5,4},{6,7},{7,6},{8,9},{9,8},{10,11... | collective-permute-start | bytes 4616 | tf_op jit(solution)/shard_map/ppermute | solution.py:400
  229.3 10.3 %collective-permute-start.7 = (f32[1,384]{1,0:T(1,128)S(1)}, f32[1,384]{1,0:T(1,128)S(1)}, u32[]{:S(2)}, u32[]{:S(2)}) collective-permute-start(f32[1,384]{1,0:T(1,128)S(1)} %own_target.5.target), channel_id=1, source_target_pairs={{1,2},{2,1},{3,4},{4,3},{5,6},{6,5},{9,10},{10,9},{11,12},{12,11},... | collective-permute-start | bytes 4616 | tf_op jit(solution)/shard_map/ppermute | solution.py:399
  235.4 4.3 %collective-permute-start.6 = (f32[1,384]{1,0:T(1,128)S(1)}, f32[1,384]{1,0:T(1,128)S(1)}, u32[]{:S(2)}, u32[]{:S(2)}) collective-permute-start(f32[1,384]{1,0:T(1,128)S(1)} %own_target.5.target), channel_id=1, source_target_pairs={{0,1},{1,0},{2,3},{3,2},{4,5},{5,4},{6,7},{7,6},{8,9},{9,8},{10,11... | collective-permute-start | bytes 4616 | tf_op jit(solution)/shard_map/ppermute | solution.py:400

commit v2 on v1

--- a/solution.py
+++ b/solution.py
@@ -16,12 +16,14 @@
 SP, DP, BP = 64, 208, 1792
 CH, PB, PW = 32, 375, 384
 LB = 256
+NB = 16
 F32, BF16 = jnp.float32, jnp.bfloat16
 
-COS = (0.9999999891722796, -19.73920453209451, 64.93911898389003, -85.45016555018871,
-       60.167831730030905, -25.968313296519984, 6.5296104072911)
-SIN = (6.283185272722459, -41.341697068957856, 81.60502462263176, -76.70155117699308,
-       42.016165826534845, -14.868611009881327, 3.199693676305946)
+COS = (1.4142134965650244, -6.978850988240614, 5.7394611707149, -1.883562987515013, 0.3106981922394431)
+SIN = (4.4428828341499464, -7.308241154547178, 3.606288958237895, -0.8457635962132565, 0.10920575375700989)
+
+PRODUCTS = ((0, 0), (0, 1), (1, 0), (1, 1), (0, 2), (2, 0))
+GP = 32
 
 
 def horner(coefficients, z):
@@ -50,10 +52,12 @@
     return lax.broadcasted_iota(jnp.int32, (rows, numbers.shape[1]), 0) == numbers
 
 
+def joined(blocks, i):
+    return jnp.concatenate([blocks[NB * i + k] for k in range(NB)], axis=1)
+
+
 def placed_parts(vals, stations, dirs, i):
-    v = jnp.concatenate([vals[2 * i], vals[2 * i + 1]], axis=1)
-    s = jnp.concatenate([stations[2 * i], stations[2 * i + 1]], axis=1)
-    d = jnp.concatenate([dirs[2 * i], dirs[2 * i + 1]], axis=1)
+    v, s, d = joined(vals, i), joined(stations, i), joined(dirs, i)
     at = one_hot(s, SP)
     by_station = jnp.concatenate(
         [jnp.where(at, part, 0.0).astype(BF16) for part in split3(v)], axis=0
@@ -72,51 +76,49 @@
     return jnp.concatenate([part.astype(BF16) for part in split3(field)], axis=1)
 
 
-def solver(freq, tec, vis, uvw, pairs, cols, stations, dirs, out, work, own=None, kept=None):
+def solver(freq, tec, vis, base, coords, pairs, cols, stations, dirs, out, work, own=None, kept=None):
     acc, re_s, im_s = work
     tec_scale = TEC_PHASE / freq[...]
     turn_scale = jnp.broadcast_to(tec_scale * (1.0 / TWO_PI), (8, 128))
     first = own is not None
     if first:
-        parts, mine, own_out = own
-        own_out[...] = picked(parts, stations[mine], dirs[mine])
+        tec_parts, base_parts, mine, own_out = own
+        own_out[...] = picked(tec_parts, stations[mine], dirs[mine])
+        parts = jnp.concatenate([tec_parts, base_parts], axis=1)
     else:
-        acc[...] = jnp.zeros_like(acc)
+        acc[...] = base[...]
 
         def place(i, carry):
             by_station, by_direction = placed_parts(tec, stations, dirs, i)
-            acc[...] += dot_nt(by_direction, by_station)
+            acc[:, 0 : 3 * SP] += dot_nt(by_direction, by_station)
             return carry
 
-        lax.fori_loop(0, CH // 2, place, 0)
+        lax.fori_loop(0, CH // NB, place, 0)
         parts = acc[...].astype(BF16)
 
     def chunk(j, carry):
         numer, weight_sum = carry
-        lanes = pl.ds(pl.multiple_of(j * LB, LB), LB)
+        lanes = pl.ds(j * LB, LB)
         first_at = one_hot(pairs[0:1, lanes], SP)
         second_at = one_hot(pairs[1:2, lanes], SP)
         sign = jnp.where(first_at, 1.0, jnp.where(second_at, -1.0, 0.0)).astype(BF16)
-        mixed = dot_nn(parts, jnp.concatenate([sign, sign, sign], axis=0))
-        coords = uvw[:, lanes]
+        mixed = dot_nn(
+            parts, jnp.concatenate([sign, sign, sign, coords[:, lanes].astype(BF16)], axis=0)
+        )
         data = vis[:, lanes]
         sums = []
         for h in range(LB // 128):
-            c = coords[:, h * 128 : (h + 1) * 128]
             sum_re = jnp.zeros((8, 128), F32)
             sum_im = jnp.zeros((8, 128), F32)
             for g in range(DP // 8):
                 rows = slice(8 * g, 8 * g + 8)
-                turns = (
-                    cols[0, rows, :] * c[0:1, :]
-                    + cols[1, rows, :] * c[1:2, :]
-                    + cols[2, rows, :] * c[2:3, :]
-                ) + turn_scale * mixed[rows, h * 128 : (h + 1) * 128]
+                turns = turn_scale * mixed[rows, h * 128 : (h + 1) * 128]
                 r = turns - jnp.round(turns)
                 z = r * r
-                flux = cols[3, rows, :]
-                re = flux * horner(COS, z)
-                im = flux * (r * horner(SIN, z))
+                flux = cols[rows, :]
+                half_sin = r * horner(SIN, z)
+                re = flux - flux * (half_sin * half_sin)
+                im = flux * (half_sin * horner(COS, z))
                 re_s[rows, h * 128 : (h + 1) * 128] = re
                 im_s[rows, h * 128 : (h + 1) * 128] = im
                 sum_re = sum_re + re
@@ -139,33 +141,32 @@
             weight_sum = weight_sum + (touched[:, :128] + touched[:, 128:])
         return numer, weight_sum
 
-    numer, weight_sum = lax.fori_loop(
-        0, BP // LB, chunk, (jnp.zeros((DP, SP), F32), jnp.zeros((SP, 128), F32))
-    )
+    numer, weight_sum = jnp.zeros((DP, SP), F32), jnp.zeros((SP, 128), F32)
+    for j in range(BP // LB):
+        numer, weight_sum = chunk(j, (numer, weight_sum))
     if kept is not None:
         kept[1][0] = kept[0][0:1, 0:B]
         kept[2][0] = kept[0][1:2, 0:B]
     numer_parts = stacked(numer * tec_scale)
     if first:
         weight_at = jnp.sum(weight_sum, axis=1, keepdims=True) * (tec_scale * tec_scale)
-        flux_col = cols[3, :, 0:1]
+        flux_col = cols[:, 0:1]
         flux_col = flux_col * flux_col
 
     def pick(i, carry):
-        s = jnp.concatenate([stations[2 * i], stations[2 * i + 1]], axis=1)
-        d = jnp.concatenate([dirs[2 * i], dirs[2 * i + 1]], axis=1)
+        s, d = joined(stations, i), joined(dirs, i)
         got = picked(numer_parts, s, d)
-        out[2 * i, 0:1, 0:PW] = got[:, :PW]
-        out[2 * i + 1, 0:1, 0:PW] = got[:, PW:]
+        for k in range(NB):
+            out[NB * i + k, 0:1, 0:PW] = got[:, k * PW : (k + 1) * PW]
         if first:
             w_at = jnp.sum(jnp.where(one_hot(s, SP), weight_at, 0.0), axis=0, keepdims=True)
             f_at = jnp.sum(jnp.where(one_hot(d, DP), flux_col, 0.0), axis=0, keepdims=True)
             den = w_at * f_at
-            out[2 * i, 0:1, PW : 2 * PW] = den[:, :PW]
-            out[2 * i + 1, 0:1, PW : 2 * PW] = den[:, PW:]
+            for k in range(NB):
+                out[NB * i + k, 0:1, PW : 2 * PW] = den[:, k * PW : (k + 1) * PW]
         return carry
 
-    lax.fori_loop(0, CH // 2, pick, 0)
+    lax.fori_loop(0, CH // NB, pick, 0)
 
 
 def params():
@@ -177,6 +178,7 @@
 
 VM = pl.BlockSpec(memory_space=pltpu.VMEM)
 SM = pl.BlockSpec(memory_space=pltpu.SMEM)
+HB = pl.BlockSpec(memory_space=pltpu.HBM)
 
 
 def call(kernel, name, out_shape, in_specs, scratch=()):
@@ -195,62 +197,98 @@
 
 
 WORK = [
-    pltpu.VMEM((DP, 3 * SP), F32),
+    pltpu.VMEM((DP, 3 * SP + GP), F32),
     pltpu.VMEM((DP, LB), F32),
     pltpu.VMEM((DP, LB), F32),
 ]
 
 
-def first_solver(ids, freq, real, imag, weight, coords, pairs, directions, flux, start, points):
+def first_solver(
+    ids, freq, real, imag, weight, coords, pairs, directions, flux, start, points, eigen, basis
+):
     def kernel(
-        ids, freq, real, imag, weight, coords, pairs, directions, flux, start, points,
-        out, own, vis, uvw, ants, cols, stations, dirs, acc, re_s, im_s, rows, tall,
+        ids, freq, real_h, imag_h, weight_h, coords_h, pairs_h, directions_h, flux_h, start_h,
+        points_h, eigen_h, basis_h,
+        out, own, eigen_out, basis_out, vis, base, uvw, ants, cols, stations, dirs,
+        acc, re_s, im_s, rows, tall, real, imag, weight, coords, pairs, directions, flux, start,
+        points, sems,
     ):
+        copies = [
+            pltpu.make_async_copy(source, target, sems.at[i])
+            for i, (source, target) in enumerate(
+                (
+                    (points_h, points), (start_h, start), (directions_h, directions),
+                    (flux_h, flux), (coords_h, coords), (pairs_h, pairs), (real_h, real),
+                    (imag_h, imag), (weight_h, weight), (eigen_h, eigen_out),
+                    (basis_h, basis_out),
+                )
+            )
+        ]
+        for copy in copies:
+            copy.start()
         vis[...] = jnp.zeros_like(vis)
+        uvw[...] = jnp.zeros_like(uvw)
+        base[...] = jnp.zeros_like(base)
+        ants[...] = jnp.full(ants.shape, -1, jnp.int32)
+        rows[...] = jnp.zeros_like(rows)
+        tall[...] = jnp.zeros_like(tall)
+        stations[...] = jnp.full(stations.shape, -1, jnp.int32)
+        dirs[...] = jnp.full(dirs.shape, -1, jnp.int32)
+        for copy in copies[:-2]:
+            copy.wait()
         vis[0:1, 0:B] = real[0]
         vis[1:2, 0:B] = imag[0]
         vis[2:3, 0:B] = weight[0]
-        uvw[...] = jnp.zeros_like(uvw)
-        uvw[:, 0:B] = coords[0] * freq[...]
-        ants[...] = jnp.full(ants.shape, -1, jnp.int32)
         ants[:, 0:B] = pairs[...]
-        rows[...] = jnp.zeros_like(rows)
-        rows[0:3, 0:D] = directions[...]
-        rows[3:4, 0:D] = flux[...]
-        for c in range(4):
-            cols[c] = jnp.broadcast_to(rows[c : c + 1, :], (128, 256)).T[:DP, :]
-        tall[...] = jnp.zeros_like(tall)
-        tall[0:S, 0:D] = start[0]
-        parts = stacked(tall[...].T[:DP, :SP])
+        rows[0:1, 0:D] = flux[...]
+        cols[...] = jnp.broadcast_to(rows[0:1, :], (128, 256)).T[:DP, :]
+        unit = freq[...] * freq[...] * (TWO_PI / TEC_PHASE)
+        for c in range(3):
+            place_parts = split3(directions[c : c + 1, :])
+            coord_parts = split3(coords[c] * unit)
+            for j, (m, n) in enumerate(PRODUCTS):
+                k = len(PRODUCTS) * c + j
+                tall[SP + k : SP + k + 1, 0:D] = place_parts[m]
+                uvw[k : k + 1, 0:B] = coord_parts[n]
+        for k in range(S):
+            tall[k : k + 1, 0:D] = start[k]
+        turned = tall[...].T[:DP, :]
+        base[:, 3 * SP : 3 * SP + GP] = turned[:, SP : SP + GP]
         q = points[...]
         s = jnp.floor((q.astype(F32) + 0.5) * (1.0 / D)).astype(jnp.int32)
         d = q - s * D
-        blank = jnp.full((1, PW), -1, jnp.int32)
         for c in range(CH):
-            stations[c] = blank
             stations[c, 0:1, 0:PB] = s[:, c * PB : (c + 1) * PB]
-            dirs[c] = blank
             dirs[c, 0:1, 0:PB] = d[:, c * PB : (c + 1) * PB]
         solver(
-            freq, None, vis, uvw, ants, cols, stations, dirs, out, (acc, re_s, im_s),
-            own=(parts, ids[0], own),
+            freq, None, vis, None, uvw, ants, cols, stations, dirs, out, (acc, re_s, im_s),
+            own=(stacked(turned[:, :SP]), turned[:, SP : SP + GP].astype(BF16), ids[0], own),
         )
+        for copy in copies[-2:]:
+            copy.wait()
 
     i32 = lambda *shape: jax.ShapeDtypeStruct(shape, jnp.int32)
+    small = [
+        pltpu.VMEM(x.shape, x.dtype)
+        for x in (real, imag, weight, coords, pairs, directions, flux, start, points)
+    ]
     return call(
         kernel,
         "first_solver",
         [
-            (CH, 1, 2 * PW), (1, PW), (3, BP), (3, BP), i32(2, BP), (4, DP, 128),
-            i32(CH, 1, PW), i32(CH, 1, PW),
+            (CH, 1, 2 * PW), (1, PW), (1, K), (PB, K), (3, BP), (DP, 3 * SP + GP), (GP, BP),
+            i32(2, BP), (DP, 128), i32(CH, 1, PW), i32(CH, 1, PW),
         ],
-        [SM] + [VM] * 10,
-        WORK + [pltpu.VMEM((8, 256), F32), pltpu.VMEM((128, 256), F32)],
-    )(ids, freq, real, imag, weight, coords, pairs, directions, flux, start, points)
+        [SM, VM] + [HB] * 11,
+        WORK
+        + [pltpu.VMEM((8, 256), F32), pltpu.VMEM((128, 256), F32)]
+        + small
+        + [pltpu.SemaphoreType.DMA((11,))],
+    )(ids, freq, real, imag, weight, coords, pairs, directions, flux, start, points, eigen, basis)
 
 
 def next_solver(freq, tec, held, last):
-    def kernel(freq, tec, vis, uvw, ants, cols, stations, dirs, out, *refs):
+    def kernel(freq, tec, vis, base, uvw, ants, cols, stations, dirs, out, *refs):
         if last:
             real, imag, acc, re_s, im_s, left = refs
             kept = (left, real, imag)
@@ -258,14 +296,15 @@
             acc, re_s, im_s = refs
             kept = None
         solver(
-            freq, tec, vis, uvw, ants, cols, stations, dirs, out, (acc, re_s, im_s), kept=kept
+            freq, tec, vis, base, uvw, ants, cols, stations, dirs, out, (acc, re_s, im_s),
+            kept=kept,
         )
 
     return call(
         kernel,
         "last_solver" if last else "next_solver",
         [(CH, 1, PW)] + ([(1, 1, B), (1, 1, B)] if last else []),
-        [VM] * 8,
+        [VM] * 9,
         WORK + ([pltpu.VMEM((2, BP), F32)] if last else []),
     )(freq, tec, *held)
 
@@ -279,11 +318,12 @@
             acc[...] += dot_nt(by_station, by_direction)
             return carry
 
-        lax.fori_loop(0, CH // 2, place, 0)
+        lax.fori_loop(0, CH // NB, place, 0)
         whole = (acc[0:SP, :] + acc[SP : 2 * SP, :]) + acc[2 * SP : 3 * SP, :]
-        out[0] = whole[:S, :D]
-
-    return call(kernel, "final_place", [(1, S, D)], [VM] * 3, [pltpu.VMEM((3 * SP, DP), F32)])(
+        for k in range(S):
+            out[k] = whole[k : k + 1, :D]
+
+    return call(kernel, "final_place", [(S, 1, D)], [VM] * 3, [pltpu.VMEM((3 * SP, DP), F32)])(
         vals, stations, dirs
     )[0]
 
@@ -383,13 +423,14 @@
     slots = lax.axis_size("slot")
     ids = jnp.stack([lax.axis_index("chan"), lax.axis_index("slot")]).astype(jnp.int32)
     freq = channel_frequency.reshape(1, 1)
-    weight = eigen_weight[None, :]
     near_pairs = [(i, i ^ 1) for i in range(slots) if i ^ 1 < slots]
     far_pairs = [(i, i - 1 if i % 2 == 0 else i + 1) for i in range(1, slots - 1)]
     far_pairs = [(i, j) for i, j in far_pairs if 0 <= j < slots]
-    sent, own, *held = first_solver(
-        ids, freq, measured_real, measured_imaginary, measured_weight, baseline_vectors,
-        antenna_pairs, directions, direction_flux, electron_content_start, pierce_station_direction,
+    sent, own, weight, basis, *held = first_solver(
+        ids, freq, measured_real, measured_imaginary, measured_weight,
+        jnp.transpose(baseline_vectors, (1, 0, 2)), antenna_pairs, directions, direction_flux,
+        jnp.transpose(electron_content_start, (1, 0, 2)), pierce_station_direction,
+        eigen_weight[None, :], eigen_basis,
     )
     denominator = None
     for iteration in range(ITERS):
@@ -398,10 +439,10 @@
         target, denominator = own_target(exchange(sent), own, denominator)
         far = lax.ppermute(target, "slot", far_pairs)
         near = lax.ppermute(target, "slot", near_pairs)
-        partial = basis_partial(ids, slots, target, near, far, weight, eigen_basis)
-        coefficients, own, spread = own_screen(exchange(partial), eigen_basis)
+        partial = basis_partial(ids, slots, target, near, far, weight, basis)
+        coefficients, own, spread = own_screen(exchange(partial), basis)
         gathered = exchange(spread)
-    tec_final = final_place(gathered, held[4], held[5])
+    tec_final = jnp.transpose(final_place(gathered, held[-2], held[-1]), (1, 0, 2))
     return tec_final, coefficients, left[0], left[1]
 
 

time: 275 us -> 249 us (0.905)
  Pallas kernels: 64.1 us -> 38.9 us
    pallas_call x3, Pallas kernels: 40.7 us -> 20 us  [next_solver(): call(kernel, 'last_solver' if last else 'next_solver', [(CH, 1, PW)] + ([...]
    pallas_call x2, Pallas kernels: 15.6 us -> 11.1 us  [the longest x1 8.66 us: first_solver(): call(kernel, 'first_solver', [(CH, 1, 2 * PW), (1, PW), (1, K), (PB, K),...]
    unnamed x25 -> x22, local copies, waits for them, and re-layouts: 9.79 us -> 9.08 us
where the time goes in v2:
time: 249 us; the launch traced here: 247 us
  blocking collectives  157 us (63%)
  Pallas kernels  38.9 us (16%)
  starting transfers between devices  24.7 us (10%)
  waiting for transfers between devices  16.6 us (7%)
  local copies, waits for them, and re-layouts  9.08 us (4%)
    all_to_all x12, blocking collectives, exchange(): lax.all_to_all(value, 'chan', split_axis=0, concat_axis=0, tiled=True)  157 us
    ppermute x4, starting transfers between devices, per_device(): far = lax.ppermute(target, 'slot', far_pairs)  24.1 us
    pallas_call x3, Pallas kernels, next_solver(): call(kernel, 'last_solver' if last else 'next_solver', [(CH, 1, PW)] + ([...  20 us
    ppermute x4, waiting for transfers between devices, per_device(): far = lax.ppermute(target, 'slot', far_pairs)  16.6 us
    unnamed x22, local copies, waits for them, and re-layouts  9.08 us
    pallas_call x1, Pallas kernels, first_solver(): call(kernel, 'first_solver', [(CH, 1, 2 * PW), (1, PW), (1, K), (PB, K),...  8.66 us
  transfers between devices with their start and end apart: 8, of which 4 were waited for; matrix products, arithmetic and copies ran while one was open for 0% of the time, Pallas kernels for 0%

profile of v2, /device:TPU:7, one launch (start us, length us, event | category | flops | bytes accessed | tf_op | source)
XLA Modules:
  0.0 247.5 jit_solution(10667119872644544932)
XLA Ops:
  1.4 1.9 copy-done
  10.4 8.7 %first_solver.1 = (f32[32,1,768]{2,1,0:T(1,128)S(1)}, f32[1,384]{1,0:T(1,128)S(1)}, f32[1,2048]{1,0:T(1,128)S(1)}, f32[375,2048]{1,0:T(8,128)S(1)}, f32[3,1792]{...) custom-call(s32[2]{0:T(128)S(1)} %pad_add_fusion.ids, ...), custom_call_target="tpu_custom_call" | custom-call | tf_op jit(solution)/shard_map/first_solver/pallas_call | solution.py:275
  19.1 17.4 %all_to_all.60.arrived = f32[32,1,768]{2,1,0:T(1,128)S(1)} all-to-all(f32[32,1,768]{2,1,0:T(1,128)S(1)} %get-tuple-element.28), channel_id=1, replica_groups=mesh['chan'=32,'slot'=8] {'chan'}, dimensions={0} | all-to-all | bytes 196608 | tf_op jit(solution)/shard_map/all_to_all | solution.py:406
  36.6 6.0 %collective-permute-start.1 = (f32[1,384]{1,0:T(1,128)S(1)}, f32[1,384]{1,0:T(1,128)S(1)}, u32[]{:S(2)}, u32[]{:S(2)}) collective-permute-start(f32[1,384]{1,0:T(1,128)S(1)} %get-tuple-element.30.target), channel_id=1, source_target_pairs={{1,2},{2,1},{3,4},{4,3},{5,6},{6,5},{9,10},{10,9},{11,12},{12,11},... | collective-permute-start | bytes 4616 | tf_op jit(solution)/shard_map/ppermute | solution.py:440
  42.7 4.2 %collective-permute-done.1.far = f32[1,384]{1,0:T(1,128)S(1)} collective-permute-done((f32[1,384]{1,0:T(1,128)S(1)}, f32[1,384]{1,0:T(1,128)S(1)}, u32[]{:S(2)}, u32[]{:S(2)}) %collective-permute-start.1) | collective-permute-done | bytes 1568 | tf_op jit(solution)/shard_map/ppermute | solution.py:440
  46.9 0.9 basis_partial.4
  47.9 15.7 %all_to_all.61.arrived = f32[32,1,2048]{2,1,0:T(1,128)S(1)} all-to-all(f32[32,1,2048]{2,1,0:T(1,128)S(1)} %basis_partial.4), channel_id=1, replica_groups=mesh['chan'=32,'slot'=8] {'chan'}, dimensions={0} | all-to-all | bytes 524288 | tf_op jit(solution)/shard_map/all_to_all | solution.py:406
  63.6 1.0 own_screen.4
  64.5 11.0 %all_to_all.62.tec = f32[32,1,384]{2,1,0:T(1,128)S(1)} all-to-all(f32[32,1,384]{2,1,0:T(1,128)S(1)} %get-tuple-element.33), channel_id=1, replica_groups=mesh['chan'=32,'slot'=8] {'chan'}, dimensions={0} | all-to-all | bytes 98304 | tf_op jit(solution)/shard_map/all_to_all | solution.py:406
  75.6 6.6 %next_solver.2 = f32[32,1,384]{2,1,0:T(1,128)S(1)} custom-call(f32[1,1]{1,0:T(1,128)} %bitcast.8.freq, f32[32,1,384]{2,1,0:T(1,128)S(1)} %all_to_all.62.tec, f32[3,1792]{1,0:T(4,128)S(1)} %get-tuple-element.34.vis, f32[208,224]{1,0:T(8,128)S(1)} %get-tuple-element.35.base, f32[32,1792]{1,0:T(8,128)S(1)} %get-tuple-element.36.uvw, ...), custom_call_target="tpu_custom_call" | custom-call | tf_op jit(solution)/shard_map/next_solver/pallas_call | solution.py:303
  82.2 10.9 %all_to_all.63.arrived = f32[32,1,384]{2,1,0:T(1,128)S(1)} all-to-all(f32[32,1,384]{2,1,0:T(1,128)S(1)} %next_solver.2), channel_id=1, replica_groups=mesh['chan'=32,'slot'=8] {'chan'}, dimensions={0} | all-to-all | bytes 98304 | tf_op jit(solution)/shard_map/all_to_all | solution.py:406
  93.2 6.0 %collective-permute-start.3 = (f32[1,384]{1,0:T(1,128)S(1)}, f32[1,384]{1,0:T(1,128)S(1)}, u32[]{:S(2)}, u32[]{:S(2)}) collective-permute-start(f32[1,384]{1,0:T(1,128)S(1)} %own_target.3.target), channel_id=1, source_target_pairs={{1,2},{2,1},{3,4},{4,3},{5,6},{6,5},{9,10},{10,9},{11,12},{12,11},... | collective-permute-start | bytes 4616 | tf_op jit(solution)/shard_map/ppermute | solution.py:440
  99.3 4.2 %collective-permute-done.3.far = f32[1,384]{1,0:T(1,128)S(1)} collective-permute-done((f32[1,384]{1,0:T(1,128)S(1)}, f32[1,384]{1,0:T(1,128)S(1)}, u32[]{:S(2)}, u32[]{:S(2)}) %collective-permute-start.3) | collective-permute-done | bytes 1568 | tf_op jit(solution)/shard_map/ppermute | solution.py:440
  104.4 15.6 %all_to_all.64.arrived = f32[32,1,2048]{2,1,0:T(1,128)S(1)} all-to-all(f32[32,1,2048]{2,1,0:T(1,128)S(1)} %basis_partial.5), channel_id=1, replica_groups=mesh['chan'=32,'slot'=8] {'chan'}, dimensions={0} | all-to-all | bytes 524288 | tf_op jit(solution)/shard_map/all_to_all | solution.py:406
  120.1 1.0 own_screen.5
  121.0 11.0 %all_to_all.65.tec = f32[32,1,384]{2,1,0:T(1,128)S(1)} all-to-all(f32[32,1,384]{2,1,0:T(1,128)S(1)} %get-tuple-element.43), channel_id=1, replica_groups=mesh['chan'=32,'slot'=8] {'chan'}, dimensions={0} | all-to-all | bytes 98304 | tf_op jit(solution)/shard_map/all_to_all | solution.py:406
  132.0 6.6 %next_solver.3 = f32[32,1,384]{2,1,0:T(1,128)S(1)} custom-call(f32[1,1]{1,0:T(1,128)} %bitcast.9.freq, f32[32,1,384]{2,1,0:T(1,128)S(1)} %all_to_all.65.tec, f32[3,1792]{1,0:T(4,128)S(1)} %get-tuple-element.34.vis, f32[208,224]{1,0:T(8,128)S(1)} %get-tuple-element.35.base, f32[32,1792]{1,0:T(8,128)S(1)} %get-tuple-element.36.uvw, ...), custom_call_target="tpu_custom_call" | custom-call | tf_op jit(solution)/shard_map/next_solver/pallas_call | solution.py:303
  138.7 10.9 %all_to_all.66.arrived = f32[32,1,384]{2,1,0:T(1,128)S(1)} all-to-all(f32[32,1,384]{2,1,0:T(1,128)S(1)} %next_solver.3), channel_id=1, replica_groups=mesh['chan'=32,'slot'=8] {'chan'}, dimensions={0} | all-to-all | bytes 98304 | tf_op jit(solution)/shard_map/all_to_all | solution.py:406
  149.6 6.0 %collective-permute-start.5 = (f32[1,384]{1,0:T(1,128)S(1)}, f32[1,384]{1,0:T(1,128)S(1)}, u32[]{:S(2)}, u32[]{:S(2)}) collective-permute-start(f32[1,384]{1,0:T(1,128)S(1)} %own_target.4.target), channel_id=1, source_target_pairs={{1,2},{2,1},{3,4},{4,3},{5,6},{6,5},{9,10},{10,9},{11,12},{12,11},... | collective-permute-start | bytes 4616 | tf_op jit(solution)/shard_map/ppermute | solution.py:440
  156.0 4.0 %collective-permute-done.5.far = f32[1,384]{1,0:T(1,128)S(1)} collective-permute-done((f32[1,384]{1,0:T(1,128)S(1)}, f32[1,384]{1,0:T(1,128)S(1)}, u32[]{:S(2)}, u32[]{:S(2)}) %collective-permute-start.5) | collective-permute-done | bytes 1568 | tf_op jit(solution)/shard_map/ppermute | solution.py:440
  159.9 0.9 basis_partial.6
  160.9 15.6 %all_to_all.67.arrived = f32[32,1,2048]{2,1,0:T(1,128)S(1)} all-to-all(f32[32,1,2048]{2,1,0:T(1,128)S(1)} %basis_partial.6), channel_id=1, replica_groups=mesh['chan'=32,'slot'=8] {'chan'}, dimensions={0} | all-to-all | bytes 524288 | tf_op jit(solution)/shard_map/all_to_all | solution.py:406
  176.5 1.0 own_screen.6
  177.5 11.0 %all_to_all.68.tec = f32[32,1,384]{2,1,0:T(1,128)S(1)} all-to-all(f32[32,1,384]{2,1,0:T(1,128)S(1)} %get-tuple-element.45), channel_id=1, replica_groups=mesh['chan'=32,'slot'=8] {'chan'}, dimensions={0} | all-to-all | bytes 98304 | tf_op jit(solution)/shard_map/all_to_all | solution.py:406
  188.5 6.7 %last_solver.1 = (f32[32,1,384]{2,1,0:T(1,128)S(1)}, f32[1,1,1770]{2,1,0:T(1,128)}, f32[1,1,1770]{2,1,0:T(1,128)}) custom-call(f32[1,1]{1,0:T(1,128)} %bitcast.10.freq, f32[32,1,384]{2,1,0:T(1,128)S(1)} %all_to_all.68.tec, f32[3,1792]{1,0:T(4,128)S(1)} %get-tuple-element.34.vis, f32[208,224]{1,0:T(8,128)S(1)} %get-tuple-element.35.base, ...), custom_call_target="tpu_custom_call" | custom-call | tf_op jit(solution)/shard_map/last_solver/pallas_call | solution.py:303
  195.2 10.9 %all_to_all.69.arrived = f32[32,1,384]{2,1,0:T(1,128)S(1)} all-to-all(f32[32,1,384]{2,1,0:T(1,128)S(1)} %get-tuple-element.46), channel_id=1, replica_groups=mesh['chan'=32,'slot'=8] {'chan'}, dimensions={0} | all-to-all | bytes 98304 | tf_op jit(solution)/shard_map/all_to_all | solution.py:406
  206.1 6.0 %collective-permute-start.7 = (f32[1,384]{1,0:T(1,128)S(1)}, f32[1,384]{1,0:T(1,128)S(1)}, u32[]{:S(2)}, u32[]{:S(2)}) collective-permute-start(f32[1,384]{1,0:T(1,128)S(1)} %own_target.5.target), channel_id=1, source_target_pairs={{1,2},{2,1},{3,4},{4,3},{5,6},{6,5},{9,10},{10,9},{11,12},{12,11},... | collective-permute-start | bytes 4616 | tf_op jit(solution)/shard_map/ppermute | solution.py:440
  212.3 4.2 %collective-permute-done.7.far = f32[1,384]{1,0:T(1,128)S(1)} collective-permute-done((f32[1,384]{1,0:T(1,128)S(1)}, f32[1,384]{1,0:T(1,128)S(1)}, u32[]{:S(2)}, u32[]{:S(2)}) %collective-permute-start.7) | collective-permute-done | bytes 1568 | tf_op jit(solution)/shard_map/ppermute | solution.py:440
  217.4 15.6 %all_to_all.70.arrived = f32[32,1,2048]{2,1,0:T(1,128)S(1)} all-to-all(f32[32,1,2048]{2,1,0:T(1,128)S(1)} %basis_partial.7), channel_id=1, replica_groups=mesh['chan'=32,'slot'=8] {'chan'}, dimensions={0} | all-to-all | bytes 524288 | tf_op jit(solution)/shard_map/all_to_all | solution.py:406
  233.0 1.0 own_screen.7
  234.0 11.0 %all_to_all.71.vals = f32[32,1,384]{2,1,0:T(1,128)S(1)} all-to-all(f32[32,1,384]{2,1,0:T(1,128)S(1)} %get-tuple-element.48), channel_id=1, replica_groups=mesh['chan'=32,'slot'=8] {'chan'}, dimensions={0} | all-to-all | bytes 98304 | tf_op jit(solution)/shard_map/all_to_all | solution.py:406
  245.0 2.4 final_place.1
  (36 shorter events, 9.9 us)
Async XLA Ops:
  1.4 1.9 copy-start
  3.2 0.8 copy-start.1
  4.1 0.8 copy-start.2
  4.9 0.7 copy-start.3
  5.6 0.7 copy-start.4
  6.3 0.7 copy-start.5
  7.0 0.7 copy-start.6
  7.7 0.7 copy-start.7
  8.4 0.7 copy-start.8
  9.1 0.7 copy-start.9
  9.8 0.7 copy-start.10
  36.6 10.3 %collective-permute-start.1 = (f32[1,384]{1,0:T(1,128)S(1)}, f32[1,384]{1,0:T(1,128)S(1)}, u32[]{:S(2)}, u32[]{:S(2)}) collective-permute-start(f32[1,384]{1,0:T(1,128)S(1)} %get-tuple-element.30.target), channel_id=1, source_target_pairs={{1,2},{2,1},{3,4},{4,3},{5,6},{6,5},{9,10},{10,9},{11,12},{12,11},... | collective-permute-start | bytes 4616 | tf_op jit(solution)/shard_map/ppermute | solution.py:440
  42.6 4.3 %collective-permute-start = (f32[1,384]{1,0:T(1,128)S(1)}, f32[1,384]{1,0:T(1,128)S(1)}, u32[]{:S(2)}, u32[]{:S(2)}) collective-permute-start(f32[1,384]{1,0:T(1,128)S(1)} %get-tuple-element.30.target), channel_id=1, source_target_pairs={{0,1},{1,0},{2,3},{3,2},{4,5},{5,4},{6,7},{7,6},{8,9},{9,8},{10,11... | collective-permute-start | bytes 4616 | tf_op jit(solution)/shard_map/ppermute | solution.py:441
  93.2 10.3 %collective-permute-start.3 = (f32[1,384]{1,0:T(1,128)S(1)}, f32[1,384]{1,0:T(1,128)S(1)}, u32[]{:S(2)}, u32[]{:S(2)}) collective-permute-start(f32[1,384]{1,0:T(1,128)S(1)} %own_target.3.target), channel_id=1, source_target_pairs={{1,2},{2,1},{3,4},{4,3},{5,6},{6,5},{9,10},{10,9},{11,12},{12,11},... | collective-permute-start | bytes 4616 | tf_op jit(solution)/shard_map/ppermute | solution.py:440
  99.2 4.3 %collective-permute-start.2 = (f32[1,384]{1,0:T(1,128)S(1)}, f32[1,384]{1,0:T(1,128)S(1)}, u32[]{:S(2)}, u32[]{:S(2)}) collective-permute-start(f32[1,384]{1,0:T(1,128)S(1)} %own_target.3.target), channel_id=1, source_target_pairs={{0,1},{1,0},{2,3},{3,2},{4,5},{5,4},{6,7},{7,6},{8,9},{9,8},{10,11... | collective-permute-start | bytes 4616 | tf_op jit(solution)/shard_map/ppermute | solution.py:441
  149.6 10.3 %collective-permute-start.5 = (f32[1,384]{1,0:T(1,128)S(1)}, f32[1,384]{1,0:T(1,128)S(1)}, u32[]{:S(2)}, u32[]{:S(2)}) collective-permute-start(f32[1,384]{1,0:T(1,128)S(1)} %own_target.4.target), channel_id=1, source_target_pairs={{1,2},{2,1},{3,4},{4,3},{5,6},{6,5},{9,10},{10,9},{11,12},{12,11},... | collective-permute-start | bytes 4616 | tf_op jit(solution)/shard_map/ppermute | solution.py:440
  155.6 4.3 %collective-permute-start.4 = (f32[1,384]{1,0:T(1,128)S(1)}, f32[1,384]{1,0:T(1,128)S(1)}, u32[]{:S(2)}, u32[]{:S(2)}) collective-permute-start(f32[1,384]{1,0:T(1,128)S(1)} %own_target.4.target), channel_id=1, source_target_pairs={{0,1},{1,0},{2,3},{3,2},{4,5},{5,4},{6,7},{7,6},{8,9},{9,8},{10,11... | collective-permute-start | bytes 4616 | tf_op jit(solution)/shard_map/ppermute | solution.py:441
  206.1 10.3 %collective-permute-start.7 = (f32[1,384]{1,0:T(1,128)S(1)}, f32[1,384]{1,0:T(1,128)S(1)}, u32[]{:S(2)}, u32[]{:S(2)}) collective-permute-start(f32[1,384]{1,0:T(1,128)S(1)} %own_target.5.target), channel_id=1, source_target_pairs={{1,2},{2,1},{3,4},{4,3},{5,6},{6,5},{9,10},{10,9},{11,12},{12,11},... | collective-permute-start | bytes 4616 | tf_op jit(solution)/shard_map/ppermute | solution.py:440
  212.2 4.3 %collective-permute-start.6 = (f32[1,384]{1,0:T(1,128)S(1)}, f32[1,384]{1,0:T(1,128)S(1)}, u32[]{:S(2)}, u32[]{:S(2)}) collective-permute-start(f32[1,384]{1,0:T(1,128)S(1)} %own_target.5.target), channel_id=1, source_target_pairs={{0,1},{1,0},{2,3},{3,2},{4,5},{5,4},{6,7},{7,6},{8,9},{9,8},{10,11... | collective-permute-start | bytes 4616 | tf_op jit(solution)/shard_map/ppermute | solution.py:441

commit v3 on v2

--- a/solution.py
+++ b/solution.py
@@ -426,12 +426,16 @@
     near_pairs = [(i, i ^ 1) for i in range(slots) if i ^ 1 < slots]
     far_pairs = [(i, i - 1 if i % 2 == 0 else i + 1) for i in range(1, slots - 1)]
     far_pairs = [(i, j) for i, j in far_pairs if 0 <= j < slots]
-    sent, own, weight, basis, *held = first_solver(
-        ids, freq, measured_real, measured_imaginary, measured_weight,
-        jnp.transpose(baseline_vectors, (1, 0, 2)), antenna_pairs, directions, direction_flux,
-        jnp.transpose(electron_content_start, (1, 0, 2)), pierce_station_direction,
-        eigen_weight[None, :], eigen_basis,
-    )
+    arguments = [
+        pltpu.with_memory_space_constraint(x, pltpu.HBM)
+        for x in (
+            measured_real, measured_imaginary, measured_weight,
+            jnp.transpose(baseline_vectors, (1, 0, 2)), antenna_pairs, directions,
+            direction_flux, jnp.transpose(electron_content_start, (1, 0, 2)),
+            pierce_station_direction, eigen_weight[None, :], eigen_basis,
+        )
+    ]
+    sent, own, weight, basis, *held = first_solver(ids, freq, *arguments)
     denominator = None
     for iteration in range(ITERS):
         if iteration > 0:

time: 249 us -> 239 us (0.960)
  local copies, waits for them, and re-layouts: 9.08 us -> 0 us
    unnamed x22 -> x0, local copies, waits for them, and re-layouts: 9.08 us -> none
where the time goes in v3:
time: 239 us
  blocking collectives  157 us (66%)
  Pallas kernels  39 us (16%)
  starting transfers between devices  24.5 us (10%)
  waiting for transfers between devices  16.8 us (7%)
    all_to_all x12, blocking collectives, exchange(): lax.all_to_all(value, 'chan', split_axis=0, concat_axis=0, tiled=True)  157 us
    ppermute x4, starting transfers between devices, per_device(): far = lax.ppermute(target, 'slot', far_pairs)  24.1 us
    pallas_call x3, Pallas kernels, next_solver(): call(kernel, 'last_solver' if last else 'next_solver', [(CH, 1, PW)] + ([...  20 us
    ppermute x4, waiting for transfers between devices, per_device(): far = lax.ppermute(target, 'slot', far_pairs)  16.8 us
    pallas_call x1, Pallas kernels, first_solver(): call(kernel, 'first_solver', [(CH, 1, 2 * PW), (1, PW), (1, K), (PB, K),...  8.77 us
  transfers between devices with their start and end apart: 8, of which 4 were waited for; matrix products, arithmetic and copies ran while one was open for 0% of the time, Pallas kernels for 0%

profile of v3, /device:TPU:7, one launch (start us, length us, event | category | flops | bytes accessed | tf_op | source)
XLA Modules:
  0.0 238.7 jit_solution(10684410824573586471)
XLA Ops:
  1.4 8.8 %first_solver.1 = (f32[32,1,768]{2,1,0:T(1,128)S(1)}, f32[1,384]{1,0:T(1,128)S(1)}, f32[1,2048]{1,0:T(1,128)S(1)}, f32[375,2048]{1,0:T(8,128)S(1)}, f32[3,1792]{...) custom-call(s32[2]{0:T(128)S(1)} %pad_add_fusion.ids, ...), custom_call_target="tpu_custom_call" | custom-call | tf_op jit(solution)/shard_map/first_solver/pallas_call | solution.py:275
  10.1 17.4 %all_to_all.60.arrived = f32[32,1,768]{2,1,0:T(1,128)S(1)} all-to-all(f32[32,1,768]{2,1,0:T(1,128)S(1)} %get-tuple-element.28), channel_id=1, replica_groups=mesh['chan'=32,'slot'=8] {'chan'}, dimensions={0} | all-to-all | bytes 196608 | tf_op jit(solution)/shard_map/all_to_all | solution.py:406
  27.6 6.0 %collective-permute-start.1 = (f32[1,384]{1,0:T(1,128)S(1)}, f32[1,384]{1,0:T(1,128)S(1)}, u32[]{:S(2)}, u32[]{:S(2)}) collective-permute-start(f32[1,384]{1,0:T(1,128)S(1)} %get-tuple-element.30.target), channel_id=1, source_target_pairs={{1,2},{2,1},{3,4},{4,3},{5,6},{6,5},{9,10},{10,9},{11,12},{12,11},... | collective-permute-start | bytes 4616 | tf_op jit(solution)/shard_map/ppermute | solution.py:444
  33.8 4.2 %collective-permute-done.1.far = f32[1,384]{1,0:T(1,128)S(1)} collective-permute-done((f32[1,384]{1,0:T(1,128)S(1)}, f32[1,384]{1,0:T(1,128)S(1)}, u32[]{:S(2)}, u32[]{:S(2)}) %collective-permute-start.1) | collective-permute-done | bytes 1568 | tf_op jit(solution)/shard_map/ppermute | solution.py:444
  38.0 0.9 basis_partial.4
  38.9 15.7 %all_to_all.61.arrived = f32[32,1,2048]{2,1,0:T(1,128)S(1)} all-to-all(f32[32,1,2048]{2,1,0:T(1,128)S(1)} %basis_partial.4), channel_id=1, replica_groups=mesh['chan'=32,'slot'=8] {'chan'}, dimensions={0} | all-to-all | bytes 524288 | tf_op jit(solution)/shard_map/all_to_all | solution.py:406
  54.6 1.0 own_screen.4
  55.6 11.0 %all_to_all.62.tec = f32[32,1,384]{2,1,0:T(1,128)S(1)} all-to-all(f32[32,1,384]{2,1,0:T(1,128)S(1)} %get-tuple-element.33), channel_id=1, replica_groups=mesh['chan'=32,'slot'=8] {'chan'}, dimensions={0} | all-to-all | bytes 98304 | tf_op jit(solution)/shard_map/all_to_all | solution.py:406
  66.6 6.6 %next_solver.2 = f32[32,1,384]{2,1,0:T(1,128)S(1)} custom-call(f32[1,1]{1,0:T(1,128)} %bitcast.8.freq, f32[32,1,384]{2,1,0:T(1,128)S(1)} %all_to_all.62.tec, f32[3,1792]{1,0:T(4,128)S(1)} %get-tuple-element.34.vis, f32[208,224]{1,0:T(8,128)S(1)} %get-tuple-element.35.base, f32[32,1792]{1,0:T(8,128)S(1)} %get-tuple-element.36.uvw, ...), custom_call_target="tpu_custom_call" | custom-call | tf_op jit(solution)/shard_map/next_solver/pallas_call | solution.py:303
  73.2 11.1 %all_to_all.63.arrived = f32[32,1,384]{2,1,0:T(1,128)S(1)} all-to-all(f32[32,1,384]{2,1,0:T(1,128)S(1)} %next_solver.2), channel_id=1, replica_groups=mesh['chan'=32,'slot'=8] {'chan'}, dimensions={0} | all-to-all | bytes 98304 | tf_op jit(solution)/shard_map/all_to_all | solution.py:406
  84.4 6.0 %collective-permute-start.3 = (f32[1,384]{1,0:T(1,128)S(1)}, f32[1,384]{1,0:T(1,128)S(1)}, u32[]{:S(2)}, u32[]{:S(2)}) collective-permute-start(f32[1,384]{1,0:T(1,128)S(1)} %own_target.3.target), channel_id=1, source_target_pairs={{1,2},{2,1},{3,4},{4,3},{5,6},{6,5},{9,10},{10,9},{11,12},{12,11},... | collective-permute-start | bytes 4616 | tf_op jit(solution)/shard_map/ppermute | solution.py:444
  90.5 4.2 %collective-permute-done.3.far = f32[1,384]{1,0:T(1,128)S(1)} collective-permute-done((f32[1,384]{1,0:T(1,128)S(1)}, f32[1,384]{1,0:T(1,128)S(1)}, u32[]{:S(2)}, u32[]{:S(2)}) %collective-permute-start.3) | collective-permute-done | bytes 1568 | tf_op jit(solution)/shard_map/ppermute | solution.py:444
  94.7 0.9 basis_partial.5
  95.6 15.6 %all_to_all.64.arrived = f32[32,1,2048]{2,1,0:T(1,128)S(1)} all-to-all(f32[32,1,2048]{2,1,0:T(1,128)S(1)} %basis_partial.5), channel_id=1, replica_groups=mesh['chan'=32,'slot'=8] {'chan'}, dimensions={0} | all-to-all | bytes 524288 | tf_op jit(solution)/shard_map/all_to_all | solution.py:406
  111.3 1.0 own_screen.5
  112.2 11.0 %all_to_all.65.tec = f32[32,1,384]{2,1,0:T(1,128)S(1)} all-to-all(f32[32,1,384]{2,1,0:T(1,128)S(1)} %get-tuple-element.43), channel_id=1, replica_groups=mesh['chan'=32,'slot'=8] {'chan'}, dimensions={0} | all-to-all | bytes 98304 | tf_op jit(solution)/shard_map/all_to_all | solution.py:406
  123.2 6.6 %next_solver.3 = f32[32,1,384]{2,1,0:T(1,128)S(1)} custom-call(f32[1,1]{1,0:T(1,128)} %bitcast.9.freq, f32[32,1,384]{2,1,0:T(1,128)S(1)} %all_to_all.65.tec, f32[3,1792]{1,0:T(4,128)S(1)} %get-tuple-element.34.vis, f32[208,224]{1,0:T(8,128)S(1)} %get-tuple-element.35.base, f32[32,1792]{1,0:T(8,128)S(1)} %get-tuple-element.36.uvw, ...), custom_call_target="tpu_custom_call" | custom-call | tf_op jit(solution)/shard_map/next_solver/pallas_call | solution.py:303
  129.9 10.9 %all_to_all.66.arrived = f32[32,1,384]{2,1,0:T(1,128)S(1)} all-to-all(f32[32,1,384]{2,1,0:T(1,128)S(1)} %next_solver.3), channel_id=1, replica_groups=mesh['chan'=32,'slot'=8] {'chan'}, dimensions={0} | all-to-all | bytes 98304 | tf_op jit(solution)/shard_map/all_to_all | solution.py:406
  140.8 6.0 %collective-permute-start.5 = (f32[1,384]{1,0:T(1,128)S(1)}, f32[1,384]{1,0:T(1,128)S(1)}, u32[]{:S(2)}, u32[]{:S(2)}) collective-permute-start(f32[1,384]{1,0:T(1,128)S(1)} %own_target.4.target), channel_id=1, source_target_pairs={{1,2},{2,1},{3,4},{4,3},{5,6},{6,5},{9,10},{10,9},{11,12},{12,11},... | collective-permute-start | bytes 4616 | tf_op jit(solution)/shard_map/ppermute | solution.py:444
  146.9 4.2 %collective-permute-done.5.far = f32[1,384]{1,0:T(1,128)S(1)} collective-permute-done((f32[1,384]{1,0:T(1,128)S(1)}, f32[1,384]{1,0:T(1,128)S(1)}, u32[]{:S(2)}, u32[]{:S(2)}) %collective-permute-start.5) | collective-permute-done | bytes 1568 | tf_op jit(solution)/shard_map/ppermute | solution.py:444
  152.1 15.6 %all_to_all.67.arrived = f32[32,1,2048]{2,1,0:T(1,128)S(1)} all-to-all(f32[32,1,2048]{2,1,0:T(1,128)S(1)} %basis_partial.6), channel_id=1, replica_groups=mesh['chan'=32,'slot'=8] {'chan'}, dimensions={0} | all-to-all | bytes 524288 | tf_op jit(solution)/shard_map/all_to_all | solution.py:406
  167.7 1.0 own_screen.6
  168.7 11.0 %all_to_all.68.tec = f32[32,1,384]{2,1,0:T(1,128)S(1)} all-to-all(f32[32,1,384]{2,1,0:T(1,128)S(1)} %get-tuple-element.45), channel_id=1, replica_groups=mesh['chan'=32,'slot'=8] {'chan'}, dimensions={0} | all-to-all | bytes 98304 | tf_op jit(solution)/shard_map/all_to_all | solution.py:406
  179.7 6.7 %last_solver.1 = (f32[32,1,384]{2,1,0:T(1,128)S(1)}, f32[1,1,1770]{2,1,0:T(1,128)}, f32[1,1,1770]{2,1,0:T(1,128)}) custom-call(f32[1,1]{1,0:T(1,128)} %bitcast.10.freq, f32[32,1,384]{2,1,0:T(1,128)S(1)} %all_to_all.68.tec, f32[3,1792]{1,0:T(4,128)S(1)} %get-tuple-element.34.vis, f32[208,224]{1,0:T(8,128)S(1)} %get-tuple-element.35.base, ...), custom_call_target="tpu_custom_call" | custom-call | tf_op jit(solution)/shard_map/last_solver/pallas_call | solution.py:303
  186.4 10.9 %all_to_all.69.arrived = f32[32,1,384]{2,1,0:T(1,128)S(1)} all-to-all(f32[32,1,384]{2,1,0:T(1,128)S(1)} %get-tuple-element.46), channel_id=1, replica_groups=mesh['chan'=32,'slot'=8] {'chan'}, dimensions={0} | all-to-all | bytes 98304 | tf_op jit(solution)/shard_map/all_to_all | solution.py:406
  197.3 6.0 %collective-permute-start.7 = (f32[1,384]{1,0:T(1,128)S(1)}, f32[1,384]{1,0:T(1,128)S(1)}, u32[]{:S(2)}, u32[]{:S(2)}) collective-permute-start(f32[1,384]{1,0:T(1,128)S(1)} %own_target.5.target), channel_id=1, source_target_pairs={{1,2},{2,1},{3,4},{4,3},{5,6},{6,5},{9,10},{10,9},{11,12},{12,11},... | collective-permute-start | bytes 4616 | tf_op jit(solution)/shard_map/ppermute | solution.py:444
  203.5 4.2 %collective-permute-done.7.far = f32[1,384]{1,0:T(1,128)S(1)} collective-permute-done((f32[1,384]{1,0:T(1,128)S(1)}, f32[1,384]{1,0:T(1,128)S(1)}, u32[]{:S(2)}, u32[]{:S(2)}) %collective-permute-start.7) | collective-permute-done | bytes 1568 | tf_op jit(solution)/shard_map/ppermute | solution.py:444
  207.7 0.9 basis_partial.7
  208.6 15.6 %all_to_all.70.arrived = f32[32,1,2048]{2,1,0:T(1,128)S(1)} all-to-all(f32[32,1,2048]{2,1,0:T(1,128)S(1)} %basis_partial.7), channel_id=1, replica_groups=mesh['chan'=32,'slot'=8] {'chan'}, dimensions={0} | all-to-all | bytes 524288 | tf_op jit(solution)/shard_map/all_to_all | solution.py:406
  224.2 1.0 own_screen.7
  225.3 11.0 %all_to_all.71.vals = f32[32,1,384]{2,1,0:T(1,128)S(1)} all-to-all(f32[32,1,384]{2,1,0:T(1,128)S(1)} %get-tuple-element.48), channel_id=1, replica_groups=mesh['chan'=32,'slot'=8] {'chan'}, dimensions={0} | all-to-all | bytes 98304 | tf_op jit(solution)/shard_map/all_to_all | solution.py:406
  236.2 2.5 %final_place.1 = f32[60,1,200]{2,1,0:T(1,128)} custom-call(f32[32,1,384]{2,1,0:T(1,128)S(1)} %all_to_all.71.vals, s32[32,1,384]{2,1,0:T(1,128)S(1)} %get-tuple-element.39.stations, s32[32,1,384]{2,1,0:T(1,128)S(1)} %get-tuple-element.40.dirs), custom_call_target="tpu_custom_call" | custom-call | tf_op jit(solution)/shard_map/final_place/pallas_call | solution.py:326
  (14 shorter events, 1.6 us)
Async XLA Ops:
  27.6 10.3 %collective-permute-start.1 = (f32[1,384]{1,0:T(1,128)S(1)}, f32[1,384]{1,0:T(1,128)S(1)}, u32[]{:S(2)}, u32[]{:S(2)}) collective-permute-start(f32[1,384]{1,0:T(1,128)S(1)} %get-tuple-element.30.target), channel_id=1, source_target_pairs={{1,2},{2,1},{3,4},{4,3},{5,6},{6,5},{9,10},{10,9},{11,12},{12,11},... | collective-permute-start | bytes 4616 | tf_op jit(solution)/shard_map/ppermute | solution.py:444
  33.7 4.3 %collective-permute-start = (f32[1,384]{1,0:T(1,128)S(1)}, f32[1,384]{1,0:T(1,128)S(1)}, u32[]{:S(2)}, u32[]{:S(2)}) collective-permute-start(f32[1,384]{1,0:T(1,128)S(1)} %get-tuple-element.30.target), channel_id=1, source_target_pairs={{0,1},{1,0},{2,3},{3,2},{4,5},{5,4},{6,7},{7,6},{8,9},{9,8},{10,11... | collective-permute-start | bytes 4616 | tf_op jit(solution)/shard_map/ppermute | solution.py:445
  84.4 10.3 %collective-permute-start.3 = (f32[1,384]{1,0:T(1,128)S(1)}, f32[1,384]{1,0:T(1,128)S(1)}, u32[]{:S(2)}, u32[]{:S(2)}) collective-permute-start(f32[1,384]{1,0:T(1,128)S(1)} %own_target.3.target), channel_id=1, source_target_pairs={{1,2},{2,1},{3,4},{4,3},{5,6},{6,5},{9,10},{10,9},{11,12},{12,11},... | collective-permute-start | bytes 4616 | tf_op jit(solution)/shard_map/ppermute | solution.py:444
  90.4 4.3 %collective-permute-start.2 = (f32[1,384]{1,0:T(1,128)S(1)}, f32[1,384]{1,0:T(1,128)S(1)}, u32[]{:S(2)}, u32[]{:S(2)}) collective-permute-start(f32[1,384]{1,0:T(1,128)S(1)} %own_target.3.target), channel_id=1, source_target_pairs={{0,1},{1,0},{2,3},{3,2},{4,5},{5,4},{6,7},{7,6},{8,9},{9,8},{10,11... | collective-permute-start | bytes 4616 | tf_op jit(solution)/shard_map/ppermute | solution.py:445
  140.8 10.3 %collective-permute-start.5 = (f32[1,384]{1,0:T(1,128)S(1)}, f32[1,384]{1,0:T(1,128)S(1)}, u32[]{:S(2)}, u32[]{:S(2)}) collective-permute-start(f32[1,384]{1,0:T(1,128)S(1)} %own_target.4.target), channel_id=1, source_target_pairs={{1,2},{2,1},{3,4},{4,3},{5,6},{6,5},{9,10},{10,9},{11,12},{12,11},... | collective-permute-start | bytes 4616 | tf_op jit(solution)/shard_map/ppermute | solution.py:444
  146.8 4.3 %collective-permute-start.4 = (f32[1,384]{1,0:T(1,128)S(1)}, f32[1,384]{1,0:T(1,128)S(1)}, u32[]{:S(2)}, u32[]{:S(2)}) collective-permute-start(f32[1,384]{1,0:T(1,128)S(1)} %own_target.4.target), channel_id=1, source_target_pairs={{0,1},{1,0},{2,3},{3,2},{4,5},{5,4},{6,7},{7,6},{8,9},{9,8},{10,11... | collective-permute-start | bytes 4616 | tf_op jit(solution)/shard_map/ppermute | solution.py:445
  197.3 10.3 %collective-permute-start.7 = (f32[1,384]{1,0:T(1,128)S(1)}, f32[1,384]{1,0:T(1,128)S(1)}, u32[]{:S(2)}, u32[]{:S(2)}) collective-permute-start(f32[1,384]{1,0:T(1,128)S(1)} %own_target.5.target), channel_id=1, source_target_pairs={{1,2},{2,1},{3,4},{4,3},{5,6},{6,5},{9,10},{10,9},{11,12},{12,11},... | collective-permute-start | bytes 4616 | tf_op jit(solution)/shard_map/ppermute | solution.py:444
  203.4 4.3 %collective-permute-start.6 = (f32[1,384]{1,0:T(1,128)S(1)}, f32[1,384]{1,0:T(1,128)S(1)}, u32[]{:S(2)}, u32[]{:S(2)}) collective-permute-start(f32[1,384]{1,0:T(1,128)S(1)} %own_target.5.target), channel_id=1, source_target_pairs={{0,1},{1,0},{2,3},{3,2},{4,5},{5,4},{6,7},{7,6},{8,9},{9,8},{10,11... | collective-permute-start | bytes 4616 | tf_op jit(solution)/shard_map/ppermute | solution.py:445

commit v4 on v3

--- a/solution.py
+++ b/solution.py
@@ -69,7 +69,11 @@
 def picked(parts, s, d):
     at = jnp.where(one_hot(s, SP), 1.0, 0.0).astype(BF16)
     rows = dot_nn(parts, jnp.concatenate([at, at, at], axis=0))
-    return jnp.sum(jnp.where(one_hot(d, DP), rows, 0.0), axis=0, keepdims=True)
+    ahead = d - lax.broadcasted_iota(jnp.int32, (8, d.shape[1]), 0)
+    chosen = jnp.zeros((8, d.shape[1]), F32)
+    for g in range(DP // 8):
+        chosen = jnp.where(ahead == 8 * g, rows[8 * g : 8 * g + 8, :], chosen)
+    return jnp.sum(chosen, axis=0, keepdims=True)
 
 
 def stacked(field):
@@ -82,7 +86,7 @@
     turn_scale = jnp.broadcast_to(tec_scale * (1.0 / TWO_PI), (8, 128))
     first = own is not None
     if first:
-        tec_parts, base_parts, mine, own_out = own
+        tec_parts, base_parts, flux_row, mine, own_out = own
         own_out[...] = picked(tec_parts, stations[mine], dirs[mine])
         parts = jnp.concatenate([tec_parts, base_parts], axis=1)
     else:
@@ -149,9 +153,9 @@
         kept[2][0] = kept[0][1:2, 0:B]
     numer_parts = stacked(numer * tec_scale)
     if first:
-        weight_at = jnp.sum(weight_sum, axis=1, keepdims=True) * (tec_scale * tec_scale)
-        flux_col = cols[:, 0:1]
-        flux_col = flux_col * flux_col
+        weight_tall = jnp.concatenate([weight_sum, jnp.zeros((128 - SP, 128), F32)], axis=0)
+        weight_row = jnp.sum(weight_tall.T, axis=0, keepdims=True) * (tec_scale * tec_scale)
+        factors = jnp.concatenate([weight_row, flux_row * flux_row], axis=1)
 
     def pick(i, carry):
         s, d = joined(stations, i), joined(dirs, i)
@@ -159,11 +163,8 @@
         for k in range(NB):
             out[NB * i + k, 0:1, 0:PW] = got[:, k * PW : (k + 1) * PW]
         if first:
-            w_at = jnp.sum(jnp.where(one_hot(s, SP), weight_at, 0.0), axis=0, keepdims=True)
-            f_at = jnp.sum(jnp.where(one_hot(d, DP), flux_col, 0.0), axis=0, keepdims=True)
-            den = w_at * f_at
             for k in range(NB):
-                out[NB * i + k, 0:1, PW : 2 * PW] = den[:, k * PW : (k + 1) * PW]
+                out[NB * i + k, 0:1, PW : 2 * PW] = factors
         return carry
 
     lax.fori_loop(0, CH // NB, pick, 0)
@@ -262,7 +263,8 @@
             dirs[c, 0:1, 0:PB] = d[:, c * PB : (c + 1) * PB]
         solver(
             freq, None, vis, None, uvw, ants, cols, stations, dirs, out, (acc, re_s, im_s),
-            own=(stacked(turned[:, :SP]), turned[:, SP : SP + GP].astype(BF16), ids[0], own),
+            own=(stacked(turned[:, :SP]), turned[:, SP : SP + GP].astype(BF16),
+                 rows[0:1, :], ids[0], own),
         )
         for copy in copies[-2:]:
             copy.wait()
@@ -328,24 +330,37 @@
     )[0]
 
 
+def own_target_first(ids, arrived, own, stations, dirs):
+    def kernel(ids, arrived, own, stations, dirs, out, den_out):
+        mine = ids[0]
+        factors = jnp.concatenate([arrived[c, 0:1, PW : 2 * PW] for c in range(CH)], axis=0)
+        total = jnp.sum(arrived[:, :, 0:PW], axis=0)
+
+        def at_points(field, numbers):
+            parts = jnp.concatenate([part.astype(BF16) for part in split3(field)], axis=0)
+            hot = jnp.where(one_hot(numbers, field.shape[1]), 1.0, 0.0).astype(BF16)
+            found = dot_nn(parts, hot)
+            return (found[0:CH] + found[CH : 2 * CH]) + found[2 * CH : 3 * CH]
+
+        weights = at_points(factors[:, 0:128], stations[mine])
+        fluxes = at_points(factors[:, 128:384], dirs[mine])
+        den = jnp.sum(weights * fluxes, axis=0, keepdims=True)
+        den_out[...] = den
+        lane = lax.broadcasted_iota(jnp.int32, (1, PW), 1)
+        out[...] = jnp.where(lane < PB, own[...] + total / den, 0.0)
+
+    return call(kernel, "own_target_first", [(1, PW), (1, PW)], [SM] + [VM] * 4)(
+        ids, arrived, own, stations, dirs
+    )
+
+
 def own_target(arrived, own, denominator):
-    first = denominator is None
-
-    def kernel(arrived, own, *refs):
+    def kernel(arrived, own, den, out):
         total = jnp.sum(arrived[...], axis=0)
-        if first:
-            out, den_out = refs
-            den = total[:, PW:]
-            den_out[...] = den
-        else:
-            den_ref, out = refs
-            den = den_ref[...]
         lane = lax.broadcasted_iota(jnp.int32, (1, PW), 1)
-        out[...] = jnp.where(lane < PB, own[...] + total[:, :PW] / den, 0.0)
-
-    if first:
-        return call(kernel, "own_target_first", [(1, PW), (1, PW)], [VM] * 2)(arrived, own)
-    return call(kernel, "own_target", [(1, PW)], [VM] * 3)(arrived, own, denominator)[0], denominator
+        out[...] = jnp.where(lane < PB, own[...] + total / den[...], 0.0)
+
+    return call(kernel, "own_target", [(1, PW)], [VM] * 3)(arrived, own, denominator)[0]
 
 
 GROUPS = [(r, min(8, PB - r)) for r in range(0, PB, 8)]
@@ -436,11 +451,13 @@
         )
     ]
     sent, own, weight, basis, *held = first_solver(ids, freq, *arguments)
-    denominator = None
     for iteration in range(ITERS):
         if iteration > 0:
             sent, *left = next_solver(freq, gathered, held, iteration == ITERS - 1)
-        target, denominator = own_target(exchange(sent), own, denominator)
+        if iteration == 0:
+            target, denominator = own_target_first(ids, exchange(sent), own, held[-2], held[-1])
+        else:
+            target = own_target(exchange(sent), own, denominator)
         far = lax.ppermute(target, "slot", far_pairs)
         near = lax.ppermute(target, "slot", near_pairs)
         partial = basis_partial(ids, slots, target, near, far, weight, basis)

time: 239 us -> 236 us (0.987)
  Pallas kernels: 39 us -> 35.7 us
    pallas_call x1, Pallas kernels: 8.77 us -> 6.16 us  [first_solver(): call(kernel, 'first_solver', [(CH, 1, 2 * PW), (1, PW), (1, K), (PB, K),...]
where the time goes in v4:
time: 236 us; the launch traced here: 235 us
  blocking collectives  157 us (67%)
  Pallas kernels  35.7 us (15%)
  starting transfers between devices  24.8 us (11%)
  waiting for transfers between devices  16.6 us (7%)
    all_to_all x12, blocking collectives, exchange(): lax.all_to_all(value, 'chan', split_axis=0, concat_axis=0, tiled=True)  157 us
    ppermute x4, starting transfers between devices, per_device(): far = lax.ppermute(target, 'slot', far_pairs)  24.2 us
    pallas_call x3, Pallas kernels, next_solver(): call(kernel, 'last_solver' if last else 'next_solver', [(CH, 1, PW)] + ([...  18.5 us
    ppermute x4, waiting for transfers between devices, per_device(): far = lax.ppermute(target, 'slot', far_pairs)  16.5 us
    pallas_call x1, Pallas kernels, first_solver(): call(kernel, 'first_solver', [(CH, 1, 2 * PW), (1, PW), (1, K), (PB, K),...  6.16 us
  transfers between devices with their start and end apart: 8, of which 4 were waited for; matrix products, arithmetic and copies ran while one was open for 0% of the time, Pallas kernels for 0%

profile of v4, /device:TPU:7, one launch (start us, length us, event | category | flops | bytes accessed | tf_op | source)
XLA Modules:
  0.0 235.4 jit_solution(11819639242667660325)
XLA Ops:
  1.4 6.2 %first_solver.1 = (f32[32,1,768]{2,1,0:T(1,128)S(1)}, f32[1,384]{1,0:T(1,128)S(1)}, f32[1,2048]{1,0:T(1,128)S(1)}, f32[375,2048]{1,0:T(8,128)S(1)}, f32[3,1792]{...) custom-call(s32[2]{0:T(128)S(1)} %pad_add_fusion.ids, ...), custom_call_target="tpu_custom_call" | custom-call | tf_op jit(solution)/shard_map/first_solver/pallas_call | solution.py:277
  7.5 17.4 %all_to_all.60.arrived = f32[32,1,768]{2,1,0:T(1,128)S(1)} all-to-all(f32[32,1,768]{2,1,0:T(1,128)S(1)} %get-tuple-element.28), channel_id=1, replica_groups=mesh['chan'=32,'slot'=8] {'chan'}, dimensions={0} | all-to-all | bytes 196608 | tf_op jit(solution)/shard_map/all_to_all | solution.py:421
  25.8 6.0 %collective-permute-start.1 = (f32[1,384]{1,0:T(1,128)S(1)}, f32[1,384]{1,0:T(1,128)S(1)}, u32[]{:S(2)}, u32[]{:S(2)}) collective-permute-start(f32[1,384]{1,0:T(1,128)S(1)} %get-tuple-element.32.target), channel_id=1, source_target_pairs={{1,2},{2,1},{3,4},{4,3},{5,6},{6,5},{9,10},{10,9},{11,12},{12,11},... | collective-permute-start | bytes 4616 | tf_op jit(solution)/shard_map/ppermute | solution.py:461
  31.9 4.2 %collective-permute-done.1.far = f32[1,384]{1,0:T(1,128)S(1)} collective-permute-done((f32[1,384]{1,0:T(1,128)S(1)}, f32[1,384]{1,0:T(1,128)S(1)}, u32[]{:S(2)}, u32[]{:S(2)}) %collective-permute-start.1) | collective-permute-done | bytes 1568 | tf_op jit(solution)/shard_map/ppermute | solution.py:461
  36.1 0.9 basis_partial.4
  37.0 15.7 %all_to_all.61.arrived = f32[32,1,2048]{2,1,0:T(1,128)S(1)} all-to-all(f32[32,1,2048]{2,1,0:T(1,128)S(1)} %basis_partial.4), channel_id=1, replica_groups=mesh['chan'=32,'slot'=8] {'chan'}, dimensions={0} | all-to-all | bytes 524288 | tf_op jit(solution)/shard_map/all_to_all | solution.py:421
  52.7 1.0 own_screen.4
  53.7 11.0 %all_to_all.62.tec = f32[32,1,384]{2,1,0:T(1,128)S(1)} all-to-all(f32[32,1,384]{2,1,0:T(1,128)S(1)} %get-tuple-element.35), channel_id=1, replica_groups=mesh['chan'=32,'slot'=8] {'chan'}, dimensions={0} | all-to-all | bytes 98304 | tf_op jit(solution)/shard_map/all_to_all | solution.py:421
  64.7 6.1 %next_solver.2 = f32[32,1,384]{2,1,0:T(1,128)S(1)} custom-call(f32[1,1]{1,0:T(1,128)} %bitcast.8.freq, f32[32,1,384]{2,1,0:T(1,128)S(1)} %all_to_all.62.tec, f32[3,1792]{1,0:T(4,128)S(1)} %get-tuple-element.36.vis, f32[208,224]{1,0:T(8,128)S(1)} %get-tuple-element.37.base, f32[32,1792]{1,0:T(8,128)S(1)} %get-tuple-element.38.uvw, ...), custom_call_target="tpu_custom_call" | custom-call | tf_op jit(solution)/shard_map/next_solver/pallas_call | solution.py:305
  70.9 10.9 %all_to_all.63.arrived = f32[32,1,384]{2,1,0:T(1,128)S(1)} all-to-all(f32[32,1,384]{2,1,0:T(1,128)S(1)} %next_solver.2), channel_id=1, replica_groups=mesh['chan'=32,'slot'=8] {'chan'}, dimensions={0} | all-to-all | bytes 98304 | tf_op jit(solution)/shard_map/all_to_all | solution.py:421
  81.8 6.0 %collective-permute-start.3 = (f32[1,384]{1,0:T(1,128)S(1)}, f32[1,384]{1,0:T(1,128)S(1)}, u32[]{:S(2)}, u32[]{:S(2)}) collective-permute-start(f32[1,384]{1,0:T(1,128)S(1)} %own_target.3.target), channel_id=1, source_target_pairs={{1,2},{2,1},{3,4},{4,3},{5,6},{6,5},{9,10},{10,9},{11,12},{12,11},... | collective-permute-start | bytes 4616 | tf_op jit(solution)/shard_map/ppermute | solution.py:461
  88.0 4.2 %collective-permute-done.3.far = f32[1,384]{1,0:T(1,128)S(1)} collective-permute-done((f32[1,384]{1,0:T(1,128)S(1)}, f32[1,384]{1,0:T(1,128)S(1)}, u32[]{:S(2)}, u32[]{:S(2)}) %collective-permute-start.3) | collective-permute-done | bytes 1568 | tf_op jit(solution)/shard_map/ppermute | solution.py:461
  92.1 0.9 basis_partial.5
  93.1 15.8 %all_to_all.64.arrived = f32[32,1,2048]{2,1,0:T(1,128)S(1)} all-to-all(f32[32,1,2048]{2,1,0:T(1,128)S(1)} %basis_partial.5), channel_id=1, replica_groups=mesh['chan'=32,'slot'=8] {'chan'}, dimensions={0} | all-to-all | bytes 524288 | tf_op jit(solution)/shard_map/all_to_all | solution.py:421
  108.9 1.0 own_screen.5
  109.9 11.0 %all_to_all.65.tec = f32[32,1,384]{2,1,0:T(1,128)S(1)} all-to-all(f32[32,1,384]{2,1,0:T(1,128)S(1)} %get-tuple-element.43), channel_id=1, replica_groups=mesh['chan'=32,'slot'=8] {'chan'}, dimensions={0} | all-to-all | bytes 98304 | tf_op jit(solution)/shard_map/all_to_all | solution.py:421
  120.9 6.1 %next_solver.3 = f32[32,1,384]{2,1,0:T(1,128)S(1)} custom-call(f32[1,1]{1,0:T(1,128)} %bitcast.9.freq, f32[32,1,384]{2,1,0:T(1,128)S(1)} %all_to_all.65.tec, f32[3,1792]{1,0:T(4,128)S(1)} %get-tuple-element.36.vis, f32[208,224]{1,0:T(8,128)S(1)} %get-tuple-element.37.base, f32[32,1792]{1,0:T(8,128)S(1)} %get-tuple-element.38.uvw, ...), custom_call_target="tpu_custom_call" | custom-call | tf_op jit(solution)/shard_map/next_solver/pallas_call | solution.py:305
  127.0 10.9 %all_to_all.66.arrived = f32[32,1,384]{2,1,0:T(1,128)S(1)} all-to-all(f32[32,1,384]{2,1,0:T(1,128)S(1)} %next_solver.3), channel_id=1, replica_groups=mesh['chan'=32,'slot'=8] {'chan'}, dimensions={0} | all-to-all | bytes 98304 | tf_op jit(solution)/shard_map/all_to_all | solution.py:421
  137.9 6.0 %collective-permute-start.5 = (f32[1,384]{1,0:T(1,128)S(1)}, f32[1,384]{1,0:T(1,128)S(1)}, u32[]{:S(2)}, u32[]{:S(2)}) collective-permute-start(f32[1,384]{1,0:T(1,128)S(1)} %own_target.4.target), channel_id=1, source_target_pairs={{1,2},{2,1},{3,4},{4,3},{5,6},{6,5},{9,10},{10,9},{11,12},{12,11},... | collective-permute-start | bytes 4616 | tf_op jit(solution)/shard_map/ppermute | solution.py:461
  144.1 4.2 %collective-permute-done.5.far = f32[1,384]{1,0:T(1,128)S(1)} collective-permute-done((f32[1,384]{1,0:T(1,128)S(1)}, f32[1,384]{1,0:T(1,128)S(1)}, u32[]{:S(2)}, u32[]{:S(2)}) %collective-permute-start.5) | collective-permute-done | bytes 1568 | tf_op jit(solution)/shard_map/ppermute | solution.py:461
  148.3 0.9 basis_partial.6
  149.2 15.6 %all_to_all.67.arrived = f32[32,1,2048]{2,1,0:T(1,128)S(1)} all-to-all(f32[32,1,2048]{2,1,0:T(1,128)S(1)} %basis_partial.6), channel_id=1, replica_groups=mesh['chan'=32,'slot'=8] {'chan'}, dimensions={0} | all-to-all | bytes 524288 | tf_op jit(solution)/shard_map/all_to_all | solution.py:421
  164.8 1.0 own_screen.6
  165.8 11.0 %all_to_all.68.tec = f32[32,1,384]{2,1,0:T(1,128)S(1)} all-to-all(f32[32,1,384]{2,1,0:T(1,128)S(1)} %get-tuple-element.45), channel_id=1, replica_groups=mesh['chan'=32,'slot'=8] {'chan'}, dimensions={0} | all-to-all | bytes 98304 | tf_op jit(solution)/shard_map/all_to_all | solution.py:421
  176.8 6.2 %last_solver.1 = (f32[32,1,384]{2,1,0:T(1,128)S(1)}, f32[1,1,1770]{2,1,0:T(1,128)}, f32[1,1,1770]{2,1,0:T(1,128)}) custom-call(f32[1,1]{1,0:T(1,128)} %bitcast.10.freq, f32[32,1,384]{2,1,0:T(1,128)S(1)} %all_to_all.68.tec, f32[3,1792]{1,0:T(4,128)S(1)} %get-tuple-element.36.vis, f32[208,224]{1,0:T(8,128)S(1)} %get-tuple-element.37.base, ...), custom_call_target="tpu_custom_call" | custom-call | tf_op jit(solution)/shard_map/last_solver/pallas_call | solution.py:305
  183.0 10.9 %all_to_all.69.arrived = f32[32,1,384]{2,1,0:T(1,128)S(1)} all-to-all(f32[32,1,384]{2,1,0:T(1,128)S(1)} %get-tuple-element.46), channel_id=1, replica_groups=mesh['chan'=32,'slot'=8] {'chan'}, dimensions={0} | all-to-all | bytes 98304 | tf_op jit(solution)/shard_map/all_to_all | solution.py:421
  193.9 6.0 %collective-permute-start.7 = (f32[1,384]{1,0:T(1,128)S(1)}, f32[1,384]{1,0:T(1,128)S(1)}, u32[]{:S(2)}, u32[]{:S(2)}) collective-permute-start(f32[1,384]{1,0:T(1,128)S(1)} %own_target.5.target), channel_id=1, source_target_pairs={{1,2},{2,1},{3,4},{4,3},{5,6},{6,5},{9,10},{10,9},{11,12},{12,11},... | collective-permute-start | bytes 4616 | tf_op jit(solution)/shard_map/ppermute | solution.py:461
  200.3 4.0 %collective-permute-done.7.far = f32[1,384]{1,0:T(1,128)S(1)} collective-permute-done((f32[1,384]{1,0:T(1,128)S(1)}, f32[1,384]{1,0:T(1,128)S(1)}, u32[]{:S(2)}, u32[]{:S(2)}) %collective-permute-start.7) | collective-permute-done | bytes 1568 | tf_op jit(solution)/shard_map/ppermute | solution.py:461
  205.2 15.6 %all_to_all.70.arrived = f32[32,1,2048]{2,1,0:T(1,128)S(1)} all-to-all(f32[32,1,2048]{2,1,0:T(1,128)S(1)} %basis_partial.7), channel_id=1, replica_groups=mesh['chan'=32,'slot'=8] {'chan'}, dimensions={0} | all-to-all | bytes 524288 | tf_op jit(solution)/shard_map/all_to_all | solution.py:421
  220.9 1.0 own_screen.7
  221.9 11.0 %all_to_all.71.vals = f32[32,1,384]{2,1,0:T(1,128)S(1)} all-to-all(f32[32,1,384]{2,1,0:T(1,128)S(1)} %get-tuple-element.48), channel_id=1, replica_groups=mesh['chan'=32,'slot'=8] {'chan'}, dimensions={0} | all-to-all | bytes 98304 | tf_op jit(solution)/shard_map/all_to_all | solution.py:421
  232.9 2.6 %final_place.1 = f32[60,1,200]{2,1,0:T(1,128)} custom-call(f32[32,1,384]{2,1,0:T(1,128)S(1)} %all_to_all.71.vals, s32[32,1,384]{2,1,0:T(1,128)S(1)} %get-tuple-element.30.stations, s32[32,1,384]{2,1,0:T(1,128)S(1)} %get-tuple-element.31.dirs), custom_call_target="tpu_custom_call" | custom-call | tf_op jit(solution)/shard_map/final_place/pallas_call | solution.py:328
  (14 shorter events, 2.6 us)
Async XLA Ops:
  25.8 10.3 %collective-permute-start.1 = (f32[1,384]{1,0:T(1,128)S(1)}, f32[1,384]{1,0:T(1,128)S(1)}, u32[]{:S(2)}, u32[]{:S(2)}) collective-permute-start(f32[1,384]{1,0:T(1,128)S(1)} %get-tuple-element.32.target), channel_id=1, source_target_pairs={{1,2},{2,1},{3,4},{4,3},{5,6},{6,5},{9,10},{10,9},{11,12},{12,11},... | collective-permute-start | bytes 4616 | tf_op jit(solution)/shard_map/ppermute | solution.py:461
  31.8 4.3 %collective-permute-start = (f32[1,384]{1,0:T(1,128)S(1)}, f32[1,384]{1,0:T(1,128)S(1)}, u32[]{:S(2)}, u32[]{:S(2)}) collective-permute-start(f32[1,384]{1,0:T(1,128)S(1)} %get-tuple-element.32.target), channel_id=1, source_target_pairs={{0,1},{1,0},{2,3},{3,2},{4,5},{5,4},{6,7},{7,6},{8,9},{9,8},{10,11... | collective-permute-start | bytes 4616 | tf_op jit(solution)/shard_map/ppermute | solution.py:462
  81.8 10.3 %collective-permute-start.3 = (f32[1,384]{1,0:T(1,128)S(1)}, f32[1,384]{1,0:T(1,128)S(1)}, u32[]{:S(2)}, u32[]{:S(2)}) collective-permute-start(f32[1,384]{1,0:T(1,128)S(1)} %own_target.3.target), channel_id=1, source_target_pairs={{1,2},{2,1},{3,4},{4,3},{5,6},{6,5},{9,10},{10,9},{11,12},{12,11},... | collective-permute-start | bytes 4616 | tf_op jit(solution)/shard_map/ppermute | solution.py:461
  87.9 4.3 %collective-permute-start.2 = (f32[1,384]{1,0:T(1,128)S(1)}, f32[1,384]{1,0:T(1,128)S(1)}, u32[]{:S(2)}, u32[]{:S(2)}) collective-permute-start(f32[1,384]{1,0:T(1,128)S(1)} %own_target.3.target), channel_id=1, source_target_pairs={{0,1},{1,0},{2,3},{3,2},{4,5},{5,4},{6,7},{7,6},{8,9},{9,8},{10,11... | collective-permute-start | bytes 4616 | tf_op jit(solution)/shard_map/ppermute | solution.py:462
  137.9 10.3 %collective-permute-start.5 = (f32[1,384]{1,0:T(1,128)S(1)}, f32[1,384]{1,0:T(1,128)S(1)}, u32[]{:S(2)}, u32[]{:S(2)}) collective-permute-start(f32[1,384]{1,0:T(1,128)S(1)} %own_target.4.target), channel_id=1, source_target_pairs={{1,2},{2,1},{3,4},{4,3},{5,6},{6,5},{9,10},{10,9},{11,12},{12,11},... | collective-permute-start | bytes 4616 | tf_op jit(solution)/shard_map/ppermute | solution.py:461
  144.0 4.3 %collective-permute-start.4 = (f32[1,384]{1,0:T(1,128)S(1)}, f32[1,384]{1,0:T(1,128)S(1)}, u32[]{:S(2)}, u32[]{:S(2)}) collective-permute-start(f32[1,384]{1,0:T(1,128)S(1)} %own_target.4.target), channel_id=1, source_target_pairs={{0,1},{1,0},{2,3},{3,2},{4,5},{5,4},{6,7},{7,6},{8,9},{9,8},{10,11... | collective-permute-start | bytes 4616 | tf_op jit(solution)/shard_map/ppermute | solution.py:462
  193.9 10.3 %collective-permute-start.7 = (f32[1,384]{1,0:T(1,128)S(1)}, f32[1,384]{1,0:T(1,128)S(1)}, u32[]{:S(2)}, u32[]{:S(2)}) collective-permute-start(f32[1,384]{1,0:T(1,128)S(1)} %own_target.5.target), channel_id=1, source_target_pairs={{1,2},{2,1},{3,4},{4,3},{5,6},{6,5},{9,10},{10,9},{11,12},{12,11},... | collective-permute-start | bytes 4616 | tf_op jit(solution)/shard_map/ppermute | solution.py:461
  200.0 4.3 %collective-permute-start.6 = (f32[1,384]{1,0:T(1,128)S(1)}, f32[1,384]{1,0:T(1,128)S(1)}, u32[]{:S(2)}, u32[]{:S(2)}) collective-permute-start(f32[1,384]{1,0:T(1,128)S(1)} %own_target.5.target), channel_id=1, source_target_pairs={{0,1},{1,0},{2,3},{3,2},{4,5},{5,4},{6,7},{7,6},{8,9},{9,8},{10,11... | collective-permute-start | bytes 4616 | tf_op jit(solution)/shard_map/ppermute | solution.py:462

commit v5 on v4

--- a/solution.py
+++ b/solution.py
@@ -80,7 +80,7 @@
     return jnp.concatenate([part.astype(BF16) for part in split3(field)], axis=1)
 
 
-def solver(freq, tec, vis, base, coords, pairs, cols, stations, dirs, out, work, own=None, kept=None):
+def solver(freq, tec, vis, base, coords, pairs, cols, stations, dirs, out, work, own=None, kept=None, ship=None):
     acc, re_s, im_s = work
     tec_scale = TEC_PHASE / freq[...]
     turn_scale = jnp.broadcast_to(tec_scale * (1.0 / TWO_PI), (8, 128))
@@ -161,13 +161,17 @@
         s, d = joined(stations, i), joined(dirs, i)
         got = picked(numer_parts, s, d)
         for k in range(NB):
-            out[NB * i + k, 0:1, 0:PW] = got[:, k * PW : (k + 1) * PW]
+            for start in (0,) if first else ship[:2]:
+                out[start + NB * i + k, 0:1, 0:PW] = got[:, k * PW : (k + 1) * PW]
         if first:
             for k in range(NB):
                 out[NB * i + k, 0:1, PW : 2 * PW] = factors
         return carry
 
     lax.fori_loop(0, CH // NB, pick, 0)
+    if not first:
+        row = ship[1] + ship[2]
+        out[row, 0:1, 0:PW] = out[row, 0:1, 0:PW] + ship[3]
 
 
 def params():
@@ -289,8 +293,13 @@
     )(ids, freq, real, imag, weight, coords, pairs, directions, flux, start, points, eigen, basis)
 
 
-def next_solver(freq, tec, held, last):
-    def kernel(freq, tec, vis, base, uvw, ants, cols, stations, dirs, out, *refs):
+def halves(ids):
+    mine = CH * (1 - ids[1] % 2)
+    return mine, CH - mine
+
+
+def next_solver(ids, freq, own, pack, tec, held, last):
+    def kernel(ids, freq, own, pack, tec, vis, base, uvw, ants, cols, stations, dirs, out, *refs):
         if last:
             real, imag, acc, re_s, im_s, left = refs
             kept = (left, real, imag)
@@ -300,15 +309,16 @@
         solver(
             freq, tec, vis, base, uvw, ants, cols, stations, dirs, out, (acc, re_s, im_s),
             kept=kept,
+            ship=halves(ids) + (ids[0], own[...] * pack[:, PW : 2 * PW]),
         )
 
     return call(
         kernel,
         "last_solver" if last else "next_solver",
-        [(CH, 1, PW)] + ([(1, 1, B), (1, 1, B)] if last else []),
-        [VM] * 9,
+        [(2 * CH, 1, PW)] + ([(1, 1, B), (1, 1, B)] if last else []),
+        [SM] + [VM] * 11,
         WORK + ([pltpu.VMEM((2, BP), F32)] if last else []),
-    )(freq, tec, *held)
+    )(ids, freq, own, pack, tec, *held)
 
 
 def final_place(vals, stations, dirs):
@@ -331,7 +341,7 @@
 
 
 def own_target_first(ids, arrived, own, stations, dirs):
-    def kernel(ids, arrived, own, stations, dirs, out, den_out):
+    def kernel(ids, arrived, own, stations, dirs, out):
         mine = ids[0]
         factors = jnp.concatenate([arrived[c, 0:1, PW : 2 * PW] for c in range(CH)], axis=0)
         total = jnp.sum(arrived[:, :, 0:PW], axis=0)
@@ -345,22 +355,29 @@
         weights = at_points(factors[:, 0:128], stations[mine])
         fluxes = at_points(factors[:, 128:384], dirs[mine])
         den = jnp.sum(weights * fluxes, axis=0, keepdims=True)
-        den_out[...] = den
+        out[:, PW : 2 * PW] = den
         lane = lax.broadcasted_iota(jnp.int32, (1, PW), 1)
-        out[...] = jnp.where(lane < PB, own[...] + total / den, 0.0)
-
-    return call(kernel, "own_target_first", [(1, PW), (1, PW)], [SM] + [VM] * 4)(
+        out[:, 0:PW] = jnp.where(lane < PB, own[...] + total / den, 0.0)
+
+    return call(kernel, "own_target_first", [(1, 2 * PW)], [SM] + [VM] * 4)(
         ids, arrived, own, stations, dirs
-    )
-
-
-def own_target(arrived, own, denominator):
-    def kernel(arrived, own, den, out):
-        total = jnp.sum(arrived[...], axis=0)
+    )[0]
+
+
+def own_target(ids, slots, arrived, own, pack, far_pack):
+    def kernel(ids, arrived, own, pack, far_pack, out, far_out):
+        mine, pair = halves(ids)
+        total = jnp.sum(arrived[pl.ds(mine, CH)], axis=0)
+        far = jnp.sum(arrived[pl.ds(pair, CH)], axis=0)
         lane = lax.broadcasted_iota(jnp.int32, (1, PW), 1)
-        out[...] = jnp.where(lane < PB, own[...] + total / den[...], 0.0)
-
-    return call(kernel, "own_target", [(1, PW)], [VM] * 3)(arrived, own, denominator)[0]
+        inner = (ids[1] > 0) & (ids[1] < slots - 1)
+        out[...] = jnp.where(lane < PB, own[...] + total / pack[:, PW : 2 * PW], 0.0)
+        ends = jnp.where(inner, PB, 0)
+        far_out[...] = jnp.where(lane < ends, far / far_pack[:, PW : 2 * PW], 0.0)
+
+    return call(kernel, "own_target", [(1, PW), (1, PW)], [SM] + [VM] * 4)(
+        ids, arrived, own, pack, far_pack
+    )
 
 
 GROUPS = [(r, min(8, PB - r)) for r in range(0, PB, 8)]
@@ -370,7 +387,7 @@
     def kernel(ids, target, near, far, weight, basis, out, tall):
         slot = ids[1]
         ends = (slot == 0).astype(F32) + (slot == slots - 1).astype(F32)
-        x = (target[...] + SMOOTHING * (near[...] + far[...])) / (1.0 + SMOOTHING * (2.0 - ends))
+        x = (target[:, 0:PW] + SMOOTHING * (near[:, 0:PW] + far[:, 0:PW])) / (1.0 + SMOOTHING * (2.0 - ends))
         tall[...] = jnp.broadcast_to(x, (128, PW)).T
         total = jnp.zeros((8, K), F32)
         for r, m in GROUPS:
@@ -451,14 +468,21 @@
         )
     ]
     sent, own, weight, basis, *held = first_solver(ids, freq, *arguments)
+    pair_groups = [
+        [c * slots + t for t in (i, (i + 1) % slots) for c in range(CH)]
+        for i in range(1, slots, 2)
+    ]
     for iteration in range(ITERS):
-        if iteration > 0:
-            sent, *left = next_solver(freq, gathered, held, iteration == ITERS - 1)
         if iteration == 0:
-            target, denominator = own_target_first(ids, exchange(sent), own, held[-2], held[-1])
+            pack = own_target_first(ids, exchange(sent), own, held[-2], held[-1])
+            target = pack
+            far = far_pack = lax.ppermute(pack, "slot", far_pairs)
         else:
-            target = own_target(exchange(sent), own, denominator)
-        far = lax.ppermute(target, "slot", far_pairs)
+            sent, *left = next_solver(ids, freq, own, pack, gathered, held, iteration == ITERS - 1)
+            arrived = lax.all_to_all(
+                sent, ("chan", "slot"), 0, 0, tiled=True, axis_index_groups=pair_groups
+            )
+            target, far = own_target(ids, slots, arrived, own, pack, far_pack)
         near = lax.ppermute(target, "slot", near_pairs)
         partial = basis_partial(ids, slots, target, near, far, weight, basis)
         coefficients, own, spread = own_screen(exchange(partial), basis)

time: 236 us -> 239 us (1.013)
  blocking collectives: 157 us -> 179 us
  starting transfers between devices: 24.8 us -> 6.59 us
  waiting for transfers between devices: 16.6 us -> 11.5 us
  Pallas kernels: 35.7 us -> 39.3 us
    all_to_all x0 -> x3, blocking collectives: none -> 53.2 us  [per_device(): lax.all_to_all(sent, ('chan', 'slot'), 0, 0, tiled=True, axis_index_group...]
    all_to_all x12 -> x9, blocking collectives: 157 us -> 126 us  [exchange(): lax.all_to_all(value, 'chan', split_axis=0, concat_axis=0, tiled=True)]
    ppermute x4 -> x1, starting transfers between devices: 24.2 us -> 6.04 us  [per_device(): far = far_pack = lax.ppermute(pack, 'slot', far_pairs)]
    ppermute x4 -> x1, waiting for transfers between devices: 16.5 us -> 4.21 us  [per_device(): far = far_pack = lax.ppermute(pack, 'slot', far_pairs)]
    ppermute x4, waiting for transfers between devices: 0.01 us -> 7.25 us  [per_device(): near = lax.ppermute(target, 'slot', near_pairs)]
    pallas_call x7, Pallas kernels: 19.4 us -> 23.1 us  [the longest x3 20.4 us: next_solver(): call(kernel, 'last_solver' if last else 'next_solver', [(2 * CH, 1, PW)]...]
  transfers between devices with their start and end apart: 8 -> 5, of which waited for: 4 -> 4; matrix products, arithmetic and copies ran while one was open for 0% -> 0% of each run, Pallas kernels for 0% -> 0%
where the time goes in v5:
time: 239 us; the launch traced here: 238 us
  blocking collectives  179 us (75%)
  Pallas kernels  39.3 us (16%)
  waiting for transfers between devices  11.5 us (5%)
  starting transfers between devices  6.59 us (3%)
    all_to_all x9, blocking collectives, exchange(): lax.all_to_all(value, 'chan', split_axis=0, concat_axis=0, tiled=True)  126 us
    all_to_all x3, blocking collectives, per_device(): lax.all_to_all(sent, ('chan', 'slot'), 0, 0, tiled=True, axis_index_group...  53.2 us
    pallas_call x3, Pallas kernels, next_solver(): call(kernel, 'last_solver' if last else 'next_solver', [(2 * CH, 1, PW)]...  20.4 us
    ppermute x4, waiting for transfers between devices, per_device(): near = lax.ppermute(target, 'slot', near_pairs)  7.25 us
    pallas_call x1, Pallas kernels, first_solver(): call(kernel, 'first_solver', [(CH, 1, 2 * PW), (1, PW), (1, K), (PB, K),...  6.16 us
    ppermute x1, starting transfers between devices, per_device(): far = far_pack = lax.ppermute(pack, 'slot', far_pairs)  6.04 us
  transfers between devices with their start and end apart: 5, of which 4 were waited for; matrix products, arithmetic and copies ran while one was open for 0% of the time, Pallas kernels for 0%

profile of v5, /device:TPU:7, one launch (start us, length us, event | category | flops | bytes accessed | tf_op | source)
XLA Modules:
  0.0 238.1 jit_solution(2773454579546557066)
XLA Ops:
  1.4 6.2 %first_solver.1 = (f32[32,1,768]{2,1,0:T(1,128)S(1)}, f32[1,384]{1,0:T(1,128)S(1)}, f32[1,2048]{1,0:T(1,128)S(1)}, f32[375,2048]{1,0:T(8,128)S(1)}, f32[3,1792]{...) custom-call(s32[2]{0:T(128)S(1)} %pad_add_fusion.ids, ...), custom_call_target="tpu_custom_call" | custom-call | tf_op jit(solution)/shard_map/first_solver/pallas_call | solution.py:281
  7.5 17.4 %all_to_all.60.arrived = f32[32,1,768]{2,1,0:T(1,128)S(1)} all-to-all(f32[32,1,768]{2,1,0:T(1,128)S(1)} %get-tuple-element.32), channel_id=1, replica_groups=mesh['chan'=32,'slot'=8] {'chan'}, dimensions={0} | all-to-all | bytes 196608 | tf_op jit(solution)/shard_map/all_to_all | solution.py:438
  24.9 0.8 own_target_first.1.target.pack
  25.8 6.0 %collective-permute-start.1 = (f32[1,768]{1,0:T(1,128)S(1)}, f32[1,768]{1,0:T(1,128)S(1)}, u32[]{:S(2)}, u32[]{:S(2)}) collective-permute-start(f32[1,768]{1,0:T(1,128)S(1)} %own_target_first.1.target.pack), channel_id=1, source_target_pairs={{1,2},{2,1},{3,4},{4,3},{5,6},{6,5},{9,10},{10,9},{11,12},{12,11},... | collective-permute-start | bytes 9224 | tf_op jit(solution)/shard_map/ppermute | solution.py:479
  31.9 4.2 %collective-permute-done.1.far.far_pack = f32[1,768]{1,0:T(1,128)S(1)} collective-permute-done((f32[1,768]{1,0:T(1,128)S(1)}, f32[1,768]{1,0:T(1,128)S(1)}, u32[]{:S(2)}, u32[]{:S(2)}) %collective-permute-start.1) | collective-permute-done | bytes 3104 | tf_op jit(solution)/shard_map/ppermute | solution.py:479
  36.1 0.9 basis_partial.4
  37.0 15.7 %all_to_all.61.arrived = f32[32,1,2048]{2,1,0:T(1,128)S(1)} all-to-all(f32[32,1,2048]{2,1,0:T(1,128)S(1)} %basis_partial.4), channel_id=1, replica_groups=mesh['chan'=32,'slot'=8] {'chan'}, dimensions={0} | all-to-all | bytes 524288 | tf_op jit(solution)/shard_map/all_to_all | solution.py:438
  52.7 1.0 own_screen.4
  53.7 11.0 %all_to_all.62.tec = f32[32,1,384]{2,1,0:T(1,128)S(1)} all-to-all(f32[32,1,384]{2,1,0:T(1,128)S(1)} %get-tuple-element.39), channel_id=1, replica_groups=mesh['chan'=32,'slot'=8] {'chan'}, dimensions={0} | all-to-all | bytes 98304 | tf_op jit(solution)/shard_map/all_to_all | solution.py:438
  64.8 6.7 %next_solver.2 = f32[64,1,384]{2,1,0:T(1,128)S(1)} custom-call(s32[2]{0:T(128)S(1)} %pad_add_fusion.ids, f32[1,1]{1,0:T(1,128)} %bitcast.8.freq, f32[1,384]{1,0:T(1,128)S(1)} %get-tuple-element.38.own, f32[1,768]{1,0:T(1,128)S(1)} %own_target_first.1.target.pack, f32[32,1,384]{2,1,0:T(1,128)S(1)} %all_to_all.62.tec, f32[3,1792]{1,0:T(4,128)S(1)} %get-tuple-element.40.vis, ...), custom_call_target="tpu_custom_call" | custom-call | tf_op jit(solution)/shard_map/next_solver/pallas_call | solution.py:315
  71.4 19.3 %all_to_all.63.arrived = f32[64,1,384]{2,1,0:T(1,128)S(1)} all-to-all(f32[64,1,384]{2,1,0:T(1,128)S(1)} %next_solver.2), channel_id=1, replica_groups={{1,9,17,25,33,41,49,57,65,73,81,89,97,105,113,121,129,137,145,153,161,1..., dimensions={0} | all-to-all | bytes 196608 | tf_op jit(solution)/shard_map/all_to_all | solution.py:482
  90.7 0.6 own_target.3
  91.6 2.4 %collective-permute-done.2.near = f32[1,384]{1,0:T(1,128)S(1)} collective-permute-done((f32[1,384]{1,0:T(1,128)S(1)}, f32[1,384]{1,0:T(1,128)S(1)}, u32[]{:S(2)}, u32[]{:S(2)}) %collective-permute-start.2) | collective-permute-done | bytes 1568 | tf_op jit(solution)/shard_map/ppermute | solution.py:486
  94.1 0.9 basis_partial.5
  95.0 16.3 %all_to_all.64.arrived = f32[32,1,2048]{2,1,0:T(1,128)S(1)} all-to-all(f32[32,1,2048]{2,1,0:T(1,128)S(1)} %basis_partial.5), channel_id=1, replica_groups=mesh['chan'=32,'slot'=8] {'chan'}, dimensions={0} | all-to-all | bytes 524288 | tf_op jit(solution)/shard_map/all_to_all | solution.py:438
  111.2 1.0 own_screen.5
  112.2 11.0 %all_to_all.65.tec = f32[32,1,384]{2,1,0:T(1,128)S(1)} all-to-all(f32[32,1,384]{2,1,0:T(1,128)S(1)} %get-tuple-element.48), channel_id=1, replica_groups=mesh['chan'=32,'slot'=8] {'chan'}, dimensions={0} | all-to-all | bytes 98304 | tf_op jit(solution)/shard_map/all_to_all | solution.py:438
  123.3 6.7 %next_solver.3 = f32[64,1,384]{2,1,0:T(1,128)S(1)} custom-call(s32[2]{0:T(128)S(1)} %pad_add_fusion.ids, f32[1,1]{1,0:T(1,128)} %bitcast.9.freq, f32[1,384]{1,0:T(1,128)S(1)} %get-tuple-element.47.own, f32[1,768]{1,0:T(1,128)S(1)} %own_target_first.1.target.pack, f32[32,1,384]{2,1,0:T(1,128)S(1)} %all_to_all.65.tec, f32[3,1792]{1,0:T(4,128)S(1)} %get-tuple-element.40.vis, ...), custom_call_target="tpu_custom_call" | custom-call | tf_op jit(solution)/shard_map/next_solver/pallas_call | solution.py:315
  129.9 16.9 %all_to_all.66.arrived = f32[64,1,384]{2,1,0:T(1,128)S(1)} all-to-all(f32[64,1,384]{2,1,0:T(1,128)S(1)} %next_solver.3), channel_id=1, replica_groups={{1,9,17,25,33,41,49,57,65,73,81,89,97,105,113,121,129,137,145,153,161,1..., dimensions={0} | all-to-all | bytes 196608 | tf_op jit(solution)/shard_map/all_to_all | solution.py:482
  147.6 2.4 %collective-permute-done.3.near = f32[1,384]{1,0:T(1,128)S(1)} collective-permute-done((f32[1,384]{1,0:T(1,128)S(1)}, f32[1,384]{1,0:T(1,128)S(1)}, u32[]{:S(2)}, u32[]{:S(2)}) %collective-permute-start.3) | collective-permute-done | bytes 1568 | tf_op jit(solution)/shard_map/ppermute | solution.py:486
  150.0 0.9 basis_partial.6
  150.9 16.3 %all_to_all.67.arrived = f32[32,1,2048]{2,1,0:T(1,128)S(1)} all-to-all(f32[32,1,2048]{2,1,0:T(1,128)S(1)} %basis_partial.6), channel_id=1, replica_groups=mesh['chan'=32,'slot'=8] {'chan'}, dimensions={0} | all-to-all | bytes 524288 | tf_op jit(solution)/shard_map/all_to_all | solution.py:438
  167.2 1.0 own_screen.6
  168.2 11.0 %all_to_all.68.tec = f32[32,1,384]{2,1,0:T(1,128)S(1)} all-to-all(f32[32,1,384]{2,1,0:T(1,128)S(1)} %get-tuple-element.52), channel_id=1, replica_groups=mesh['chan'=32,'slot'=8] {'chan'}, dimensions={0} | all-to-all | bytes 98304 | tf_op jit(solution)/shard_map/all_to_all | solution.py:438
  179.2 7.1 %last_solver.1 = (f32[64,1,384]{2,1,0:T(1,128)S(1)}, f32[1,1,1770]{2,1,0:T(1,128)}, f32[1,1,1770]{2,1,0:T(1,128)}) custom-call(s32[2]{0:T(128)S(1)} %pad_add_fusion.ids, f32[1,1]{1,0:T(1,128)} %bitcast.10.freq, f32[1,384]{1,0:T(1,128)S(1)} %get-tuple-element.51.own, f32[1,768]{1,0:T(1,128)S(1)} %own_target_first.1.target.pack, ...), custom_call_target="tpu_custom_call" | custom-call | tf_op jit(solution)/shard_map/last_solver/pallas_call | solution.py:315
  186.3 16.9 %all_to_all.69.arrived = f32[64,1,384]{2,1,0:T(1,128)S(1)} all-to-all(f32[64,1,384]{2,1,0:T(1,128)S(1)} %get-tuple-element.53), channel_id=1, replica_groups={{1,9,17,25,33,41,49,57,65,73,81,89,97,105,113,121,129,137,145,153,161,1..., dimensions={0} | all-to-all | bytes 196608 | tf_op jit(solution)/shard_map/all_to_all | solution.py:482
  204.0 2.4 %collective-permute-done.4.near = f32[1,384]{1,0:T(1,128)S(1)} collective-permute-done((f32[1,384]{1,0:T(1,128)S(1)}, f32[1,384]{1,0:T(1,128)S(1)}, u32[]{:S(2)}, u32[]{:S(2)}) %collective-permute-start.4) | collective-permute-done | bytes 1568 | tf_op jit(solution)/shard_map/ppermute | solution.py:486
  206.4 0.9 basis_partial.7
  207.3 16.3 %all_to_all.70.arrived = f32[32,1,2048]{2,1,0:T(1,128)S(1)} all-to-all(f32[32,1,2048]{2,1,0:T(1,128)S(1)} %basis_partial.7), channel_id=1, replica_groups=mesh['chan'=32,'slot'=8] {'chan'}, dimensions={0} | all-to-all | bytes 524288 | tf_op jit(solution)/shard_map/all_to_all | solution.py:438
  223.6 1.0 own_screen.7
  224.6 11.0 %all_to_all.71.vals = f32[32,1,384]{2,1,0:T(1,128)S(1)} all-to-all(f32[32,1,384]{2,1,0:T(1,128)S(1)} %get-tuple-element.56), channel_id=1, replica_groups=mesh['chan'=32,'slot'=8] {'chan'}, dimensions={0} | all-to-all | bytes 98304 | tf_op jit(solution)/shard_map/all_to_all | solution.py:438
  235.6 2.5 %final_place.1 = f32[60,1,200]{2,1,0:T(1,128)} custom-call(f32[32,1,384]{2,1,0:T(1,128)S(1)} %all_to_all.71.vals, s32[32,1,384]{2,1,0:T(1,128)S(1)} %get-tuple-element.34.stations, s32[32,1,384]{2,1,0:T(1,128)S(1)} %get-tuple-element.35.dirs), custom_call_target="tpu_custom_call" | custom-call | tf_op jit(solution)/shard_map/final_place/pallas_call | solution.py:338
  (8 shorter events, 1.9 us)
Async XLA Ops:
  25.8 10.4 %collective-permute-start.1 = (f32[1,768]{1,0:T(1,128)S(1)}, f32[1,768]{1,0:T(1,128)S(1)}, u32[]{:S(2)}, u32[]{:S(2)}) collective-permute-start(f32[1,768]{1,0:T(1,128)S(1)} %own_target_first.1.target.pack), channel_id=1, source_target_pairs={{1,2},{2,1},{3,4},{4,3},{5,6},{6,5},{9,10},{10,9},{11,12},{12,11},... | collective-permute-start | bytes 9224 | tf_op jit(solution)/shard_map/ppermute | solution.py:479
  31.8 4.3 %collective-permute-start = (f32[1,768]{1,0:T(1,128)S(1)}, f32[1,768]{1,0:T(1,128)S(1)}, u32[]{:S(2)}, u32[]{:S(2)}) collective-permute-start(f32[1,768]{1,0:T(1,128)S(1)} %own_target_first.1.target.pack), channel_id=1, source_target_pairs={{0,1},{1,0},{2,3},{3,2},{4,5},{5,4},{6,7},{7,6},{8,9},{9,8},{10,11... | collective-permute-start | bytes 9224 | tf_op jit(solution)/shard_map/ppermute | solution.py:486
  91.4 2.7 %collective-permute-start.2 = (f32[1,384]{1,0:T(1,128)S(1)}, f32[1,384]{1,0:T(1,128)S(1)}, u32[]{:S(2)}, u32[]{:S(2)}) collective-permute-start(f32[1,384]{1,0:T(1,128)S(1)} %get-tuple-element.45.target), channel_id=1, source_target_pairs={{0,1},{1,0},{2,3},{3,2},{4,5},{5,4},{6,7},{7,6},{8,9},{9,8},{10,11... | collective-permute-start | bytes 4616 | tf_op jit(solution)/shard_map/ppermute | solution.py:486
  147.5 2.5 %collective-permute-start.3 = (f32[1,384]{1,0:T(1,128)S(1)}, f32[1,384]{1,0:T(1,128)S(1)}, u32[]{:S(2)}, u32[]{:S(2)}) collective-permute-start(f32[1,384]{1,0:T(1,128)S(1)} %get-tuple-element.49.target), channel_id=1, source_target_pairs={{0,1},{1,0},{2,3},{3,2},{4,5},{5,4},{6,7},{7,6},{8,9},{9,8},{10,11... | collective-permute-start | bytes 4616 | tf_op jit(solution)/shard_map/ppermute | solution.py:486
  203.9 2.5 %collective-permute-start.4 = (f32[1,384]{1,0:T(1,128)S(1)}, f32[1,384]{1,0:T(1,128)S(1)}, u32[]{:S(2)}, u32[]{:S(2)}) collective-permute-start(f32[1,384]{1,0:T(1,128)S(1)} %get-tuple-element.54.target), channel_id=1, source_target_pairs={{0,1},{1,0},{2,3},{3,2},{4,5},{5,4},{6,7},{7,6},{8,9},{9,8},{10,11... | collective-permute-start | bytes 4616 | tf_op jit(solution)/shard_map/ppermute | solution.py:486

commit v6 on v4

--- a/solution.py
+++ b/solution.py
@@ -71,7 +71,7 @@
     rows = dot_nn(parts, jnp.concatenate([at, at, at], axis=0))
     ahead = d - lax.broadcasted_iota(jnp.int32, (8, d.shape[1]), 0)
     chosen = jnp.zeros((8, d.shape[1]), F32)
-    for g in range(DP // 8):
+    for g in range(D // 8):
         chosen = jnp.where(ahead == 8 * g, rows[8 * g : 8 * g + 8, :], chosen)
     return jnp.sum(chosen, axis=0, keepdims=True)
 
@@ -84,6 +84,8 @@
     acc, re_s, im_s = work
     tec_scale = TEC_PHASE / freq[...]
     turn_scale = jnp.broadcast_to(tec_scale * (1.0 / TWO_PI), (8, 128))
+    re_s[D:DP, :] = jnp.zeros((DP - D, LB), F32)
+    im_s[D:DP, :] = jnp.zeros((DP - D, LB), F32)
     first = own is not None
     if first:
         tec_parts, base_parts, flux_row, mine, own_out = own
@@ -114,7 +116,7 @@
         for h in range(LB // 128):
             sum_re = jnp.zeros((8, 128), F32)
             sum_im = jnp.zeros((8, 128), F32)
-            for g in range(DP // 8):
+            for g in range(D // 8):
                 rows = slice(8 * g, 8 * g + 8)
                 turns = turn_scale * mixed[rows, h * 128 : (h + 1) * 128]
                 r = turns - jnp.round(turns)
@@ -379,13 +381,14 @@
                 total = total + piece
         row = jnp.sum(total, axis=0, keepdims=True) + jnp.sum(piece, axis=0, keepdims=True)
         row = row * weight[...]
+        tile = jnp.concatenate([row[:, k : k + 128] for k in range(0, K, 128)], axis=0)
         for c in range(CH):
-            out[c] = row
+            out[c] = tile
 
     return call(
         kernel,
         "basis_partial",
-        [(CH, 1, K)],
+        [(CH, K // 128, 128)],
         [SM] + [VM] * 5,
         [pltpu.VMEM((PW, 128), F32)],
     )(ids, target, near, far, weight, basis)[0]
@@ -393,13 +396,15 @@
 
 def own_screen(arrived, basis):
     def kernel(arrived, basis, coef, own, out, tall):
-        row = jnp.sum(arrived[...], axis=0)
-        coef[...] = row
-        spread = jnp.broadcast_to(row, (8, K))
+        tile = jnp.sum(arrived[...], axis=0)
+        coef[...] = tile
+        spread = [jnp.broadcast_to(tile[k : k + 1, :], (8, 128)) for k in range(K // 128)]
         tall[PW - 16 : PW, :] = jnp.zeros((16, 128), F32)
         for r, m in GROUPS:
-            piece = basis[r : r + m, :] * spread[0:m, :]
-            parts = [piece[:, k : k + 128] for k in range(0, K, 128)]
+            parts = [
+                basis[r : r + m, 128 * k : 128 * k + 128] * part[0:m, :]
+                for k, part in enumerate(spread)
+            ]
             while len(parts) > 1:
                 parts = [u + v for u, v in zip(parts[0::2], parts[1::2])]
             tall[r : r + m, :] = parts[0]
@@ -411,7 +416,7 @@
     return call(
         kernel,
         "own_screen",
-        [(1, K), (1, PW), (CH, 1, PW)],
+        [(K // 128, 128), (1, PW), (CH, 1, PW)],
         [VM, VM],
         [pltpu.VMEM((PW, 128), F32)],
     )(arrived, basis)
@@ -464,7 +469,7 @@
         coefficients, own, spread = own_screen(exchange(partial), basis)
         gathered = exchange(spread)
     tec_final = jnp.transpose(final_place(gathered, held[-2], held[-1]), (1, 0, 2))
-    return tec_final, coefficients, left[0], left[1]
+    return tec_final, coefficients.reshape(1, K), left[0], left[1]
 
 
 def solution(mesh):

time: 236 us -> 235 us (level)
  no operation moved by 1% of the time
where the time goes in v6:
time: 235 us; the launch traced here: 234 us
  blocking collectives  157 us (67%)
  Pallas kernels  34.8 us (15%)
  starting transfers between devices  24.5 us (10%)
  waiting for transfers between devices  16.8 us (7%)
    all_to_all x12, blocking collectives, exchange(): lax.all_to_all(value, 'chan', split_axis=0, concat_axis=0, tiled=True)  157 us
    ppermute x4, starting transfers between devices, per_device(): far = lax.ppermute(target, 'slot', far_pairs)  24.1 us
    pallas_call x3, Pallas kernels, next_solver(): call(kernel, 'last_solver' if last else 'next_solver', [(CH, 1, PW)] + ([...  18.2 us
    ppermute x4, waiting for transfers between devices, per_device(): far = lax.ppermute(target, 'slot', far_pairs)  16.8 us
    pallas_call x1, Pallas kernels, first_solver(): call(kernel, 'first_solver', [(CH, 1, 2 * PW), (1, PW), (1, K), (PB, K),...  6.1 us
  transfers between devices with their start and end apart: 8, of which 4 were waited for; matrix products, arithmetic and copies ran while one was open for 0% of the time, Pallas kernels for 0%

profile of v6, /device:TPU:7, one launch (start us, length us, event | category | flops | bytes accessed | tf_op | source)
XLA Modules:
  0.0 234.3 jit_solution(3421971553797373057)
XLA Ops:
  1.4 6.1 %first_solver.1 = (f32[32,1,768]{2,1,0:T(1,128)S(1)}, f32[1,384]{1,0:T(1,128)S(1)}, f32[1,2048]{1,0:T(1,128)S(1)}, f32[375,2048]{1,0:T(8,128)S(1)}, f32[3,1792]{...) custom-call(s32[2]{0:T(128)S(1)} %pad_add_fusion.ids, ...), custom_call_target="tpu_custom_call" | custom-call | tf_op jit(solution)/shard_map/first_solver/pallas_call | solution.py:279
  7.5 17.4 %all_to_all.60.arrived = f32[32,1,768]{2,1,0:T(1,128)S(1)} all-to-all(f32[32,1,768]{2,1,0:T(1,128)S(1)} %get-tuple-element.28), channel_id=1, replica_groups=mesh['chan'=32,'slot'=8] {'chan'}, dimensions={0} | all-to-all | bytes 196608 | tf_op jit(solution)/shard_map/all_to_all | solution.py:426
  25.7 6.0 %collective-permute-start.1 = (f32[1,384]{1,0:T(1,128)S(1)}, f32[1,384]{1,0:T(1,128)S(1)}, u32[]{:S(2)}, u32[]{:S(2)}) collective-permute-start(f32[1,384]{1,0:T(1,128)S(1)} %get-tuple-element.32.target), channel_id=1, source_target_pairs={{1,2},{2,1},{3,4},{4,3},{5,6},{6,5},{9,10},{10,9},{11,12},{12,11},... | collective-permute-start | bytes 4616 | tf_op jit(solution)/shard_map/ppermute | solution.py:466
  31.8 4.2 %collective-permute-done.1.far = f32[1,384]{1,0:T(1,128)S(1)} collective-permute-done((f32[1,384]{1,0:T(1,128)S(1)}, f32[1,384]{1,0:T(1,128)S(1)}, u32[]{:S(2)}, u32[]{:S(2)}) %collective-permute-start.1) | collective-permute-done | bytes 1568 | tf_op jit(solution)/shard_map/ppermute | solution.py:466
  36.0 0.9 basis_partial.4
  37.0 15.7 %all_to_all.61.arrived = f32[32,16,128]{2,1,0:T(8,128)S(1)} all-to-all(f32[32,16,128]{2,1,0:T(8,128)S(1)} %basis_partial.4), channel_id=1, replica_groups=mesh['chan'=32,'slot'=8] {'chan'}, dimensions={0} | all-to-all | bytes 524288 | tf_op jit(solution)/shard_map/all_to_all | solution.py:426
  52.7 0.8 own_screen.4
  53.5 11.0 %all_to_all.62.tec = f32[32,1,384]{2,1,0:T(1,128)S(1)} all-to-all(f32[32,1,384]{2,1,0:T(1,128)S(1)} %get-tuple-element.35), channel_id=1, replica_groups=mesh['chan'=32,'slot'=8] {'chan'}, dimensions={0} | all-to-all | bytes 98304 | tf_op jit(solution)/shard_map/all_to_all | solution.py:426
  64.5 6.1 %next_solver.2 = f32[32,1,384]{2,1,0:T(1,128)S(1)} custom-call(f32[1,1]{1,0:T(1,128)} %bitcast.9.freq, f32[32,1,384]{2,1,0:T(1,128)S(1)} %all_to_all.62.tec, f32[3,1792]{1,0:T(4,128)S(1)} %get-tuple-element.36.vis, f32[208,224]{1,0:T(8,128)S(1)} %get-tuple-element.37.base, f32[32,1792]{1,0:T(8,128)S(1)} %get-tuple-element.38.uvw, ...), custom_call_target="tpu_custom_call" | custom-call | tf_op jit(solution)/shard_map/next_solver/pallas_call | solution.py:307
  70.6 10.9 %all_to_all.63.arrived = f32[32,1,384]{2,1,0:T(1,128)S(1)} all-to-all(f32[32,1,384]{2,1,0:T(1,128)S(1)} %next_solver.2), channel_id=1, replica_groups=mesh['chan'=32,'slot'=8] {'chan'}, dimensions={0} | all-to-all | bytes 98304 | tf_op jit(solution)/shard_map/all_to_all | solution.py:426
  81.5 6.0 %collective-permute-start.3 = (f32[1,384]{1,0:T(1,128)S(1)}, f32[1,384]{1,0:T(1,128)S(1)}, u32[]{:S(2)}, u32[]{:S(2)}) collective-permute-start(f32[1,384]{1,0:T(1,128)S(1)} %own_target.3.target), channel_id=1, source_target_pairs={{1,2},{2,1},{3,4},{4,3},{5,6},{6,5},{9,10},{10,9},{11,12},{12,11},... | collective-permute-start | bytes 4616 | tf_op jit(solution)/shard_map/ppermute | solution.py:466
  87.7 4.2 %collective-permute-done.3.far = f32[1,384]{1,0:T(1,128)S(1)} collective-permute-done((f32[1,384]{1,0:T(1,128)S(1)}, f32[1,384]{1,0:T(1,128)S(1)}, u32[]{:S(2)}, u32[]{:S(2)}) %collective-permute-start.3) | collective-permute-done | bytes 1568 | tf_op jit(solution)/shard_map/ppermute | solution.py:466
  91.9 0.9 basis_partial.5
  92.8 15.6 %all_to_all.64.arrived = f32[32,16,128]{2,1,0:T(8,128)S(1)} all-to-all(f32[32,16,128]{2,1,0:T(8,128)S(1)} %basis_partial.5), channel_id=1, replica_groups=mesh['chan'=32,'slot'=8] {'chan'}, dimensions={0} | all-to-all | bytes 524288 | tf_op jit(solution)/shard_map/all_to_all | solution.py:426
  108.4 0.8 own_screen.5
  109.3 11.0 %all_to_all.65.tec = f32[32,1,384]{2,1,0:T(1,128)S(1)} all-to-all(f32[32,1,384]{2,1,0:T(1,128)S(1)} %get-tuple-element.43), channel_id=1, replica_groups=mesh['chan'=32,'slot'=8] {'chan'}, dimensions={0} | all-to-all | bytes 98304 | tf_op jit(solution)/shard_map/all_to_all | solution.py:426
  120.2 6.1 %next_solver.3 = f32[32,1,384]{2,1,0:T(1,128)S(1)} custom-call(f32[1,1]{1,0:T(1,128)} %bitcast.10.freq, f32[32,1,384]{2,1,0:T(1,128)S(1)} %all_to_all.65.tec, f32[3,1792]{1,0:T(4,128)S(1)} %get-tuple-element.36.vis, f32[208,224]{1,0:T(8,128)S(1)} %get-tuple-element.37.base, f32[32,1792]{1,0:T(8,128)S(1)} %get-tuple-element.38.uvw, ...), custom_call_target="tpu_custom_call" | custom-call | tf_op jit(solution)/shard_map/next_solver/pallas_call | solution.py:307
  126.3 10.9 %all_to_all.66.arrived = f32[32,1,384]{2,1,0:T(1,128)S(1)} all-to-all(f32[32,1,384]{2,1,0:T(1,128)S(1)} %next_solver.3), channel_id=1, replica_groups=mesh['chan'=32,'slot'=8] {'chan'}, dimensions={0} | all-to-all | bytes 98304 | tf_op jit(solution)/shard_map/all_to_all | solution.py:426
  137.2 6.0 %collective-permute-start.5 = (f32[1,384]{1,0:T(1,128)S(1)}, f32[1,384]{1,0:T(1,128)S(1)}, u32[]{:S(2)}, u32[]{:S(2)}) collective-permute-start(f32[1,384]{1,0:T(1,128)S(1)} %own_target.4.target), channel_id=1, source_target_pairs={{1,2},{2,1},{3,4},{4,3},{5,6},{6,5},{9,10},{10,9},{11,12},{12,11},... | collective-permute-start | bytes 4616 | tf_op jit(solution)/shard_map/ppermute | solution.py:466
  143.4 4.2 %collective-permute-done.5.far = f32[1,384]{1,0:T(1,128)S(1)} collective-permute-done((f32[1,384]{1,0:T(1,128)S(1)}, f32[1,384]{1,0:T(1,128)S(1)}, u32[]{:S(2)}, u32[]{:S(2)}) %collective-permute-start.5) | collective-permute-done | bytes 1568 | tf_op jit(solution)/shard_map/ppermute | solution.py:466
  147.6 0.9 basis_partial.6
  148.5 15.6 %all_to_all.67.arrived = f32[32,16,128]{2,1,0:T(8,128)S(1)} all-to-all(f32[32,16,128]{2,1,0:T(8,128)S(1)} %basis_partial.6), channel_id=1, replica_groups=mesh['chan'=32,'slot'=8] {'chan'}, dimensions={0} | all-to-all | bytes 524288 | tf_op jit(solution)/shard_map/all_to_all | solution.py:426
  165.0 11.0 %all_to_all.68.tec = f32[32,1,384]{2,1,0:T(1,128)S(1)} all-to-all(f32[32,1,384]{2,1,0:T(1,128)S(1)} %get-tuple-element.45), channel_id=1, replica_groups=mesh['chan'=32,'slot'=8] {'chan'}, dimensions={0} | all-to-all | bytes 98304 | tf_op jit(solution)/shard_map/all_to_all | solution.py:426
  176.0 6.1 %last_solver.1 = (f32[32,1,384]{2,1,0:T(1,128)S(1)}, f32[1,1,1770]{2,1,0:T(1,128)}, f32[1,1,1770]{2,1,0:T(1,128)}) custom-call(f32[1,1]{1,0:T(1,128)} %bitcast.11.freq, f32[32,1,384]{2,1,0:T(1,128)S(1)} %all_to_all.68.tec, f32[3,1792]{1,0:T(4,128)S(1)} %get-tuple-element.36.vis, f32[208,224]{1,0:T(8,128)S(1)} %get-tuple-element.37.base, ...), custom_call_target="tpu_custom_call" | custom-call | tf_op jit(solution)/shard_map/last_solver/pallas_call | solution.py:307
  182.1 10.9 %all_to_all.69.arrived = f32[32,1,384]{2,1,0:T(1,128)S(1)} all-to-all(f32[32,1,384]{2,1,0:T(1,128)S(1)} %get-tuple-element.46), channel_id=1, replica_groups=mesh['chan'=32,'slot'=8] {'chan'}, dimensions={0} | all-to-all | bytes 98304 | tf_op jit(solution)/shard_map/all_to_all | solution.py:426
  193.0 6.0 %collective-permute-start.7 = (f32[1,384]{1,0:T(1,128)S(1)}, f32[1,384]{1,0:T(1,128)S(1)}, u32[]{:S(2)}, u32[]{:S(2)}) collective-permute-start(f32[1,384]{1,0:T(1,128)S(1)} %own_target.5.target), channel_id=1, source_target_pairs={{1,2},{2,1},{3,4},{4,3},{5,6},{6,5},{9,10},{10,9},{11,12},{12,11},... | collective-permute-start | bytes 4616 | tf_op jit(solution)/shard_map/ppermute | solution.py:466
  199.2 4.2 %collective-permute-done.7.far = f32[1,384]{1,0:T(1,128)S(1)} collective-permute-done((f32[1,384]{1,0:T(1,128)S(1)}, f32[1,384]{1,0:T(1,128)S(1)}, u32[]{:S(2)}, u32[]{:S(2)}) %collective-permute-start.7) | collective-permute-done | bytes 1568 | tf_op jit(solution)/shard_map/ppermute | solution.py:466
  203.4 0.9 basis_partial.7
  204.3 15.6 %all_to_all.70.arrived = f32[32,16,128]{2,1,0:T(8,128)S(1)} all-to-all(f32[32,16,128]{2,1,0:T(8,128)S(1)} %basis_partial.7), channel_id=1, replica_groups=mesh['chan'=32,'slot'=8] {'chan'}, dimensions={0} | all-to-all | bytes 524288 | tf_op jit(solution)/shard_map/all_to_all | solution.py:426
  220.0 0.9 own_screen.7
  220.8 11.0 %all_to_all.71.vals = f32[32,1,384]{2,1,0:T(1,128)S(1)} all-to-all(f32[32,1,384]{2,1,0:T(1,128)S(1)} %get-tuple-element.48), channel_id=1, replica_groups=mesh['chan'=32,'slot'=8] {'chan'}, dimensions={0} | all-to-all | bytes 98304 | tf_op jit(solution)/shard_map/all_to_all | solution.py:426
  231.8 2.5 %final_place.1 = f32[60,1,200]{2,1,0:T(1,128)} custom-call(f32[32,1,384]{2,1,0:T(1,128)S(1)} %all_to_all.71.vals, s32[32,1,384]{2,1,0:T(1,128)S(1)} %get-tuple-element.30.stations, s32[32,1,384]{2,1,0:T(1,128)S(1)} %get-tuple-element.31.dirs), custom_call_target="tpu_custom_call" | custom-call | tf_op jit(solution)/shard_map/final_place/pallas_call | solution.py:330
  (14 shorter events, 2.3 us)
Async XLA Ops:
  25.7 10.3 %collective-permute-start.1 = (f32[1,384]{1,0:T(1,128)S(1)}, f32[1,384]{1,0:T(1,128)S(1)}, u32[]{:S(2)}, u32[]{:S(2)}) collective-permute-start(f32[1,384]{1,0:T(1,128)S(1)} %get-tuple-element.32.target), channel_id=1, source_target_pairs={{1,2},{2,1},{3,4},{4,3},{5,6},{6,5},{9,10},{10,9},{11,12},{12,11},... | collective-permute-start | bytes 4616 | tf_op jit(solution)/shard_map/ppermute | solution.py:466
  31.7 4.3 %collective-permute-start = (f32[1,384]{1,0:T(1,128)S(1)}, f32[1,384]{1,0:T(1,128)S(1)}, u32[]{:S(2)}, u32[]{:S(2)}) collective-permute-start(f32[1,384]{1,0:T(1,128)S(1)} %get-tuple-element.32.target), channel_id=1, source_target_pairs={{0,1},{1,0},{2,3},{3,2},{4,5},{5,4},{6,7},{7,6},{8,9},{9,8},{10,11... | collective-permute-start | bytes 4616 | tf_op jit(solution)/shard_map/ppermute | solution.py:467
  81.5 10.3 %collective-permute-start.3 = (f32[1,384]{1,0:T(1,128)S(1)}, f32[1,384]{1,0:T(1,128)S(1)}, u32[]{:S(2)}, u32[]{:S(2)}) collective-permute-start(f32[1,384]{1,0:T(1,128)S(1)} %own_target.3.target), channel_id=1, source_target_pairs={{1,2},{2,1},{3,4},{4,3},{5,6},{6,5},{9,10},{10,9},{11,12},{12,11},... | collective-permute-start | bytes 4616 | tf_op jit(solution)/shard_map/ppermute | solution.py:466
  87.6 4.3 %collective-permute-start.2 = (f32[1,384]{1,0:T(1,128)S(1)}, f32[1,384]{1,0:T(1,128)S(1)}, u32[]{:S(2)}, u32[]{:S(2)}) collective-permute-start(f32[1,384]{1,0:T(1,128)S(1)} %own_target.3.target), channel_id=1, source_target_pairs={{0,1},{1,0},{2,3},{3,2},{4,5},{5,4},{6,7},{7,6},{8,9},{9,8},{10,11... | collective-permute-start | bytes 4616 | tf_op jit(solution)/shard_map/ppermute | solution.py:467
  137.2 10.3 %collective-permute-start.5 = (f32[1,384]{1,0:T(1,128)S(1)}, f32[1,384]{1,0:T(1,128)S(1)}, u32[]{:S(2)}, u32[]{:S(2)}) collective-permute-start(f32[1,384]{1,0:T(1,128)S(1)} %own_target.4.target), channel_id=1, source_target_pairs={{1,2},{2,1},{3,4},{4,3},{5,6},{6,5},{9,10},{10,9},{11,12},{12,11},... | collective-permute-start | bytes 4616 | tf_op jit(solution)/shard_map/ppermute | solution.py:466
  143.3 4.3 %collective-permute-start.4 = (f32[1,384]{1,0:T(1,128)S(1)}, f32[1,384]{1,0:T(1,128)S(1)}, u32[]{:S(2)}, u32[]{:S(2)}) collective-permute-start(f32[1,384]{1,0:T(1,128)S(1)} %own_target.4.target), channel_id=1, source_target_pairs={{0,1},{1,0},{2,3},{3,2},{4,5},{5,4},{6,7},{7,6},{8,9},{9,8},{10,11... | collective-permute-start | bytes 4616 | tf_op jit(solution)/shard_map/ppermute | solution.py:467
  193.0 10.3 %collective-permute-start.7 = (f32[1,384]{1,0:T(1,128)S(1)}, f32[1,384]{1,0:T(1,128)S(1)}, u32[]{:S(2)}, u32[]{:S(2)}) collective-permute-start(f32[1,384]{1,0:T(1,128)S(1)} %own_target.5.target), channel_id=1, source_target_pairs={{1,2},{2,1},{3,4},{4,3},{5,6},{6,5},{9,10},{10,9},{11,12},{12,11},... | collective-permute-start | bytes 4616 | tf_op jit(solution)/shard_map/ppermute | solution.py:466
  199.1 4.3 %collective-permute-start.6 = (f32[1,384]{1,0:T(1,128)S(1)}, f32[1,384]{1,0:T(1,128)S(1)}, u32[]{:S(2)}, u32[]{:S(2)}) collective-permute-start(f32[1,384]{1,0:T(1,128)S(1)} %own_target.5.target), channel_id=1, source_target_pairs={{0,1},{1,0},{2,3},{3,2},{4,5},{5,4},{6,7},{7,6},{8,9},{9,8},{10,11... | collective-permute-start | bytes 4616 | tf_op jit(solution)/shard_map/ppermute | solution.py:467
